TPU v7x, 256 devices: a whole 4x4x8 slice. The times are simulated.
256 devices in a mesh: wav: 32 (over y, x, core), lev: 8 (over z).
Axes of the slice: x: 4, y: 4, z: 8, core: 2. Of those that a mesh axis runs over, the one named last changes fastest.
Arguments:
- spectral: bfloat16 [224, 401, 1024], P('wav', None, 'lev'), may hold values from -0.1796875 to 0.1796875
- legendre: bfloat16 [224, 401, 256], P('wav', None, 'lev'), may hold values from -0.4375 to 0.4375
- wave_pair: int32 [224], replicated, may hold values from -1 to 199, as said below
- lat_slot: int32 [256], replicated, may hold values from 0 to 799, as said below
Outputs:
- gridded: bfloat16 [256, 512, 1616], P('wav', 'lev')
Inputs may be any that keep to these rules, and one draw needn't show every extreme that they name: `wave_pair`: each pair number 0 to 199 appears exactly once; all other entries are -1. `lat_slot`: the entries are distinct latitudes.
All inputs are finite; a program needn't handle non-finite values.
Results may differ from a plain program's by a relative error of at most 0.0055.
Values may be sent and summed in bfloat16 or wider, within the bound.
No kernel may reach another device: no remote copies, remote signals or barrier semaphores. Data moves between devices by JAX's collectives and lax.ppermute only.
A program may use at most 64 MiB of HBM per device.

v0:
```python
import math

import jax
import jax.numpy as jnp
from jax import lax
from jax.sharding import PartitionSpec as P

NLAT = 800


def from_everyone(shard, axis):
    copies = jnp.broadcast_to(shard, (lax.axis_size(axis), *shard.shape))
    return lax.all_to_all(copies, axis, split_axis=0, concat_axis=0, tiled=True)


def laid_out(blocks, dim):
    dims = list(blocks.shape[1:])
    dims[dim] *= blocks.shape[0]
    return jnp.moveaxis(blocks, 0, dim).reshape(dims)


def gather_directly(shard, axis, dim):
    blocks = from_everyone(shard, axis)
    return laid_out(blocks, dim)


def fold_masks(pair_ids, fold_count, wave_count):
    fold_rows = jnp.arange(fold_count, dtype=jnp.int32)
    filled = pair_ids >= 0
    border = wave_count - pair_ids
    lower = filled[:, None] & (fold_rows[None, :] < border[:, None])
    upper = filled[:, None] & (fold_rows[None, :] >= border[:, None])
    return jnp.stack([lower, upper], axis=1)


def trig_parts(wave_numbers, steps, counts_b):
    residue = wave_numbers[None, None] * steps[None, :, None, None] % counts_b
    angles = residue.astype(jnp.float32) * (2.0 * math.pi) / counts_b.astype(jnp.float32)
    return (jnp.cos(angles), jnp.sin(angles))


def synthesis_table(pair_ids, row_lats, lat_count, lon_width, wave_count):
    filled = pair_ids >= 0
    wave_numbers = jnp.stack([pair_ids, wave_count - 1 - pair_ids], axis=1)
    lon_count = 20 + 4 * jnp.minimum(row_lats, lat_count - 1 - row_lats)
    highest = jnp.minimum(wave_count - 1, (lon_count - 1) // 2)
    counts_b = lon_count[:, None, None, None]
    coarse_count = (lon_width + 63) // 64
    coarse_steps = jnp.arange(coarse_count, dtype=jnp.int32) * 64
    fine_steps = jnp.arange(64, dtype=jnp.int32)
    cos_coarse, sin_coarse = trig_parts(wave_numbers, coarse_steps, counts_b)
    cos_fine, sin_fine = trig_parts(wave_numbers, fine_steps, counts_b)
    cos_all = (
        cos_coarse[:, :, None] * cos_fine[:, None] - sin_coarse[:, :, None] * sin_fine[:, None]
    )
    sin_all = (
        sin_coarse[:, :, None] * cos_fine[:, None] + cos_coarse[:, :, None] * sin_fine[:, None]
    )
    row_total = row_lats.shape[0]
    cos_all = cos_all.reshape(row_total, coarse_count * 64, wave_numbers.shape[0], 2)[:, :lon_width]
    sin_all = sin_all.reshape(row_total, coarse_count * 64, wave_numbers.shape[0], 2)[:, :lon_width]
    columns = jnp.arange(lon_width, dtype=jnp.int32)
    valid = (
        filled[None, None, :, None]
        & (wave_numbers[None, None] <= highest[:, None, None, None])
        & (columns[None, :, None, None] < counts_b)
    )
    factor = jnp.where(wave_numbers == 0, 1.0, 2.0).astype(jnp.float32)[None, None]
    real_part = jnp.where(valid, factor * cos_all, 0.0)
    imag_part = jnp.where(valid, -factor * sin_all, 0.0)
    return jnp.stack([real_part, imag_part], axis=-1).astype(jnp.bfloat16)


def legendre_sum(coefficients, weights, half_masks):
    paired = coefficients.reshape(
        coefficients.shape[0], coefficients.shape[1], coefficients.shape[2] // 2, 2
    )
    masked = jnp.where(
        half_masks[:, :, :, None, None], paired[:, None], jnp.zeros((), paired.dtype)
    )
    summed = jnp.einsum("shtlc,sta->ashcl", masked, weights, preferred_element_type=jnp.float32)
    return summed.astype(jnp.bfloat16)


def on_device(spectral, legendre, wave_pair, lat_slot):
    slot_count = spectral.shape[0]
    fold_count = spectral.shape[1]
    wave_count = fold_count - 1
    lat_count = NLAT
    lon_width = 2 * lat_count + 16
    wav_devices = lax.axis_size("wav")
    wav_index = lax.axis_index("wav")
    own_pairs = lax.dynamic_slice_in_dim(wave_pair, wav_index * slot_count, slot_count)
    half_masks = fold_masks(own_pairs, fold_count, wave_count)
    fourier = legendre_sum(spectral, gather_directly(legendre, "lev", 2), half_masks)
    row_count = lat_slot.shape[0] // wav_devices
    row_lats = lax.dynamic_slice_in_dim(lat_slot, wav_index * row_count, row_count)
    group_rows = max(1, row_count // 25)
    while row_count % group_rows:
        group_rows -= 1
    group_count = row_count // group_rows
    received = lax.all_to_all(fourier, "wav", split_axis=0, concat_axis=1, tiled=True)
    layer_items = received.shape[4]
    grouped = received.reshape((group_count, group_rows) + received.shape[1:])
    lat_groups = row_lats.reshape(group_count, group_rows)

    def one_group(args):
        values, group_lats = args
        basis = synthesis_table(wave_pair, group_lats, lat_count, lon_width, wave_count)
        result = jnp.einsum("rjghc,rghcl->rlj", basis, values, preferred_element_type=jnp.float32)
        return result.astype(jnp.bfloat16)

    gridded_groups = lax.map(one_group, (grouped, lat_groups))
    return gridded_groups.reshape(row_count, layer_items, lon_width)


def solution(mesh):
    return jax.shard_map(
        on_device,
        mesh=mesh,
        in_specs=(P("wav", None, "lev"), P("wav", None, "lev"), P(), P()),
        out_specs=P("wav", "lev", None),
        check_vma=False,
    )
```

profile of v0, /device:TPU:1, one launch (start us, length us, event | category | flops | bytes accessed | tf_op | source)
XLA Modules:
  0.0 264.1 jit_solution(804061478563402776)
XLA Ops:
  2.4 9.1 %all-to-all-start = ((bf16[8,7,401,32]{2,3,1,0:T(8,128)(2,1)}), bf16[8,7,401,32]{2,3,1,0:T(8,128)(2,1)S(1)}, u32[]{:S(2)}, u32[]{:S(2)}) async-start(bf16[8,7,401,32]{2,3,1,0:T(8,128)(2,1)} %broadcast_in_dim.98), calls=%async_computation | async-start | bytes 3670016 | tf_op jit(solution)/shard_map/all_to_all | solution.py:13
  16.9 40.7 %all-to-all-done = bf16[8,7,401,32]{2,3,1,0:T(8,128)(2,1)S(1)} async-done(((bf16[8,7,401,32]{2,3,1,0:T(8,128)(2,1)}), bf16[8,7,401,32]{2,3,1,0:T(8,128)(2,1)S(1)}, u32[]{:S(2)}, u32[]{:S(2)}) %all-to-all-start) | async-done | bytes 1437216 | tf_op jit(solution)/shard_map/all_to_all | solution.py:13
  63.2 7.6 %all-to-all-start.1 = ((bf16[32,2,7168]{2,1,0:T(2,128)(2,1)}), bf16[32,2,7168]{2,1,0:T(2,128)(2,1)S(1)}, u32[]{:S(2)}, u32[]{:S(2)}) async-start(bf16[32,2,7168]{2,1,0:T(2,128)(2,1)} %reshape.588), calls=%async_computation.1 | async-start | bytes 1835008 | tf_op jit(solution)/shard_map/all_to_all | solution.py:102
  70.9 15.5 %all-to-all-done.1 = bf16[32,2,7168]{2,1,0:T(2,128)(2,1)S(1)} async-done(((bf16[32,2,7168]{2,1,0:T(2,128)(2,1)}), bf16[32,2,7168]{2,1,0:T(2,128)(2,1)S(1)}, u32[]{:S(2)}, u32[]{:S(2)}) %all-to-all-start.1) | async-done | bytes 917536 | tf_op jit(solution)/shard_map/all_to_all | solution.py:102
  90.8 173.3 %while.15 = (s32[]{:T(128)}, bf16[8,1,64,1616]{3,2,1,0:T(8,128)(2,1)}, bf16[8,1,224,2,2,64]{2,5,3,4,1,0:T(8,128)(2,1)}, s32[224]{0:T(256)S(1)}, s32[8,1]{0,1:T(1...) while((s32[]{:T(128)}, ...), condition=%wide.region_1.2_spmd, body=%wide.region_0.1_spmd.sunk | while | flops 196876992 | bytes 53313796 | solution.py:113
  98.1 3.6 %copy.36 = f32[1,1616,224,2]{1,2,3,0:T(8,128)} copy(f32[1,1616,224,2]{2,1,3,0:T(8,128)} %slice.24) | data formatting | bytes 5791744 | tf_op jit(solution)/shard_map/while
  103.6 3.8 %copy.37 = f32[1,1616,224,2]{1,2,3,0:T(8,128)} copy(f32[1,1616,224,2]{2,1,3,0:T(8,128)} %slice.25) | data formatting | bytes 5791744 | tf_op jit(solution)/shard_map/while
  119.8 3.6 %copy.36 = f32[1,1616,224,2]{1,2,3,0:T(8,128)} copy(f32[1,1616,224,2]{2,1,3,0:T(8,128)} %slice.24) | data formatting | bytes 5791744 | tf_op jit(solution)/shard_map/while
  125.3 3.8 %copy.37 = f32[1,1616,224,2]{1,2,3,0:T(8,128)} copy(f32[1,1616,224,2]{2,1,3,0:T(8,128)} %slice.25) | data formatting | bytes 5791744 | tf_op jit(solution)/shard_map/while
  129.1 2.7 %fusion.66 = (bf16[1616,224,2,1]{0,1,2,3:T(8,128)(2,1)S(1)}, bf16[1616,224,2,1]{0,1,2,3:T(8,128)(2,1)S(1)}) fusion(f32[1,1616,224,2]{1,2,3,0:T(8,128)S(1)} %copy-done.1, f32[224,2]{0,1:T(2,128)S(1)} %get-tuple-element.206, pred[1616]{0:T(1024)(128)(4,1)S(1)} %iota_compare_fusion.2, pred[224,2]{0,1:T(4,128)(4,1)S(1)} %compare_and_fusion.4, ...), kind=kLoop, calls=%fused_computation.15.clone.1 | loop fusion | flops 5067776 | bytes 8693264 | tf_op jit(solution)/shard_map/while/body/eval_jaxpr/stack | solution.py:71
  141.4 3.6 %copy.36 = f32[1,1616,224,2]{1,2,3,0:T(8,128)} copy(f32[1,1616,224,2]{2,1,3,0:T(8,128)} %slice.24) | data formatting | bytes 5791744 | tf_op jit(solution)/shard_map/while
  146.9 3.8 %copy.37 = f32[1,1616,224,2]{1,2,3,0:T(8,128)} copy(f32[1,1616,224,2]{2,1,3,0:T(8,128)} %slice.25) | data formatting | bytes 5791744 | tf_op jit(solution)/shard_map/while
  150.8 2.7 %fusion.66 = (bf16[1616,224,2,1]{0,1,2,3:T(8,128)(2,1)S(1)}, bf16[1616,224,2,1]{0,1,2,3:T(8,128)(2,1)S(1)}) fusion(f32[1,1616,224,2]{1,2,3,0:T(8,128)S(1)} %copy-done.1, f32[224,2]{0,1:T(2,128)S(1)} %get-tuple-element.206, pred[1616]{0:T(1024)(128)(4,1)S(1)} %iota_compare_fusion.2, pred[224,2]{0,1:T(4,128)(4,1)S(1)} %compare_and_fusion.4, ...), kind=kLoop, calls=%fused_computation.15.clone.1 | loop fusion | flops 5067776 | bytes 8693264 | tf_op jit(solution)/shard_map/while/body/eval_jaxpr/stack | solution.py:71
  163.1 3.6 %copy.36 = f32[1,1616,224,2]{1,2,3,0:T(8,128)} copy(f32[1,1616,224,2]{2,1,3,0:T(8,128)} %slice.24) | data formatting | bytes 5791744 | tf_op jit(solution)/shard_map/while
  168.6 3.8 %copy.37 = f32[1,1616,224,2]{1,2,3,0:T(8,128)} copy(f32[1,1616,224,2]{2,1,3,0:T(8,128)} %slice.25) | data formatting | bytes 5791744 | tf_op jit(solution)/shard_map/while
  184.7 3.6 %copy.36 = f32[1,1616,224,2]{1,2,3,0:T(8,128)} copy(f32[1,1616,224,2]{2,1,3,0:T(8,128)} %slice.24) | data formatting | bytes 5791744 | tf_op jit(solution)/shard_map/while
  190.2 3.8 %copy.37 = f32[1,1616,224,2]{1,2,3,0:T(8,128)} copy(f32[1,1616,224,2]{2,1,3,0:T(8,128)} %slice.25) | data formatting | bytes 5791744 | tf_op jit(solution)/shard_map/while
  194.1 2.7 %fusion.66 = (bf16[1616,224,2,1]{0,1,2,3:T(8,128)(2,1)S(1)}, bf16[1616,224,2,1]{0,1,2,3:T(8,128)(2,1)S(1)}) fusion(f32[1,1616,224,2]{1,2,3,0:T(8,128)S(1)} %copy-done.1, f32[224,2]{0,1:T(2,128)S(1)} %get-tuple-element.206, pred[1616]{0:T(1024)(128)(4,1)S(1)} %iota_compare_fusion.2, pred[224,2]{0,1:T(4,128)(4,1)S(1)} %compare_and_fusion.4, ...), kind=kLoop, calls=%fused_computation.15.clone.1 | loop fusion | flops 5067776 | bytes 8693264 | tf_op jit(solution)/shard_map/while/body/eval_jaxpr/stack | solution.py:71
  206.4 3.6 %copy.36 = f32[1,1616,224,2]{1,2,3,0:T(8,128)} copy(f32[1,1616,224,2]{2,1,3,0:T(8,128)} %slice.24) | data formatting | bytes 5791744 | tf_op jit(solution)/shard_map/while
  211.9 3.8 %copy.37 = f32[1,1616,224,2]{1,2,3,0:T(8,128)} copy(f32[1,1616,224,2]{2,1,3,0:T(8,128)} %slice.25) | data formatting | bytes 5791744 | tf_op jit(solution)/shard_map/while
  228.1 3.6 %copy.36 = f32[1,1616,224,2]{1,2,3,0:T(8,128)} copy(f32[1,1616,224,2]{2,1,3,0:T(8,128)} %slice.24) | data formatting | bytes 5791744 | tf_op jit(solution)/shard_map/while
  233.6 3.8 %copy.37 = f32[1,1616,224,2]{1,2,3,0:T(8,128)} copy(f32[1,1616,224,2]{2,1,3,0:T(8,128)} %slice.25) | data formatting | bytes 5791744 | tf_op jit(solution)/shard_map/while
  249.7 3.6 %copy.36 = f32[1,1616,224,2]{1,2,3,0:T(8,128)} copy(f32[1,1616,224,2]{2,1,3,0:T(8,128)} %slice.24) | data formatting | bytes 5791744 | tf_op jit(solution)/shard_map/while
  255.2 3.8 %copy.37 = f32[1,1616,224,2]{1,2,3,0:T(8,128)} copy(f32[1,1616,224,2]{2,1,3,0:T(8,128)} %slice.25) | data formatting | bytes 5791744 | tf_op jit(solution)/shard_map/while
  (159 shorter events, 113.4 us)
Async XLA Ops:
  0.0 70.8 %copy-start = (s32[256]{0:T(256)S(1)}, s32[256]{0:T(256)}, u32[]{:S(2)}) copy-start(s32[256]{0:T(256)} %param.9) | copy-start | bytes 3076
  2.4 9.1 %copy-start.3 = (bf16[7,401,128]{2,1,0:T(8,128)(2,1)S(1)}, bf16[7,401,128]{2,1,0:T(8,128)(2,1)}, u32[]{:S(2)}) copy-start(bf16[7,401,128]{2,1,0:T(8,128)(2,1)} %param.6) | copy-start | bytes 2155780
  2.4 55.2 %all-to-all-start = ((bf16[8,7,401,32]{2,3,1,0:T(8,128)(2,1)}), bf16[8,7,401,32]{2,3,1,0:T(8,128)(2,1)S(1)}, u32[]{:S(2)}, u32[]{:S(2)}) async-start(bf16[8,7,401,32]{2,3,1,0:T(8,128)(2,1)} %broadcast_in_dim.98), calls=%async_computation | async-start | bytes 3670016 | tf_op jit(solution)/shard_map/all_to_all | solution.py:13
  13.0 3.6 %copy-start.4 = (s32[224]{0:T(256)S(1)}, s32[224]{0:T(256)}, u32[]{:S(2)}) copy-start(s32[224]{0:T(256)} %param.8) | copy-start | bytes 2692
  57.6 1.2 copy-start.2
  63.2 23.2 %all-to-all-start.1 = ((bf16[32,2,7168]{2,1,0:T(2,128)(2,1)}), bf16[32,2,7168]{2,1,0:T(2,128)(2,1)S(1)}, u32[]{:S(2)}, u32[]{:S(2)}) async-start(bf16[32,2,7168]{2,1,0:T(2,128)(2,1)} %reshape.588), calls=%async_computation.1 | async-start | bytes 1835008 | tf_op jit(solution)/shard_map/all_to_all | solution.py:102
  103.6 3.8 %copy-start.1 = (f32[1,1616,224,2]{1,2,3,0:T(8,128)S(1)}, f32[1,1616,224,2]{1,2,3,0:T(8,128)}, u32[]{:S(2)}) copy-start(f32[1,1616,224,2]{1,2,3,0:T(8,128)} %copy.36) | copy-start | bytes 8687620 | tf_op jit(solution)/shard_map/while
  125.3 3.8 %copy-start.1 = (f32[1,1616,224,2]{1,2,3,0:T(8,128)S(1)}, f32[1,1616,224,2]{1,2,3,0:T(8,128)}, u32[]{:S(2)}) copy-start(f32[1,1616,224,2]{1,2,3,0:T(8,128)} %copy.36) | copy-start | bytes 8687620 | tf_op jit(solution)/shard_map/while
  146.9 3.8 %copy-start.1 = (f32[1,1616,224,2]{1,2,3,0:T(8,128)S(1)}, f32[1,1616,224,2]{1,2,3,0:T(8,128)}, u32[]{:S(2)}) copy-start(f32[1,1616,224,2]{1,2,3,0:T(8,128)} %copy.36) | copy-start | bytes 8687620 | tf_op jit(solution)/shard_map/while
  168.6 3.8 %copy-start.1 = (f32[1,1616,224,2]{1,2,3,0:T(8,128)S(1)}, f32[1,1616,224,2]{1,2,3,0:T(8,128)}, u32[]{:S(2)}) copy-start(f32[1,1616,224,2]{1,2,3,0:T(8,128)} %copy.36) | copy-start | bytes 8687620 | tf_op jit(solution)/shard_map/while
  190.2 3.8 %copy-start.1 = (f32[1,1616,224,2]{1,2,3,0:T(8,128)S(1)}, f32[1,1616,224,2]{1,2,3,0:T(8,128)}, u32[]{:S(2)}) copy-start(f32[1,1616,224,2]{1,2,3,0:T(8,128)} %copy.36) | copy-start | bytes 8687620 | tf_op jit(solution)/shard_map/while
  211.9 3.8 %copy-start.1 = (f32[1,1616,224,2]{1,2,3,0:T(8,128)S(1)}, f32[1,1616,224,2]{1,2,3,0:T(8,128)}, u32[]{:S(2)}) copy-start(f32[1,1616,224,2]{1,2,3,0:T(8,128)} %copy.36) | copy-start | bytes 8687620 | tf_op jit(solution)/shard_map/while
  233.5 3.8 %copy-start.1 = (f32[1,1616,224,2]{1,2,3,0:T(8,128)S(1)}, f32[1,1616,224,2]{1,2,3,0:T(8,128)}, u32[]{:S(2)}) copy-start(f32[1,1616,224,2]{1,2,3,0:T(8,128)} %copy.36) | copy-start | bytes 8687620 | tf_op jit(solution)/shard_map/while
  255.2 3.8 %copy-start.1 = (f32[1,1616,224,2]{1,2,3,0:T(8,128)S(1)}, f32[1,1616,224,2]{1,2,3,0:T(8,128)}, u32[]{:S(2)}) copy-start(f32[1,1616,224,2]{1,2,3,0:T(8,128)} %copy.36) | copy-start | bytes 8687620 | tf_op jit(solution)/shard_map/while
where the time goes:
time: 265 us; the launch traced here: 264 us
  local copies, waits for them, and re-layouts  111 us (42%)
  waiting for transfers between devices  56.2 us (21%)
  other arithmetic  50.6 us (19%)
  matrix products  19.1 us (7%)
  starting transfers between devices  16.7 us (6%)
  loops' own time  10.5 us (4%)
    while x32, local copies, waits for them, and re-layouts  59.1 us
    all_to_all x1, waiting for transfers between devices, from_everyone(): return lax.all_to_all(copies, axis, split_axis=0, concat_axis=0, tiled=True)  40.7 us
    cos x16, other arithmetic, trig_parts(): return (jnp.cos(angles), jnp.sin(angles))  22.2 us
    another operation x8, other arithmetic, synthesis_table(): return jnp.stack([real_part, imag_part], axis=-1).astype(jnp.bfloat16)  21.4 us
    dot_general x8, matrix products, one_group(): jnp.einsum('rjghc,rghcl->rlj', basis, values, preferred_element_type=jnp....  18.4 us
    all_to_all x1, waiting for transfers between devices, on_device(): lax.all_to_all(fourier, 'wav', split_axis=0, concat_axis=1, tiled=True)  15.5 us
    slice x8, local copies, waits for them, and re-layouts, synthesis_table(): cos_all.reshape(row_total, coarse_count * 64, wave_numbers.shape[0], 2)  15.1 us
    slice x8, local copies, waits for them, and re-layouts, synthesis_table(): sin_all.reshape(row_total, coarse_count * 64, wave_numbers.shape[0], 2)  15.1 us
  transfers between devices with their start and end apart: 2, of which 2 were waited for; matrix products, arithmetic and copies ran while one was open for 2% of the time, Pallas kernels for 0%

commit v1 on v0

v1 whole, which is shorter than its diff:
```python
import jax
import jax.numpy as jnp
from jax import lax
from jax.experimental import pallas as pl
from jax.experimental.pallas import tpu as pltpu
from jax.sharding import PartitionSpec as P

NLAT = 800
WAVES = 400
FOLD = 401
WIDTH = 1616
SLOTS = 7
ROWS = 8
QBLK = 32
MAIN = 384
REST = FOLD - MAIN
PACKED = SLOTS * MAIN + 128
KEEP = 448
KP = 512
FINE = 256
COARSE = 7

COS = (1.0, -19.739208221435547, 64.93938446044922, -85.45662689208984, 60.24171447753906,
       -26.402057647705078, 7.7920684814453125, -1.4433850049972534)
SIN = (6.2831854820251465, -41.34170150756836, 81.6051025390625, -76.70254516601562,
       42.02196502685547, -14.884664535522461, 3.2164907455444336)


def horner(coefs, v):
    total = jnp.full_like(v, coefs[-1])
    for c in coefs[-2::-1]:
        total = total * v + c
    return total


def cos_sin(x, n, inv):
    r = x - jnp.floor(x * inv + 0.5) * n
    u = r * inv
    v = u * u
    return horner(COS, v), u * horner(SIN, v)


def pack_kernel(leg, out, scr):
    total = jnp.zeros((QBLK, 128), jnp.float32)
    scr[...] = total
    for s in range(SLOTS):
        out[:, MAIN * s : MAIN * (s + 1)] = leg[s, :, 0:MAIN]
        scr[:, 0:REST] = leg[s, :, MAIN:FOLD].astype(jnp.float32)
        tail = scr[...]
        total = total + (pltpu.roll(tail, REST * s, 1) if s else tail)
    out[:, SLOTS * MAIN : PACKED] = total.astype(jnp.bfloat16)


def mask_kernel(pairs, spec, out, scr):
    t_main = lax.broadcasted_iota(jnp.int32, (MAIN, 128), 0)
    t_rest = lax.broadcasted_iota(jnp.int32, (128, 128), 0) + MAIN
    for s in range(SLOTS):
        border = WAVES - pairs[s]
        border = jnp.where(pairs[s] >= 0, border, FOLD)
        main = spec[s, 0:MAIN, :].astype(jnp.float32)
        low = jnp.where(t_main < border, main, 0.0)
        out[s, 0:MAIN, 0:128] = low.astype(jnp.bfloat16)
        out[s, 0:MAIN, 128:256] = (main - low).astype(jnp.bfloat16)
        scr[...] = jnp.zeros((128, 128), jnp.float32)
        scr[REST * s : REST * (s + 1), :] = spec[s, MAIN:FOLD, :].astype(jnp.float32)
        rest = scr[...]
        low = jnp.where(t_rest - REST * s < border, rest, 0.0)
        out[s, MAIN:KP, 0:128] = low.astype(jnp.bfloat16)
        out[s, MAIN:KP, 128:256] = (rest - low).astype(jnp.bfloat16)


def legendre_kernel(place, rhs, x0, p1, m1, p2, m2, p3, m3, p4, m4, out):
    z = place[0]
    for s in range(SLOTS):
        def lhs(ref):
            return jnp.concatenate(
                [ref[:, MAIN * s : MAIN * (s + 1)], ref[:, SLOTS * MAIN : PACKED]], axis=1)
        left = jnp.concatenate([lhs(r) for r in (x0, p1, m1, p2, m2, p3, m3, p4, m4)], axis=0)
        got = jnp.dot(left, rhs[s], preferred_element_type=jnp.float32)
        for i, d in enumerate((0, 1, -1, 2, -2, 3, -3, 4)):
            block = lax.rem(z - d + 8, 8)
            for h in range(2):
                part = got[QBLK * i : QBLK * (i + 1), 128 * h : 128 * (h + 1)]
                out[pl.ds(4 * block, 4), 2 * s + h] = part.reshape(4, ROWS, 128).astype(jnp.bfloat16)


def table_kernel(lats, waves, fine, coarse):
    a = lats[pl.program_id(0)]
    lon = 20 + 4 * jnp.minimum(a, NLAT - 1 - a)
    highest = jnp.minimum(WAVES - 1, (lon - 1) // 2).astype(jnp.float32)
    m = waves[...]
    n = jnp.full((1, KP), lon, jnp.int32).astype(jnp.float32)
    inv = 1.0 / n
    scale = jnp.where((m >= 0.0) & (m <= highest), jnp.where(m == 0.0, 1.0, 2.0), 0.0)

    def at(step, count):
        j = step * lax.broadcasted_iota(jnp.int32, (count, KP), 0)
        return cos_sin(j.astype(jnp.float32) * m, n, inv)

    cos_b, sin_b = at(1, 32)
    cos_a, sin_a = at(32, 8)
    cos_a = cos_a * scale
    sin_a = sin_a * scale
    for i in range(FINE // 32):
        ca = cos_a[i : i + 1, :]
        sa = sin_a[i : i + 1, :]
        rows = slice(32 * i, 32 * (i + 1))
        fine[0, rows, 0:KP] = (ca * cos_b - sa * sin_b).astype(jnp.bfloat16)
        fine[0, rows, KP : 2 * KP] = (-(sa * cos_b + ca * sin_b)).astype(jnp.bfloat16)
    cos_c, sin_c = at(FINE, 8)
    coarse[0, :, 0:KP] = cos_c
    coarse[0, :, KP : 2 * KP] = sin_c


def synth_kernel(lats, recv, fine, coarse, out, scr, lhs):
    q = pl.program_id(0)
    a = lats[q]
    lon = 20 + 4 * jnp.minimum(a, NLAT - 1 - a)

    @pl.when(q == 0)
    def _():
        for i in range(7):
            scr[512 * i : 512 * (i + 1), :] = (
                recv[64 * i : 64 * (i + 1)].astype(jnp.float32).reshape(512, 128))
        scr[KEEP * ROWS : KP * ROWS, :] = jnp.zeros(((KP - KEEP) * ROWS, 128), jnp.float32)

    row = lax.broadcasted_iota(jnp.int32, (128, 128), 0)
    col = lax.broadcasted_iota(jnp.int32, (128, 128), 1)
    source = jnp.where(row < 64, 2 * row, 2 * row - 127)
    perm = jnp.where(col == source, 1.0, 0.0).astype(jnp.bfloat16)
    values = scr[pl.ds(q, KP, stride=ROWS), :].astype(jnp.bfloat16)
    nt = (((1,), (1,)), ((), ()))
    turned = lax.dot_general(perm, values, nt, preferred_element_type=jnp.float32)
    re = turned[0:64, :]
    im = turned[64:128, :]
    for jc in range(COARSE):
        cc = coarse[0, jc : jc + 1, 0:KP]
        sc = coarse[0, jc : jc + 1, KP : 2 * KP]
        lhs[64 * jc : 64 * (jc + 1), 0:KP] = (cc * re - sc * im).astype(jnp.bfloat16)
        lhs[64 * jc : 64 * (jc + 1), KP : 2 * KP] = (sc * re + cc * im).astype(jnp.bfloat16)
    result = lax.dot_general(lhs[...], fine[0], nt, preferred_element_type=jnp.float32)
    column = lax.broadcasted_iota(jnp.int32, (64, FINE), 1)
    for jc in range(COARSE):
        width = min(FINE, WIDTH - FINE * jc)
        block = result[64 * jc : 64 * (jc + 1), :]
        block = jnp.where(column < lon - FINE * jc, block, 0.0).astype(jnp.bfloat16)
        out[0, :, FINE * jc : FINE * jc + width] = block[:, 0:width]


def cost(flops, moved):
    return pl.CostEstimate(flops=flops, transcendentals=0, bytes_accessed=moved)


def gather_pieces(x):
    def shift(v, d):
        return lax.ppermute(v, "lev", [(i, (i + d) % 8) for i in range(8)])

    p1, m1 = shift(x, 1), shift(x, -1)
    p2, m2 = shift(x, 2), shift(x, -2)
    p3, m3 = shift(p2, 1), shift(m2, -1)
    half = QBLK // 2
    p4, m4 = shift(p2[:half], 2), shift(m2[half:], -2)
    return x, p1, m1, p2, m2, p3, m3, p4, m4


def on_device(spectral, legendre, wave_pair, lat_slot):
    bf16, f32 = jnp.bfloat16, jnp.float32
    smem = pl.BlockSpec(memory_space=pltpu.SMEM)
    vmem = pl.BlockSpec(memory_space=pltpu.VMEM)
    z = lax.axis_index("lev").astype(jnp.int32)
    w = lax.axis_index("wav").astype(jnp.int32)
    own_pairs = lax.dynamic_slice_in_dim(wave_pair, w * SLOTS, SLOTS)
    own_lats = lax.dynamic_slice_in_dim(lat_slot, w * ROWS, ROWS)
    waves = jnp.stack([wave_pair, WAVES - 1 - wave_pair], axis=1)
    waves = jnp.where(wave_pair[:, None] >= 0, waves, -1).reshape(1, KEEP)
    waves = jnp.pad(waves, ((0, 0), (0, KP - KEEP)), constant_values=-1).astype(f32)

    packed = pl.pallas_call(
        pack_kernel,
        out_shape=jax.ShapeDtypeStruct((QBLK, PACKED), bf16),
        in_specs=[vmem], out_specs=vmem,
        scratch_shapes=[pltpu.VMEM((QBLK, 128), f32)],
        name="pack",
    )(jnp.transpose(legendre, (0, 2, 1)))
    pieces = gather_pieces(packed)

    rhs = pl.pallas_call(
        mask_kernel,
        out_shape=jax.ShapeDtypeStruct((SLOTS, KP, 256), bf16),
        in_specs=[smem, vmem], out_specs=vmem,
        scratch_shapes=[pltpu.VMEM((128, 128), f32)],
        cost_estimate=cost(2_000_000_000, 2_500_000),
        name="mask",
    )(own_pairs, spectral)

    fine, coarse = pl.pallas_call(
        table_kernel,
        out_shape=(jax.ShapeDtypeStruct((ROWS, FINE, 2 * KP), bf16),
                   jax.ShapeDtypeStruct((ROWS, 8, 2 * KP), f32)),
        grid_spec=pltpu.PrefetchScalarGridSpec(
            num_scalar_prefetch=1, grid=(ROWS,),
            in_specs=[pl.BlockSpec((1, KP), lambda q, lats: (0, 0))],
            out_specs=(pl.BlockSpec((1, FINE, 2 * KP), lambda q, lats: (q, 0, 0)),
                       pl.BlockSpec((1, 8, 2 * KP), lambda q, lats: (q, 0, 0)))),
        cost_estimate=cost(4_000_000_000, 4_500_000),
        name="tables",
    )(own_lats, waves)

    fourier = pl.pallas_call(
        legendre_kernel,
        out_shape=jax.ShapeDtypeStruct((32, 2 * SLOTS, ROWS, 128), bf16),
        in_specs=[smem] + [vmem] * 10, out_specs=vmem,
        cost_estimate=cost(2 * 256 * 512 * 256 * SLOTS, 4_000_000),
        name="legendre",
    )(z.reshape(1), rhs, *pieces)

    received = lax.all_to_all(fourier, "wav", split_axis=0, concat_axis=0, tiled=True)

    return pl.pallas_call(
        synth_kernel,
        out_shape=jax.ShapeDtypeStruct((ROWS, 64, WIDTH), bf16),
        grid_spec=pltpu.PrefetchScalarGridSpec(
            num_scalar_prefetch=1, grid=(ROWS,),
            in_specs=[pl.BlockSpec((KEEP, ROWS, 128), lambda q, lats: (0, 0, 0)),
                      pl.BlockSpec((1, FINE, 2 * KP), lambda q, lats: (q, 0, 0)),
                      pl.BlockSpec((1, 8, 2 * KP), lambda q, lats: (q, 0, 0))],
            out_specs=pl.BlockSpec((1, 64, WIDTH), lambda q, lats: (q, 0, 0)),
            scratch_shapes=[pltpu.VMEM((KP * ROWS, 128), f32),
                            pltpu.VMEM((64 * COARSE, 2 * KP), bf16)]),
        cost_estimate=cost(2 * 448 * 1024 * 256 * ROWS, 18_000_000),
        name="synth",
    )(own_lats, received.reshape(KEEP, ROWS, 128), fine, coarse)


def solution(mesh):
    return jax.shard_map(
        on_device,
        mesh=mesh,
        in_specs=(P("wav", None, "lev"), P("wav", None, "lev"), P(), P()),
        out_specs=P("wav", "lev", None),
        check_vma=False,
    )
```

time: 265 us -> 71.4 us (0.27)
  local copies, waits for them, and re-layouts: 111 us -> 3.76 us
  other arithmetic: 50.6 us -> 1.29 us
  waiting for transfers between devices: 56.2 us -> 15.7 us
  Pallas kernels: 0 us -> 23.8 us
  matrix products: 19.1 us -> 0 us
  loops' own time: 10.5 us -> 0 us
  starting transfers between devices: 16.7 us -> 26.2 us
    while x33 -> x0, local copies, waits for them, and re-layouts: 61.7 us -> none
    all_to_all x2 -> x1, waiting for transfers between devices: 56.2 us -> 8.07 us  [on_device(): lax.all_to_all(fourier, 'wav', split_axis=0, concat_axis=0, tiled=True)]
    slice x16 -> x2, local copies, waits for them, and re-layouts: 30.3 us -> 0.01 us  [gather_pieces(): p4, m4 = (shift(p2[:half], 2), shift(m2[half:], -2))]
    pallas_call x0 -> x5, Pallas kernels: none -> 23.8 us  [the longest x1 9.38 us: on_device(): pl.pallas_call(synth_kernel, out_shape=jax.ShapeDtypeStruct((ROWS, 64, WI...]
    cos x16 -> x0, other arithmetic: 22.2 us -> none  [trig_parts(): return (jnp.cos(angles), jnp.sin(angles))]
    another operation x17 -> x0, other arithmetic: 21.5 us -> none  [the longest x8 21.4 us: synthesis_table(): return jnp.stack([real_part, imag_part], axis=-1).astype(jnp.bfloat16)]
    dot_general x9 -> x0, matrix products: 19.1 us -> none  [the longest x8 18.4 us: one_group(): jnp.einsum('rjghc,rghcl->rlj', basis, values, preferred_element_type=jnp....]
    ppermute x0 -> x8, starting transfers between devices: none -> 17.6 us  [shift(): return lax.ppermute(v, 'lev', [(i, (i + d) % 8) for i in range(8)])]
  transfers between devices with their start and end apart: 2 -> 9, of which waited for: 2 -> 5; matrix products, arithmetic and copies ran while one was open for 2% -> 5% of each run, Pallas kernels for 0% -> 13%
where the time goes in v1:
time: 71.4 us; the launch traced here: 70.9 us
  starting transfers between devices  26.2 us (37%)
  Pallas kernels  23.8 us (33%)
  waiting for transfers between devices  15.7 us (22%)
  local copies, waits for them, and re-layouts  3.76 us (5%)
  other arithmetic  1.29 us (2%)
    ppermute x8, starting transfers between devices, shift(): return lax.ppermute(v, 'lev', [(i, (i + d) % 8) for i in range(8)])  17.6 us
    pallas_call x1, Pallas kernels, on_device(): pl.pallas_call(synth_kernel, out_shape=jax.ShapeDtypeStruct((ROWS, 64, WI...  9.38 us
    all_to_all x1, starting transfers between devices, on_device(): lax.all_to_all(fourier, 'wav', split_axis=0, concat_axis=0, tiled=True)  8.55 us
    all_to_all x1, waiting for transfers between devices, on_device(): lax.all_to_all(fourier, 'wav', split_axis=0, concat_axis=0, tiled=True)  8.07 us
    ppermute x8, waiting for transfers between devices, shift(): return lax.ppermute(v, 'lev', [(i, (i + d) % 8) for i in range(8)])  7.63 us
    pallas_call x1, Pallas kernels, on_device(): pl.pallas_call(table_kernel, out_shape=(jax.ShapeDtypeStruct((ROWS, FINE,...  6.05 us
    pallas_call x1, Pallas kernels, on_device(): pl.pallas_call(legendre_kernel, out_shape=jax.ShapeDtypeStruct((32, 2 * S...  3.55 us
    pallas_call x1, Pallas kernels, on_device(): pl.pallas_call(mask_kernel, out_shape=jax.ShapeDtypeStruct((SLOTS, KP, 25...  3.07 us
  transfers between devices with their start and end apart: 9, of which 5 were waited for; matrix products, arithmetic and copies ran while one was open for 5% of the time, Pallas kernels for 13%

profile of v1, /device:TPU:1, one launch (start us, length us, event | category | flops | bytes accessed | tf_op | source)
XLA Modules:
  0.0 70.9 jit_solution(245416867686437634)
XLA Ops:
  0.0 1.7 %pack.1.x0 = bf16[32,2816]{1,0:T(8,128)(2,1)} custom-call(bf16[7,32,401]{2,1,0:T(8,128)(2,1)} %bitcast.6), custom_call_target="tpu_custom_call" | custom-call | tf_op jit(solution)/shard_map/pack/pallas_call | solution.py:178
  1.7 6.8 %collective-permute-start.3 = (bf16[32,2816]{1,0:T(8,128)(2,1)}, bf16[32,2816]{1,0:T(8,128)(2,1)S(1)}, u32[]{:S(2)}, u32[]{:S(2)}) collective-permute-start(bf16[32,2816]{1,0:T(8,128)(2,1)} %pack.1.x0), channel_id=1, source_target_pairs={{0,6},{1,7},{2,0},{3,1},{4,2},{5,3},{6,4},{7,5},{8,14},{9,15},{10,... | collective-permute-start | bytes 540680 | tf_op jit(solution)/shard_map/ppermute | solution.py:156
  8.6 3.1 %collective-permute-start.1 = (bf16[32,2816]{1,0:T(8,128)(2,1)}, bf16[32,2816]{1,0:T(8,128)(2,1)S(1)}, u32[]{:S(2)}, u32[]{:S(2)}) collective-permute-start(bf16[32,2816]{1,0:T(8,128)(2,1)} %pack.1.x0), channel_id=1, source_target_pairs={{0,7},{1,0},{2,1},{3,2},{4,3},{5,4},{6,5},{7,6},{8,15},{9,8},{10,9... | collective-permute-start | bytes 540680 | tf_op jit(solution)/shard_map/ppermute | solution.py:156
  11.7 1.3 %dynamic_slice.7.pairs = s32[7]{0:T(128)} dynamic-slice(s32[224]{0:T(256)} %param.6, s32[]{:T(128)S(6)} %select_n.21), dynamic_slice_sizes={7} | dynamic-slice | bytes 60 | tf_op jit(solution)/shard_map/dynamic_slice | solution.py:172
  13.0 0.7 broadcast_subtract_fusion
  13.7 1.7 %collective-permute-done.3.m2 = bf16[32,2816]{1,0:T(8,128)(2,1)S(1)} collective-permute-done((bf16[32,2816]{1,0:T(8,128)(2,1)}, bf16[32,2816]{1,0:T(8,128)(2,1)S(1)}, u32[]{:S(2)}, u32[]{:S(2)}) %collective-permute-start.3) | collective-permute-done | bytes 180256 | tf_op jit(solution)/shard_map/ppermute | solution.py:156
  15.3 5.2 %collective-permute-start.7 = (bf16[16,2816]{1,0:T(8,128)(2,1)S(1)}, bf16[16,2816]{1,0:T(8,128)(2,1)S(1)}, u32[]{:S(2)}, u32[]{:S(2)}) collective-permute-start(bf16[16,2816]{1,0:T(8,128)(2,1)S(1)} %slice.9), channel_id=1, source_target_pairs={{0,6},{1,7},{2,0},{3,1},{4,2},{5,3},{6,4},{7,5},{8,14},{9,15},{10,... | collective-permute-start | bytes 270344 | tf_op jit(solution)/shard_map/ppermute | solution.py:156
  20.6 0.1 collective-permute-start.6
  20.7 2.4 %collective-permute-start.5 = (bf16[32,2816]{1,0:T(8,128)(2,1)S(1)}, bf16[32,2816]{1,0:T(8,128)(2,1)S(1)}, u32[]{:S(2)}, u32[]{:S(2)}) collective-permute-start(bf16[32,2816]{1,0:T(8,128)(2,1)S(1)} %collective-permute-done.3.m2), channel_id=1, source_target_pairs={{0,7},{1,0},{2,1},{3,2},{4,3},{5,4},{6,5},{7,6},{8,15},{9,8},{10,9... | collective-permute-start | bytes 540680 | tf_op jit(solution)/shard_map/ppermute | solution.py:156
  23.0 3.1 %mask.1.rhs = bf16[7,512,256]{2,1,0:T(8,128)(2,1)} custom-call(s32[7]{0:T(128)} %dynamic_slice.7.pairs, bf16[7,401,128]{2,1,0:T(8,128)(2,1)} %spec.1), custom_call_target="tpu_custom_call" | custom-call | flops 2000000000 | bytes 2500000 | tf_op jit(solution)/shard_map/mask/pallas_call | solution.py:187
  26.2 1.2 %collective-permute-done.6.p4 = bf16[16,2816]{1,0:T(8,128)(2,1)S(1)} collective-permute-done((bf16[16,2816]{1,0:T(8,128)(2,1)S(1)}, bf16[16,2816]{1,0:T(8,128)(2,1)S(1)}, u32[]{:S(2)}, u32[]{:S(2)}) %collective-permute-start.6) | collective-permute-done | bytes 90144 | tf_op jit(solution)/shard_map/ppermute | solution.py:156
  27.4 0.1 collective-permute-done.5.m3
  27.4 4.7 %collective-permute-done.4.p3 = bf16[32,2816]{1,0:T(8,128)(2,1)S(1)} collective-permute-done((bf16[32,2816]{1,0:T(8,128)(2,1)S(1)}, bf16[32,2816]{1,0:T(8,128)(2,1)S(1)}, u32[]{:S(2)}, u32[]{:S(2)}) %collective-permute-start.4) | collective-permute-done | bytes 180256 | tf_op jit(solution)/shard_map/ppermute | solution.py:156
  32.1 0.7 copy-done.6
  32.8 3.5 %legendre.1 = bf16[32,14,8,128]{3,2,1,0:T(8,128)(2,1)} custom-call(s32[1]{0:T(128)} %bitcast.place, bf16[7,512,256]{2,1,0:T(8,128)(2,1)} %mask.1.rhs, bf16[32,2816]{1,0:T(8,128)(2,1)} %pack.1.x0, bf16[32,2816]{1,0:T(8,128)(2,1)} %copy-done.4, bf16[32,2816]{1,0:T(8,128)(2,1)} %copy-done.3, bf16[32,2816]{1,0:T(8,128)(2,1)} %copy-done.2, ...), custom_call_target="tpu_custom_call" | custom-call | flops 469762048 | bytes 4000000 | tf_op jit(solution)/shard_map/legendre/pallas_call | solution.py:209
  36.4 8.5 %all-to-all-start = ((bf16[32,14,8,128]{3,2,1,0:T(8,128)(2,1)}), bf16[32,14,8,128]{3,2,1,0:T(8,128)(2,1)S(1)}, u32[]{:S(2)}, u32[]{:S(2)}) async-start(bf16[32,14,8,128]{3,2,1,0:T(8,128)(2,1)} %legendre.1), calls=%async_computation | async-start | bytes 1835008 | tf_op jit(solution)/shard_map/all_to_all | solution.py:217
  44.9 0.1 copy.5
  45.1 0.1 select_n.23
  45.2 0.6 dynamic_slice.6.lats
  45.8 0.6 pad_convert_fusion.waves
  46.4 6.1 %tables.1 = (bf16[8,256,1024]{2,1,0:T(8,128)(2,1)}, f32[8,8,1024]{2,1,0:T(8,128)}) custom-call(s32[8]{0:T(128)} %dynamic_slice.6.lats, f32[1,512]{1,0:T(1,128)} %pad_convert_fusion.waves), custom_call_target="tpu_custom_call" | custom-call | flops 4000000000 | bytes 4500000 | tf_op jit(solution)/shard_map/tables/pallas_call | solution.py:196
  52.5 8.1 %all-to-all-done = bf16[32,14,8,128]{3,2,1,0:T(8,128)(2,1)S(1)} async-done(((bf16[32,14,8,128]{3,2,1,0:T(8,128)(2,1)}), bf16[32,14,8,128]{3,2,1,0:T(8,128)(2,1)S(1)}, u32[]{:S(2)}, u32[]{:S(2)}) %all-to-all-start) | async-done | bytes 917536 | tf_op jit(solution)/shard_map/all_to_all | solution.py:217
  60.6 0.9 %copy-done = bf16[32,14,8,128]{3,2,1,0:T(8,128)(2,1)} copy-done((bf16[32,14,8,128]{3,2,1,0:T(8,128)(2,1)}, bf16[32,14,8,128]{3,2,1,0:T(8,128)(2,1)S(1)}, u32[]{:S(2)}) %copy-start) | copy-done | bytes 917528
  61.5 9.4 %synth.1 = bf16[8,64,1616]{2,1,0:T(8,128)(2,1)} custom-call(s32[8]{0:T(128)} %dynamic_slice.6.lats, bf16[448,8,128]{2,1,0:T(8,128)(2,1)} %bitcast.5, bf16[8,256,1024]{2,1,0:T(8,128)(2,1)} %get-tuple-element.7.fine, f32[8,8,1024]{2,1,0:T(8,128)} %get-tuple-element.8.coarse), custom_call_target="tpu_custom_call" | custom-call | flops 1879048192 | bytes 18000000 | tf_op jit(solution)/shard_map/synth/pallas_call | solution.py:219
  (31 shorter events, 0.1 us)
Async XLA Ops:
  1.7 13.6 %collective-permute-start.3 = (bf16[32,2816]{1,0:T(8,128)(2,1)}, bf16[32,2816]{1,0:T(8,128)(2,1)S(1)}, u32[]{:S(2)}, u32[]{:S(2)}) collective-permute-start(bf16[32,2816]{1,0:T(8,128)(2,1)} %pack.1.x0), channel_id=1, source_target_pairs={{0,6},{1,7},{2,0},{3,1},{4,2},{5,3},{6,4},{7,5},{8,14},{9,15},{10,... | collective-permute-start | bytes 540680 | tf_op jit(solution)/shard_map/ppermute | solution.py:156
  8.6 12.0 %collective-permute-start.2 = (bf16[32,2816]{1,0:T(8,128)(2,1)}, bf16[32,2816]{1,0:T(8,128)(2,1)S(1)}, u32[]{:S(2)}, u32[]{:S(2)}) collective-permute-start(bf16[32,2816]{1,0:T(8,128)(2,1)} %pack.1.x0), channel_id=1, source_target_pairs={{0,2},{1,3},{2,4},{3,5},{4,6},{5,7},{6,0},{7,1},{8,10},{9,11},{10,... | collective-permute-start | bytes 540680 | tf_op jit(solution)/shard_map/ppermute | solution.py:156
  8.6 14.4 %collective-permute-start.1 = (bf16[32,2816]{1,0:T(8,128)(2,1)}, bf16[32,2816]{1,0:T(8,128)(2,1)S(1)}, u32[]{:S(2)}, u32[]{:S(2)}) collective-permute-start(bf16[32,2816]{1,0:T(8,128)(2,1)} %pack.1.x0), channel_id=1, source_target_pairs={{0,7},{1,0},{2,1},{3,2},{4,3},{5,4},{6,5},{7,6},{8,15},{9,8},{10,9... | collective-permute-start | bytes 540680 | tf_op jit(solution)/shard_map/ppermute | solution.py:156
  11.7 14.4 %collective-permute-start = (bf16[32,2816]{1,0:T(8,128)(2,1)}, bf16[32,2816]{1,0:T(8,128)(2,1)S(1)}, u32[]{:S(2)}, u32[]{:S(2)}) collective-permute-start(bf16[32,2816]{1,0:T(8,128)(2,1)} %pack.1.x0), channel_id=1, source_target_pairs={{0,1},{1,2},{2,3},{3,4},{4,5},{5,6},{6,7},{7,0},{8,9},{9,10},{10,1... | collective-permute-start | bytes 540680 | tf_op jit(solution)/shard_map/ppermute | solution.py:156
  15.3 10.8 %copy-start.1 = (bf16[32,2816]{1,0:T(8,128)(2,1)}, bf16[32,2816]{1,0:T(8,128)(2,1)S(1)}, u32[]{:S(2)}) copy-start(bf16[32,2816]{1,0:T(8,128)(2,1)S(1)} %collective-permute-done.3.m2) | copy-start | bytes 540676
  15.3 10.8 %collective-permute-start.7 = (bf16[16,2816]{1,0:T(8,128)(2,1)S(1)}, bf16[16,2816]{1,0:T(8,128)(2,1)S(1)}, u32[]{:S(2)}, u32[]{:S(2)}) collective-permute-start(bf16[16,2816]{1,0:T(8,128)(2,1)S(1)} %slice.9), channel_id=1, source_target_pairs={{0,6},{1,7},{2,0},{3,1},{4,2},{5,3},{6,4},{7,5},{8,14},{9,15},{10,... | collective-permute-start | bytes 270344 | tf_op jit(solution)/shard_map/ppermute | solution.py:156
  20.6 5.5 %copy-start.2 = (bf16[32,2816]{1,0:T(8,128)(2,1)}, bf16[32,2816]{1,0:T(8,128)(2,1)S(1)}, u32[]{:S(2)}) copy-start(bf16[32,2816]{1,0:T(8,128)(2,1)S(1)} %collective-permute-done.2.p2) | copy-start | bytes 540676
  20.6 6.8 %collective-permute-start.6 = (bf16[16,2816]{1,0:T(8,128)(2,1)S(1)}, bf16[16,2816]{1,0:T(8,128)(2,1)S(1)}, u32[]{:S(2)}, u32[]{:S(2)}) collective-permute-start(bf16[16,2816]{1,0:T(8,128)(2,1)S(1)} %slice.8), channel_id=1, source_target_pairs={{0,2},{1,3},{2,4},{3,5},{4,6},{5,7},{6,0},{7,1},{8,10},{9,11},{10,... | collective-permute-start | bytes 270344 | tf_op jit(solution)/shard_map/ppermute | solution.py:156
  20.7 6.8 %collective-permute-start.5 = (bf16[32,2816]{1,0:T(8,128)(2,1)S(1)}, bf16[32,2816]{1,0:T(8,128)(2,1)S(1)}, u32[]{:S(2)}, u32[]{:S(2)}) collective-permute-start(bf16[32,2816]{1,0:T(8,128)(2,1)S(1)} %collective-permute-done.3.m2), channel_id=1, source_target_pairs={{0,7},{1,0},{2,1},{3,2},{4,3},{5,4},{6,5},{7,6},{8,15},{9,8},{10,9... | collective-permute-start | bytes 540680 | tf_op jit(solution)/shard_map/ppermute | solution.py:156
  23.0 3.1 %copy-start.3 = (bf16[32,2816]{1,0:T(8,128)(2,1)}, bf16[32,2816]{1,0:T(8,128)(2,1)S(1)}, u32[]{:S(2)}) copy-start(bf16[32,2816]{1,0:T(8,128)(2,1)S(1)} %collective-permute-done.1.m1) | copy-start | bytes 540676
  23.0 9.1 %collective-permute-start.4 = (bf16[32,2816]{1,0:T(8,128)(2,1)S(1)}, bf16[32,2816]{1,0:T(8,128)(2,1)S(1)}, u32[]{:S(2)}, u32[]{:S(2)}) collective-permute-start(bf16[32,2816]{1,0:T(8,128)(2,1)S(1)} %collective-permute-done.2.p2), channel_id=1, source_target_pairs={{0,1},{1,2},{2,3},{3,4},{4,5},{5,6},{6,7},{7,0},{8,9},{9,10},{10,1... | collective-permute-start | bytes 540680 | tf_op jit(solution)/shard_map/ppermute | solution.py:156
  26.1 6.0 %copy-start.4 = (bf16[32,2816]{1,0:T(8,128)(2,1)}, bf16[32,2816]{1,0:T(8,128)(2,1)S(1)}, u32[]{:S(2)}) copy-start(bf16[32,2816]{1,0:T(8,128)(2,1)S(1)} %collective-permute-done.p1) | copy-start | bytes 540676
  26.2 6.0 %copy-start.7 = (bf16[16,2816]{1,0:T(8,128)(2,1)}, bf16[16,2816]{1,0:T(8,128)(2,1)S(1)}, u32[]{:S(2)}) copy-start(bf16[16,2816]{1,0:T(8,128)(2,1)S(1)} %collective-permute-done.7.m4) | copy-start | bytes 270340
  27.4 4.8 %copy-start.8 = (bf16[16,2816]{1,0:T(8,128)(2,1)}, bf16[16,2816]{1,0:T(8,128)(2,1)S(1)}, u32[]{:S(2)}) copy-start(bf16[16,2816]{1,0:T(8,128)(2,1)S(1)} %collective-permute-done.6.p4) | copy-start | bytes 270340
  27.4 4.7 %copy-start.5 = (bf16[32,2816]{1,0:T(8,128)(2,1)}, bf16[32,2816]{1,0:T(8,128)(2,1)S(1)}, u32[]{:S(2)}) copy-start(bf16[32,2816]{1,0:T(8,128)(2,1)S(1)} %collective-permute-done.5.m3) | copy-start | bytes 540676
  32.1 0.7 copy-start.6
  36.3 8.6 %copy-start.9 = (s32[224]{0:T(256)S(1)}, s32[224]{0:T(256)}, u32[]{:S(2)}) copy-start(s32[224]{0:T(256)} %param.6) | copy-start | bytes 2692
  36.4 8.9 %copy-start.10 = (s32[256]{0:T(256)S(1)}, s32[256]{0:T(256)}, u32[]{:S(2)}) copy-start(s32[256]{0:T(256)} %param.7) | copy-start | bytes 3076
  36.4 24.2 %all-to-all-start = ((bf16[32,14,8,128]{3,2,1,0:T(8,128)(2,1)}), bf16[32,14,8,128]{3,2,1,0:T(8,128)(2,1)S(1)}, u32[]{:S(2)}, u32[]{:S(2)}) async-start(bf16[32,14,8,128]{3,2,1,0:T(8,128)(2,1)} %legendre.1), calls=%async_computation | async-start | bytes 1835008 | tf_op jit(solution)/shard_map/all_to_all | solution.py:217
  60.6 0.9 %copy-start = (bf16[32,14,8,128]{3,2,1,0:T(8,128)(2,1)}, bf16[32,14,8,128]{3,2,1,0:T(8,128)(2,1)S(1)}, u32[]{:S(2)}) copy-start(bf16[32,14,8,128]{3,2,1,0:T(8,128)(2,1)S(1)} %all-to-all-done) | copy-start | bytes 2752516

commit v2 on v1

--- a/solution.py
+++ b/solution.py
@@ -85,66 +85,90 @@
 
 
 def table_kernel(lats, waves, fine, coarse):
-    a = lats[pl.program_id(0)]
-    lon = 20 + 4 * jnp.minimum(a, NLAT - 1 - a)
-    highest = jnp.minimum(WAVES - 1, (lon - 1) // 2).astype(jnp.float32)
     m = waves[...]
-    n = jnp.full((1, KP), lon, jnp.int32).astype(jnp.float32)
-    inv = 1.0 / n
-    scale = jnp.where((m >= 0.0) & (m <= highest), jnp.where(m == 0.0, 1.0, 2.0), 0.0)
-
-    def at(step, count):
-        j = step * lax.broadcasted_iota(jnp.int32, (count, KP), 0)
-        return cos_sin(j.astype(jnp.float32) * m, n, inv)
-
-    cos_b, sin_b = at(1, 32)
-    cos_a, sin_a = at(32, 8)
-    cos_a = cos_a * scale
-    sin_a = sin_a * scale
-    for i in range(FINE // 32):
-        ca = cos_a[i : i + 1, :]
-        sa = sin_a[i : i + 1, :]
-        rows = slice(32 * i, 32 * (i + 1))
-        fine[0, rows, 0:KP] = (ca * cos_b - sa * sin_b).astype(jnp.bfloat16)
-        fine[0, rows, KP : 2 * KP] = (-(sa * cos_b + ca * sin_b)).astype(jnp.bfloat16)
-    cos_c, sin_c = at(FINE, 8)
-    coarse[0, :, 0:KP] = cos_c
-    coarse[0, :, KP : 2 * KP] = sin_c
-
-
-def synth_kernel(lats, recv, fine, coarse, out, scr, lhs):
-    q = pl.program_id(0)
-    a = lats[q]
-    lon = 20 + 4 * jnp.minimum(a, NLAT - 1 - a)
-
-    @pl.when(q == 0)
-    def _():
-        for i in range(7):
-            scr[512 * i : 512 * (i + 1), :] = (
-                recv[64 * i : 64 * (i + 1)].astype(jnp.float32).reshape(512, 128))
-        scr[KEEP * ROWS : KP * ROWS, :] = jnp.zeros(((KP - KEEP) * ROWS, 128), jnp.float32)
+
+    def one_row(q, carry):
+        a = lats[q]
+        lon = 20 + 4 * jnp.minimum(a, NLAT - 1 - a)
+        highest = jnp.minimum(WAVES - 1, (lon - 1) // 2).astype(jnp.float32)
+        n = jnp.full((1, KP), lon, jnp.int32).astype(jnp.float32)
+        inv = 1.0 / n
+        scale = jnp.where((m >= 0.0) & (m <= highest), jnp.where(m == 0.0, 1.0, 2.0), 0.0)
+
+        def at(step, count):
+            j = step * lax.broadcasted_iota(jnp.int32, (count, KP), 0)
+            return cos_sin(j.astype(jnp.float32) * m, n, inv)
+
+        cos_b, sin_b = at(1, 32)
+        cos_a, sin_a = at(32, 8)
+        cos_a = cos_a * scale
+        sin_a = sin_a * scale
+        for i in range(FINE // 32):
+            ca = cos_a[i : i + 1, :]
+            sa = sin_a[i : i + 1, :]
+            rows = slice(32 * i, 32 * (i + 1))
+            fine[q, rows, 0:KP] = (ca * cos_b - sa * sin_b).astype(jnp.bfloat16)
+            fine[q, rows, KP : 2 * KP] = (-(sa * cos_b + ca * sin_b)).astype(jnp.bfloat16)
+        cos_c, sin_c = at(FINE, 8)
+        coarse[q, :, 0:KP] = cos_c
+        coarse[q, :, KP : 2 * KP] = sin_c
+        return carry
+
+    lax.fori_loop(0, ROWS, one_row, 0)
+
+
+def synth_kernel(lats, recv, tables, coarse, out, scr, lhs, rows, fine, sems, in_sems):
+    def fetch(q):
+        return pltpu.make_async_copy(tables.at[q], fine.at[q], in_sems.at[q])
+
+    for q in range(ROWS):
+        fetch(q).start()
+    for i in range(7):
+        scr[512 * i : 512 * (i + 1), :] = (
+            recv[64 * i : 64 * (i + 1)].astype(jnp.float32).reshape(512, 128))
+    scr[KEEP * ROWS : KP * ROWS, :] = jnp.zeros(((KP - KEEP) * ROWS, 128), jnp.float32)
 
     row = lax.broadcasted_iota(jnp.int32, (128, 128), 0)
     col = lax.broadcasted_iota(jnp.int32, (128, 128), 1)
     source = jnp.where(row < 64, 2 * row, 2 * row - 127)
     perm = jnp.where(col == source, 1.0, 0.0).astype(jnp.bfloat16)
-    values = scr[pl.ds(q, KP, stride=ROWS), :].astype(jnp.bfloat16)
+    column = lax.broadcasted_iota(jnp.int32, (64, FINE), 1)
     nt = (((1,), (1,)), ((), ()))
-    turned = lax.dot_general(perm, values, nt, preferred_element_type=jnp.float32)
-    re = turned[0:64, :]
-    im = turned[64:128, :]
-    for jc in range(COARSE):
-        cc = coarse[0, jc : jc + 1, 0:KP]
-        sc = coarse[0, jc : jc + 1, KP : 2 * KP]
-        lhs[64 * jc : 64 * (jc + 1), 0:KP] = (cc * re - sc * im).astype(jnp.bfloat16)
-        lhs[64 * jc : 64 * (jc + 1), KP : 2 * KP] = (sc * re + cc * im).astype(jnp.bfloat16)
-    result = lax.dot_general(lhs[...], fine[0], nt, preferred_element_type=jnp.float32)
-    column = lax.broadcasted_iota(jnp.int32, (64, FINE), 1)
-    for jc in range(COARSE):
-        width = min(FINE, WIDTH - FINE * jc)
-        block = result[64 * jc : 64 * (jc + 1), :]
-        block = jnp.where(column < lon - FINE * jc, block, 0.0).astype(jnp.bfloat16)
-        out[0, :, FINE * jc : FINE * jc + width] = block[:, 0:width]
+
+    def rotate(q, to):
+        values = scr[pl.ds(q, KP, stride=ROWS), :].astype(jnp.bfloat16)
+        turned = lax.dot_general(perm, values, nt, preferred_element_type=jnp.float32)
+        re = turned[0:64, :]
+        im = turned[64:128, :]
+        for jc in range(COARSE):
+            cc = coarse[q, jc : jc + 1, 0:KP]
+            sc = coarse[q, jc : jc + 1, KP : 2 * KP]
+            at = slice(64 * jc, 64 * (jc + 1))
+            lhs[to, at, 0:KP] = (cc * re - sc * im).astype(jnp.bfloat16)
+            lhs[to, at, KP : 2 * KP] = (sc * re + cc * im).astype(jnp.bfloat16)
+
+    def copy(q):
+        return pltpu.make_async_copy(rows.at[q], out.at[q], sems.at[q])
+
+    def one_row(q, carry):
+        slot = lax.rem(q, 2)
+        fetch(q).wait()
+        a = lats[q]
+        lon = 20 + 4 * jnp.minimum(a, NLAT - 1 - a)
+        result = lax.dot_general(lhs[slot], fine[q], nt, preferred_element_type=jnp.float32)
+        rotate(jnp.minimum(q + 1, ROWS - 1), 1 - slot)
+        for jc in range(COARSE):
+            width = min(FINE, WIDTH - FINE * jc)
+            block = result[64 * jc : 64 * (jc + 1), :]
+            block = jnp.where(column < lon - FINE * jc, block, 0.0).astype(jnp.bfloat16)
+            rows[q, :, FINE * jc : FINE * jc + width] = block[:, 0:width]
+        copy(q).start()
+        return carry
+
+    rotate(0, 0)
+    lax.fori_loop(0, ROWS, one_row, 0)
+    for q in range(ROWS):
+        copy(q).wait()
 
 
 def cost(flops, moved):
@@ -175,61 +199,69 @@
     waves = jnp.where(wave_pair[:, None] >= 0, waves, -1).reshape(1, KEEP)
     waves = jnp.pad(waves, ((0, 0), (0, KP - KEEP)), constant_values=-1).astype(f32)
 
+    def here(v):
+        return pltpu.with_memory_space_constraint(v, pltpu.VMEM)
+
+    def params(mib):
+        return pltpu.CompilerParams(vmem_limit_bytes=mib * 2**20)
+
     packed = pl.pallas_call(
         pack_kernel,
-        out_shape=jax.ShapeDtypeStruct((QBLK, PACKED), bf16),
+        out_shape=pltpu.VMEM((QBLK, PACKED), bf16),
         in_specs=[vmem], out_specs=vmem,
         scratch_shapes=[pltpu.VMEM((QBLK, 128), f32)],
+        compiler_params=params(4),
         name="pack",
     )(jnp.transpose(legendre, (0, 2, 1)))
     pieces = gather_pieces(packed)
 
     rhs = pl.pallas_call(
         mask_kernel,
-        out_shape=jax.ShapeDtypeStruct((SLOTS, KP, 256), bf16),
+        out_shape=pltpu.VMEM((SLOTS, KP, 256), bf16),
         in_specs=[smem, vmem], out_specs=vmem,
         scratch_shapes=[pltpu.VMEM((128, 128), f32)],
         cost_estimate=cost(2_000_000_000, 2_500_000),
+        compiler_params=params(6),
         name="mask",
     )(own_pairs, spectral)
 
     fine, coarse = pl.pallas_call(
         table_kernel,
-        out_shape=(jax.ShapeDtypeStruct((ROWS, FINE, 2 * KP), bf16),
-                   jax.ShapeDtypeStruct((ROWS, 8, 2 * KP), f32)),
-        grid_spec=pltpu.PrefetchScalarGridSpec(
-            num_scalar_prefetch=1, grid=(ROWS,),
-            in_specs=[pl.BlockSpec((1, KP), lambda q, lats: (0, 0))],
-            out_specs=(pl.BlockSpec((1, FINE, 2 * KP), lambda q, lats: (q, 0, 0)),
-                       pl.BlockSpec((1, 8, 2 * KP), lambda q, lats: (q, 0, 0)))),
+        out_shape=(pltpu.HBM((ROWS, FINE, 2 * KP), bf16),
+                   pltpu.VMEM((ROWS, 8, 2 * KP), f32)),
+        in_specs=[smem, vmem], out_specs=(vmem, vmem),
         cost_estimate=cost(4_000_000_000, 4_500_000),
+        compiler_params=params(8),
         name="tables",
     )(own_lats, waves)
 
     fourier = pl.pallas_call(
         legendre_kernel,
-        out_shape=jax.ShapeDtypeStruct((32, 2 * SLOTS, ROWS, 128), bf16),
+        out_shape=pltpu.VMEM((32, 2 * SLOTS, ROWS, 128), bf16),
         in_specs=[smem] + [vmem] * 10, out_specs=vmem,
         cost_estimate=cost(2 * 256 * 512 * 256 * SLOTS, 4_000_000),
+        compiler_params=params(12),
         name="legendre",
-    )(z.reshape(1), rhs, *pieces)
+    )(z.reshape(1), here(rhs), *[here(p) for p in pieces])
 
     received = lax.all_to_all(fourier, "wav", split_axis=0, concat_axis=0, tiled=True)
 
     return pl.pallas_call(
         synth_kernel,
         out_shape=jax.ShapeDtypeStruct((ROWS, 64, WIDTH), bf16),
-        grid_spec=pltpu.PrefetchScalarGridSpec(
-            num_scalar_prefetch=1, grid=(ROWS,),
-            in_specs=[pl.BlockSpec((KEEP, ROWS, 128), lambda q, lats: (0, 0, 0)),
-                      pl.BlockSpec((1, FINE, 2 * KP), lambda q, lats: (q, 0, 0)),
-                      pl.BlockSpec((1, 8, 2 * KP), lambda q, lats: (q, 0, 0))],
-            out_specs=pl.BlockSpec((1, 64, WIDTH), lambda q, lats: (q, 0, 0)),
-            scratch_shapes=[pltpu.VMEM((KP * ROWS, 128), f32),
-                            pltpu.VMEM((64 * COARSE, 2 * KP), bf16)]),
+        in_specs=[smem, vmem, pl.BlockSpec(memory_space=pltpu.HBM), vmem],
+        out_specs=pl.BlockSpec(memory_space=pltpu.HBM),
+        scratch_shapes=[pltpu.VMEM((KP * ROWS, 128), f32),
+                        pltpu.VMEM((2, 64 * COARSE, 2 * KP), bf16),
+                        pltpu.VMEM((ROWS, 64, WIDTH), bf16),
+                        pltpu.VMEM((ROWS, FINE, 2 * KP), bf16),
+                        pltpu.SemaphoreType.DMA((ROWS,)),
+                        pltpu.SemaphoreType.DMA((ROWS,))],
         cost_estimate=cost(2 * 448 * 1024 * 256 * ROWS, 18_000_000),
+        compiler_params=params(16),
         name="synth",
-    )(own_lats, received.reshape(KEEP, ROWS, 128), fine, coarse)
+    )(own_lats, here(received.reshape(KEEP, ROWS, 128)),
+      pltpu.with_memory_space_constraint(fine, pltpu.HBM), here(coarse))
 
 
 def solution(mesh):

time: 71.4 us -> 65.6 us (0.919)
  Pallas kernels: 23.8 us -> 15.8 us
  waiting for transfers between devices: 15.7 us -> 19 us
    pallas_call x4, Pallas kernels: 14.4 us -> 7.81 us  [the longest x1 4.94 us: on_device(): pl.pallas_call(table_kernel, out_shape=(pltpu.HBM((ROWS, FINE, 2 * KP), b...]
    all_to_all x1, waiting for transfers between devices: 8.07 us -> 10.3 us  [on_device(): lax.all_to_all(fourier, 'wav', split_axis=0, concat_axis=0, tiled=True)]
    pallas_call x1, Pallas kernels: 9.38 us -> 8.03 us  [on_device(): pl.pallas_call(synth_kernel, out_shape=jax.ShapeDtypeStruct((ROWS, 64, WI...]
    ppermute x8, waiting for transfers between devices: 7.63 us -> 8.75 us  [shift(): return lax.ppermute(v, 'lev', [(i, (i + d) % 8) for i in range(8)])]
    unnamed x22 -> x8, local copies, waits for them, and re-layouts: 1.62 us -> 2.06 us
  transfers between devices with their start and end apart: 9 -> 9, of which waited for: 5 -> 4; matrix products, arithmetic and copies ran while one was open for 5% -> 3% of each run, Pallas kernels for 13% -> 9%
where the time goes in v2:
time: 65.6 us; the launch traced here: 65.3 us
  starting transfers between devices  26.5 us (40%)
  waiting for transfers between devices  19 us (29%)
  Pallas kernels  15.8 us (24%)
  local copies, waits for them, and re-layouts  3.17 us (5%)
  other arithmetic  0.7 us (1%)
    ppermute x8, starting transfers between devices, shift(): return lax.ppermute(v, 'lev', [(i, (i + d) % 8) for i in range(8)])  17.9 us
    all_to_all x1, waiting for transfers between devices, on_device(): lax.all_to_all(fourier, 'wav', split_axis=0, concat_axis=0, tiled=True)  10.3 us
    ppermute x8, waiting for transfers between devices, shift(): return lax.ppermute(v, 'lev', [(i, (i + d) % 8) for i in range(8)])  8.75 us
    all_to_all x1, starting transfers between devices, on_device(): lax.all_to_all(fourier, 'wav', split_axis=0, concat_axis=0, tiled=True)  8.61 us
    pallas_call x1, Pallas kernels, on_device(): pl.pallas_call(synth_kernel, out_shape=jax.ShapeDtypeStruct((ROWS, 64, WI...  8.03 us
    pallas_call x1, Pallas kernels, on_device(): pl.pallas_call(table_kernel, out_shape=(pltpu.HBM((ROWS, FINE, 2 * KP), b...  4.94 us
    unnamed x8, local copies, waits for them, and re-layouts  2.06 us
    pallas_call x1, Pallas kernels, on_device(): pl.pallas_call(legendre_kernel, out_shape=pltpu.VMEM((32, 2 * SLOTS, ROWS...  1.6 us
  transfers between devices with their start and end apart: 9, of which 4 were waited for; matrix products, arithmetic and copies ran while one was open for 3% of the time, Pallas kernels for 9%

profile of v2, /device:TPU:1, one launch (start us, length us, event | category | flops | bytes accessed | tf_op | source)
XLA Modules:
  0.0 65.3 jit_solution(3769241902702665668)
XLA Ops:
  0.0 0.9 %copy-done = bf16[7,401,32]{1,2,0:T(8,128)(2,1)S(1)} copy-done((bf16[7,401,32]{1,2,0:T(8,128)(2,1)S(1)}, bf16[7,401,32]{1,2,0:T(8,128)(2,1)}, u32[]{:S(2)}) %copy-start) | copy-done | bytes 179672
  0.9 0.1 pack.1.x0
  1.1 6.9 %collective-permute-start.3 = (bf16[32,2816]{1,0:T(8,128)(2,1)S(1)}, bf16[32,2816]{1,0:T(8,128)(2,1)S(1)}, u32[]{:S(2)}, u32[]{:S(2)}) collective-permute-start(bf16[32,2816]{1,0:T(8,128)(2,1)S(1)} %pack.1.x0), channel_id=1, source_target_pairs={{0,6},{1,7},{2,0},{3,1},{4,2},{5,3},{6,4},{7,5},{8,14},{9,15},{10,... | collective-permute-start | bytes 540680 | tf_op jit(solution)/shard_map/ppermute | solution.py:180
  8.0 0.0 collective-permute-start.2
  8.0 3.1 %collective-permute-start.1 = (bf16[32,2816]{1,0:T(8,128)(2,1)S(1)}, bf16[32,2816]{1,0:T(8,128)(2,1)S(1)}, u32[]{:S(2)}, u32[]{:S(2)}) collective-permute-start(bf16[32,2816]{1,0:T(8,128)(2,1)S(1)} %pack.1.x0), channel_id=1, source_target_pairs={{0,7},{1,0},{2,1},{3,2},{4,3},{5,4},{6,5},{7,6},{8,15},{9,8},{10,9... | collective-permute-start | bytes 540680 | tf_op jit(solution)/shard_map/ppermute | solution.py:180
  11.1 0.0 collective-permute-start
  11.1 0.8 %dynamic_slice.7.pairs = s32[7]{0:T(128)S(1)} dynamic-slice(s32[224]{0:T(256)} %param.6, s32[]{:T(128)S(6)} %select_n.21), dynamic_slice_sizes={7} | dynamic-slice | bytes 60 | tf_op jit(solution)/shard_map/dynamic_slice | solution.py:196
  11.8 0.7 %broadcast_subtract_fusion = s32[224]{0:T(256)S(1)} fusion(s32[224]{0:T(256)} %param.6), kind=kLoop, calls=%fused_computation.2 | loop fusion | flops 224 | bytes 1792 | tf_op jit(solution)/shard_map/sub | solution.py:198
  12.5 1.9 %collective-permute-done.3.m2 = bf16[32,2816]{1,0:T(8,128)(2,1)S(1)} collective-permute-done((bf16[32,2816]{1,0:T(8,128)(2,1)S(1)}, bf16[32,2816]{1,0:T(8,128)(2,1)S(1)}, u32[]{:S(2)}, u32[]{:S(2)}) %collective-permute-start.3) | collective-permute-done | bytes 180256 | tf_op jit(solution)/shard_map/ppermute | solution.py:180
  14.4 5.3 %collective-permute-start.7 = (bf16[16,2816]{1,0:T(8,128)(2,1)S(1)}, bf16[16,2816]{1,0:T(8,128)(2,1)S(1)}, u32[]{:S(2)}, u32[]{:S(2)}) collective-permute-start(bf16[16,2816]{1,0:T(8,128)(2,1)S(1)} %slice.9), channel_id=1, source_target_pairs={{0,6},{1,7},{2,0},{3,1},{4,2},{5,3},{6,4},{7,5},{8,14},{9,15},{10,... | collective-permute-start | bytes 270344 | tf_op jit(solution)/shard_map/ppermute | solution.py:180
  19.7 0.1 collective-permute-start.6
  19.8 2.4 %collective-permute-start.5 = (bf16[32,2816]{1,0:T(8,128)(2,1)S(1)}, bf16[32,2816]{1,0:T(8,128)(2,1)S(1)}, u32[]{:S(2)}, u32[]{:S(2)}) collective-permute-start(bf16[32,2816]{1,0:T(8,128)(2,1)S(1)} %collective-permute-done.3.m2), channel_id=1, source_target_pairs={{0,7},{1,0},{2,1},{3,2},{4,3},{5,4},{6,5},{7,6},{8,15},{9,8},{10,9... | collective-permute-start | bytes 540680 | tf_op jit(solution)/shard_map/ppermute | solution.py:180
  22.3 1.1 %copy-done.1 = bf16[7,401,128]{2,1,0:T(8,128)(2,1)S(1)} copy-done((bf16[7,401,128]{2,1,0:T(8,128)(2,1)S(1)}, bf16[7,401,128]{2,1,0:T(8,128)(2,1)}, u32[]{:S(2)}) %copy-start.1) | copy-done | bytes 718616
  23.4 1.2 %mask.1.rhs = bf16[7,512,256]{2,1,0:T(8,128)(2,1)S(1)} custom-call(s32[7]{0:T(128)S(1)} %dynamic_slice.7.pairs, bf16[7,401,128]{2,1,0:T(8,128)(2,1)S(1)} %copy-done.1), custom_call_target="tpu_custom_call" | custom-call | flops 2000000000 | bytes 2500000 | tf_op jit(solution)/shard_map/mask/pallas_call | solution.py:218
  24.6 2.0 %collective-permute-done.6.p4 = bf16[16,2816]{1,0:T(8,128)(2,1)S(1)} collective-permute-done((bf16[16,2816]{1,0:T(8,128)(2,1)S(1)}, bf16[16,2816]{1,0:T(8,128)(2,1)S(1)}, u32[]{:S(2)}, u32[]{:S(2)}) %collective-permute-start.6) | collective-permute-done | bytes 90144 | tf_op jit(solution)/shard_map/ppermute | solution.py:180
  26.5 4.9 %collective-permute-done.4.p3 = bf16[32,2816]{1,0:T(8,128)(2,1)S(1)} collective-permute-done((bf16[32,2816]{1,0:T(8,128)(2,1)S(1)}, bf16[32,2816]{1,0:T(8,128)(2,1)S(1)}, u32[]{:S(2)}, u32[]{:S(2)}) %collective-permute-start.4) | collective-permute-done | bytes 180256 | tf_op jit(solution)/shard_map/ppermute | solution.py:180
  31.4 1.6 %legendre.1 = bf16[32,14,8,128]{3,2,1,0:T(8,128)(2,1)} custom-call(s32[1]{0:T(128)} %bitcast.place, bf16[7,512,256]{2,1,0:T(8,128)(2,1)S(1)} %mask.1.rhs, bf16[32,2816]{1,0:T(8,128)(2,1)S(1)} %pack.1.x0, bf16[32,2816]{1,0:T(8,128)(2,1)S(1)} %collective-permute-done.p1, bf16[32,2816]{1,0:T(8,128)(2,1)S(1)} %collective-permute-done.1.m1, ...), custom_call_target="tpu_custom_call" | custom-call | flops 469762048 | bytes 4000000 | tf_op jit(solution)/shard_map/legendre/pallas_call | solution.py:238
  33.0 8.6 %all-to-all-start = ((bf16[32,14,8,128]{3,2,1,0:T(8,128)(2,1)}), bf16[32,14,8,128]{3,2,1,0:T(8,128)(2,1)S(1)}, u32[]{:S(2)}, u32[]{:S(2)}) async-start(bf16[32,14,8,128]{3,2,1,0:T(8,128)(2,1)} %legendre.1), calls=%async_computation | async-start | bytes 1835008 | tf_op jit(solution)/shard_map/all_to_all | solution.py:247
  41.7 0.1 copy.5
  41.8 0.1 select_n.23
  42.0 0.1 dynamic_slice.6.lats
  42.1 4.9 %tables.1 = (bf16[8,256,1024]{2,1,0:T(8,128)(2,1)}, f32[8,8,1024]{2,1,0:T(8,128)S(1)}) custom-call(s32[8]{0:T(128)S(1)} %dynamic_slice.6.lats, f32[1,512]{1,0:T(1,128)S(1)} %pad_convert_fusion.waves), custom_call_target="tpu_custom_call" | custom-call | flops 4000000000 | bytes 4500000 | tf_op jit(solution)/shard_map/tables/pallas_call | solution.py:228
  47.0 10.3 %all-to-all-done = bf16[32,14,8,128]{3,2,1,0:T(8,128)(2,1)S(1)} async-done(((bf16[32,14,8,128]{3,2,1,0:T(8,128)(2,1)}), bf16[32,14,8,128]{3,2,1,0:T(8,128)(2,1)S(1)}, u32[]{:S(2)}, u32[]{:S(2)}) %all-to-all-start) | async-done | bytes 917536 | tf_op jit(solution)/shard_map/all_to_all | solution.py:247
  57.3 8.0 %synth.1 = bf16[8,64,1616]{2,1,0:T(8,128)(2,1)} custom-call(s32[8]{0:T(128)S(1)} %dynamic_slice.6.lats, bf16[448,8,128]{2,1,0:T(8,128)(2,1)S(1)} %bitcast.5, bf16[8,256,1024]{2,1,0:T(8,128)(2,1)} %get-tuple-element.7.tables, f32[8,8,1024]{2,1,0:T(8,128)S(1)} %get-tuple-element.8.coarse), custom_call_target="tpu_custom_call" | custom-call | flops 1879048192 | bytes 18000000 | tf_op jit(solution)/shard_map/synth/pallas_call | solution.py:249
  (17 shorter events, 0.1 us)
Async XLA Ops:
  0.0 0.9 %copy-start = (bf16[7,401,32]{1,2,0:T(8,128)(2,1)S(1)}, bf16[7,401,32]{1,2,0:T(8,128)(2,1)}, u32[]{:S(2)}) copy-start(bf16[7,401,32]{1,2,0:T(8,128)(2,1)} %param.5) | copy-start | bytes 538948
  1.1 13.4 %collective-permute-start.3 = (bf16[32,2816]{1,0:T(8,128)(2,1)S(1)}, bf16[32,2816]{1,0:T(8,128)(2,1)S(1)}, u32[]{:S(2)}, u32[]{:S(2)}) collective-permute-start(bf16[32,2816]{1,0:T(8,128)(2,1)S(1)} %pack.1.x0), channel_id=1, source_target_pairs={{0,6},{1,7},{2,0},{3,1},{4,2},{5,3},{6,4},{7,5},{8,14},{9,15},{10,... | collective-permute-start | bytes 540680 | tf_op jit(solution)/shard_map/ppermute | solution.py:180
  8.0 11.8 %collective-permute-start.2 = (bf16[32,2816]{1,0:T(8,128)(2,1)S(1)}, bf16[32,2816]{1,0:T(8,128)(2,1)S(1)}, u32[]{:S(2)}, u32[]{:S(2)}) collective-permute-start(bf16[32,2816]{1,0:T(8,128)(2,1)S(1)} %pack.1.x0), channel_id=1, source_target_pairs={{0,2},{1,3},{2,4},{3,5},{4,6},{5,7},{6,0},{7,1},{8,10},{9,11},{10,... | collective-permute-start | bytes 540680 | tf_op jit(solution)/shard_map/ppermute | solution.py:180
  8.0 14.3 %collective-permute-start.1 = (bf16[32,2816]{1,0:T(8,128)(2,1)S(1)}, bf16[32,2816]{1,0:T(8,128)(2,1)S(1)}, u32[]{:S(2)}, u32[]{:S(2)}) collective-permute-start(bf16[32,2816]{1,0:T(8,128)(2,1)S(1)} %pack.1.x0), channel_id=1, source_target_pairs={{0,7},{1,0},{2,1},{3,2},{4,3},{5,4},{6,5},{7,6},{8,15},{9,8},{10,9... | collective-permute-start | bytes 540680 | tf_op jit(solution)/shard_map/ppermute | solution.py:180
  11.1 13.5 %collective-permute-start = (bf16[32,2816]{1,0:T(8,128)(2,1)S(1)}, bf16[32,2816]{1,0:T(8,128)(2,1)S(1)}, u32[]{:S(2)}, u32[]{:S(2)}) collective-permute-start(bf16[32,2816]{1,0:T(8,128)(2,1)S(1)} %pack.1.x0), channel_id=1, source_target_pairs={{0,1},{1,2},{2,3},{3,4},{4,5},{5,6},{6,7},{7,0},{8,9},{9,10},{10,1... | collective-permute-start | bytes 540680 | tf_op jit(solution)/shard_map/ppermute | solution.py:180
  14.4 10.1 %collective-permute-start.7 = (bf16[16,2816]{1,0:T(8,128)(2,1)S(1)}, bf16[16,2816]{1,0:T(8,128)(2,1)S(1)}, u32[]{:S(2)}, u32[]{:S(2)}) collective-permute-start(bf16[16,2816]{1,0:T(8,128)(2,1)S(1)} %slice.9), channel_id=1, source_target_pairs={{0,6},{1,7},{2,0},{3,1},{4,2},{5,3},{6,4},{7,5},{8,14},{9,15},{10,... | collective-permute-start | bytes 270344 | tf_op jit(solution)/shard_map/ppermute | solution.py:180
  19.7 6.8 %collective-permute-start.6 = (bf16[16,2816]{1,0:T(8,128)(2,1)S(1)}, bf16[16,2816]{1,0:T(8,128)(2,1)S(1)}, u32[]{:S(2)}, u32[]{:S(2)}) collective-permute-start(bf16[16,2816]{1,0:T(8,128)(2,1)S(1)} %slice.8), channel_id=1, source_target_pairs={{0,2},{1,3},{2,4},{3,5},{4,6},{5,7},{6,0},{7,1},{8,10},{9,11},{10,... | collective-permute-start | bytes 270344 | tf_op jit(solution)/shard_map/ppermute | solution.py:180
  19.8 6.7 %collective-permute-start.5 = (bf16[32,2816]{1,0:T(8,128)(2,1)S(1)}, bf16[32,2816]{1,0:T(8,128)(2,1)S(1)}, u32[]{:S(2)}, u32[]{:S(2)}) collective-permute-start(bf16[32,2816]{1,0:T(8,128)(2,1)S(1)} %collective-permute-done.3.m2), channel_id=1, source_target_pairs={{0,7},{1,0},{2,1},{3,2},{4,3},{5,4},{6,5},{7,6},{8,15},{9,8},{10,9... | collective-permute-start | bytes 540680 | tf_op jit(solution)/shard_map/ppermute | solution.py:180
  22.3 9.2 %collective-permute-start.4 = (bf16[32,2816]{1,0:T(8,128)(2,1)S(1)}, bf16[32,2816]{1,0:T(8,128)(2,1)S(1)}, u32[]{:S(2)}, u32[]{:S(2)}) collective-permute-start(bf16[32,2816]{1,0:T(8,128)(2,1)S(1)} %collective-permute-done.2.p2), channel_id=1, source_target_pairs={{0,1},{1,2},{2,3},{3,4},{4,5},{5,6},{6,7},{7,0},{8,9},{9,10},{10,1... | collective-permute-start | bytes 540680 | tf_op jit(solution)/shard_map/ppermute | solution.py:180
  22.3 1.1 %copy-start.1 = (bf16[7,401,128]{2,1,0:T(8,128)(2,1)S(1)}, bf16[7,401,128]{2,1,0:T(8,128)(2,1)}, u32[]{:S(2)}) copy-start(bf16[7,401,128]{2,1,0:T(8,128)(2,1)} %spec.1) | copy-start | bytes 2155780
  33.0 8.6 %copy-start.2 = (s32[224]{0:T(256)S(1)}, s32[224]{0:T(256)}, u32[]{:S(2)}) copy-start(s32[224]{0:T(256)} %param.6) | copy-start | bytes 2692
  33.0 8.9 %copy-start.3 = (s32[256]{0:T(256)S(1)}, s32[256]{0:T(256)}, u32[]{:S(2)}) copy-start(s32[256]{0:T(256)} %param.7) | copy-start | bytes 3076
  33.0 24.3 %all-to-all-start = ((bf16[32,14,8,128]{3,2,1,0:T(8,128)(2,1)}), bf16[32,14,8,128]{3,2,1,0:T(8,128)(2,1)S(1)}, u32[]{:S(2)}, u32[]{:S(2)}) async-start(bf16[32,14,8,128]{3,2,1,0:T(8,128)(2,1)} %legendre.1), calls=%async_computation | async-start | bytes 1835008 | tf_op jit(solution)/shard_map/all_to_all | solution.py:247

commit v3 on v2

--- a/solution.py
+++ b/solution.py
@@ -109,7 +109,9 @@
             rows = slice(32 * i, 32 * (i + 1))
             fine[q, rows, 0:KP] = (ca * cos_b - sa * sin_b).astype(jnp.bfloat16)
             fine[q, rows, KP : 2 * KP] = (-(sa * cos_b + ca * sin_b)).astype(jnp.bfloat16)
-        cos_c, sin_c = at(FINE, 8)
+        step = lax.broadcasted_iota(jnp.int32, (8, KP), 0)
+        step = FINE * jnp.where(step == 0, 3, step)
+        cos_c, sin_c = cos_sin(step.astype(jnp.float32) * m, n, inv)
         coarse[q, :, 0:KP] = cos_c
         coarse[q, :, KP : 2 * KP] = sin_c
         return carry
@@ -117,7 +119,8 @@
     lax.fori_loop(0, ROWS, one_row, 0)
 
 
-def synth_kernel(lats, recv, tables, coarse, out, scr, lhs, rows, fine, sems, in_sems):
+def synth_kernel(lats, recv, tables, coarse, out, scr, turn_a, turn_b, lhs_a, lhs_b, rows,
+                 fine, sems, in_sems):
     def fetch(q):
         return pltpu.make_async_copy(tables.at[q], fine.at[q], in_sems.at[q])
 
@@ -135,38 +138,65 @@
     column = lax.broadcasted_iota(jnp.int32, (64, FINE), 1)
     nt = (((1,), (1,)), ((), ()))
 
-    def rotate(q, to):
+    def turn_row(q, turn):
         values = scr[pl.ds(q, KP, stride=ROWS), :].astype(jnp.bfloat16)
-        turned = lax.dot_general(perm, values, nt, preferred_element_type=jnp.float32)
-        re = turned[0:64, :]
-        im = turned[64:128, :]
-        for jc in range(COARSE):
-            cc = coarse[q, jc : jc + 1, 0:KP]
-            sc = coarse[q, jc : jc + 1, KP : 2 * KP]
-            at = slice(64 * jc, 64 * (jc + 1))
-            lhs[to, at, 0:KP] = (cc * re - sc * im).astype(jnp.bfloat16)
-            lhs[to, at, KP : 2 * KP] = (sc * re + cc * im).astype(jnp.bfloat16)
+        turn[...] = lax.dot_general(perm, values, nt, preferred_element_type=jnp.float32)
+
+    def rotate(q, turn, lhs):
+        for lane in range(0, KP, 128):
+            here = slice(lane, lane + 128)
+            beside = slice(KP + lane, KP + lane + 128)
+            for g in range(0, 64, 16):
+                def put(block, left, right):
+                    at = slice(64 * block + g, 64 * block + g + 16)
+                    lhs[at, here] = left.astype(jnp.bfloat16)
+                    lhs[at, beside] = right.astype(jnp.bfloat16)
+
+                re = turn[g : g + 16, here]
+                im = turn[64 + g : 80 + g, here]
+                cc = coarse[q, 0:1, here]
+                sc = coarse[q, 0:1, beside]
+                re, im = cc * re - sc * im, sc * re + cc * im
+                put(0, re, im)
+                for step in range(1, 4):
+                    cc = coarse[q, step : step + 1, here]
+                    sc = coarse[q, step : step + 1, beside]
+                    put(2 * step - 1, cc * re, cc * im)
+                    put(2 * step, sc * im, -sc * re)
 
     def copy(q):
         return pltpu.make_async_copy(rows.at[q], out.at[q], sems.at[q])
 
-    def one_row(q, carry):
-        slot = lax.rem(q, 2)
+    def one_row(q, lhs, other, turn, spare):
         fetch(q).wait()
         a = lats[q]
         lon = 20 + 4 * jnp.minimum(a, NLAT - 1 - a)
-        result = lax.dot_general(lhs[slot], fine[q], nt, preferred_element_type=jnp.float32)
-        rotate(jnp.minimum(q + 1, ROWS - 1), 1 - slot)
-        for jc in range(COARSE):
+        result = lax.dot_general(lhs[...], fine[q], nt, preferred_element_type=jnp.float32)
+        rotate(jnp.minimum(q + 1, ROWS - 1), turn, other)
+        turn_row(jnp.minimum(q + 2, ROWS - 1), spare)
+
+        def put(jc, block):
             width = min(FINE, WIDTH - FINE * jc)
-            block = result[64 * jc : 64 * (jc + 1), :]
             block = jnp.where(column < lon - FINE * jc, block, 0.0).astype(jnp.bfloat16)
             rows[q, :, FINE * jc : FINE * jc + width] = block[:, 0:width]
+
+        put(3, result[0:64, :])
+        for step in range(1, 4):
+            even = result[128 * step - 64 : 128 * step, :]
+            odd = result[128 * step : 128 * step + 64, :]
+            put(3 + step, even - odd)
+            put(3 - step, even + odd)
         copy(q).start()
+
+    def two_rows(i, carry):
+        one_row(2 * i, lhs_a, lhs_b, turn_b, turn_a)
+        one_row(2 * i + 1, lhs_b, lhs_a, turn_a, turn_b)
         return carry
 
-    rotate(0, 0)
-    lax.fori_loop(0, ROWS, one_row, 0)
+    turn_row(0, turn_a)
+    turn_row(1, turn_b)
+    rotate(0, turn_a, lhs_a)
+    lax.fori_loop(0, ROWS // 2, two_rows, 0)
     for q in range(ROWS):
         copy(q).wait()
 
@@ -252,7 +282,10 @@
         in_specs=[smem, vmem, pl.BlockSpec(memory_space=pltpu.HBM), vmem],
         out_specs=pl.BlockSpec(memory_space=pltpu.HBM),
         scratch_shapes=[pltpu.VMEM((KP * ROWS, 128), f32),
-                        pltpu.VMEM((2, 64 * COARSE, 2 * KP), bf16),
+                        pltpu.VMEM((128, KP), f32),
+                        pltpu.VMEM((128, KP), f32),
+                        pltpu.VMEM((64 * COARSE, 2 * KP), bf16),
+                        pltpu.VMEM((64 * COARSE, 2 * KP), bf16),
                         pltpu.VMEM((ROWS, 64, WIDTH), bf16),
                         pltpu.VMEM((ROWS, FINE, 2 * KP), bf16),
                         pltpu.SemaphoreType.DMA((ROWS,)),

time: 65.6 us -> 66.6 us (1.015)
  Pallas kernels: 15.8 us -> 16.8 us
    pallas_call x1, Pallas kernels: 8.03 us -> 9.02 us  [on_device(): pl.pallas_call(synth_kernel, out_shape=jax.ShapeDtypeStruct((ROWS, 64, WI...]
where the time goes in v3:
time: 66.6 us; the launch traced here: 66.3 us
  starting transfers between devices  26.5 us (40%)
  waiting for transfers between devices  19 us (29%)
  Pallas kernels  16.8 us (25%)
  local copies, waits for them, and re-layouts  3.17 us (5%)
  other arithmetic  0.7 us (1%)
    ppermute x8, starting transfers between devices, shift(): return lax.ppermute(v, 'lev', [(i, (i + d) % 8) for i in range(8)])  17.9 us
    all_to_all x1, waiting for transfers between devices, on_device(): lax.all_to_all(fourier, 'wav', split_axis=0, concat_axis=0, tiled=True)  10.3 us
    pallas_call x1, Pallas kernels, on_device(): pl.pallas_call(synth_kernel, out_shape=jax.ShapeDtypeStruct((ROWS, 64, WI...  9.02 us
    ppermute x8, waiting for transfers between devices, shift(): return lax.ppermute(v, 'lev', [(i, (i + d) % 8) for i in range(8)])  8.75 us
    all_to_all x1, starting transfers between devices, on_device(): lax.all_to_all(fourier, 'wav', split_axis=0, concat_axis=0, tiled=True)  8.61 us
    pallas_call x1, Pallas kernels, on_device(): pl.pallas_call(table_kernel, out_shape=(pltpu.HBM((ROWS, FINE, 2 * KP), b...  4.95 us
    unnamed x8, local copies, waits for them, and re-layouts  2.06 us
    pallas_call x1, Pallas kernels, on_device(): pl.pallas_call(legendre_kernel, out_shape=pltpu.VMEM((32, 2 * SLOTS, ROWS...  1.6 us
  transfers between devices with their start and end apart: 9, of which 4 were waited for; matrix products, arithmetic and copies ran while one was open for 3% of the time, Pallas kernels for 9%

profile of v3, /device:TPU:1, one launch (start us, length us, event | category | flops | bytes accessed | tf_op | source)
XLA Modules:
  0.0 66.3 jit_solution(6261966162311871269)
XLA Ops:
  0.0 0.9 %copy-done = bf16[7,401,32]{1,2,0:T(8,128)(2,1)S(1)} copy-done((bf16[7,401,32]{1,2,0:T(8,128)(2,1)S(1)}, bf16[7,401,32]{1,2,0:T(8,128)(2,1)}, u32[]{:S(2)}) %copy-start) | copy-done | bytes 179672
  0.9 0.1 pack.1.x0
  1.1 6.9 %collective-permute-start.3 = (bf16[32,2816]{1,0:T(8,128)(2,1)S(1)}, bf16[32,2816]{1,0:T(8,128)(2,1)S(1)}, u32[]{:S(2)}, u32[]{:S(2)}) collective-permute-start(bf16[32,2816]{1,0:T(8,128)(2,1)S(1)} %pack.1.x0), channel_id=1, source_target_pairs={{0,6},{1,7},{2,0},{3,1},{4,2},{5,3},{6,4},{7,5},{8,14},{9,15},{10,... | collective-permute-start | bytes 540680 | tf_op jit(solution)/shard_map/ppermute | solution.py:210
  8.0 0.0 collective-permute-start.2
  8.0 3.1 %collective-permute-start.1 = (bf16[32,2816]{1,0:T(8,128)(2,1)S(1)}, bf16[32,2816]{1,0:T(8,128)(2,1)S(1)}, u32[]{:S(2)}, u32[]{:S(2)}) collective-permute-start(bf16[32,2816]{1,0:T(8,128)(2,1)S(1)} %pack.1.x0), channel_id=1, source_target_pairs={{0,7},{1,0},{2,1},{3,2},{4,3},{5,4},{6,5},{7,6},{8,15},{9,8},{10,9... | collective-permute-start | bytes 540680 | tf_op jit(solution)/shard_map/ppermute | solution.py:210
  11.1 0.0 collective-permute-start
  11.1 0.8 %dynamic_slice.7.pairs = s32[7]{0:T(128)S(1)} dynamic-slice(s32[224]{0:T(256)} %param.6, s32[]{:T(128)S(6)} %select_n.21), dynamic_slice_sizes={7} | dynamic-slice | bytes 60 | tf_op jit(solution)/shard_map/dynamic_slice | solution.py:226
  11.8 0.7 %broadcast_subtract_fusion = s32[224]{0:T(256)S(1)} fusion(s32[224]{0:T(256)} %param.6), kind=kLoop, calls=%fused_computation.2 | loop fusion | flops 224 | bytes 1792 | tf_op jit(solution)/shard_map/sub | solution.py:228
  12.5 1.9 %collective-permute-done.3.m2 = bf16[32,2816]{1,0:T(8,128)(2,1)S(1)} collective-permute-done((bf16[32,2816]{1,0:T(8,128)(2,1)S(1)}, bf16[32,2816]{1,0:T(8,128)(2,1)S(1)}, u32[]{:S(2)}, u32[]{:S(2)}) %collective-permute-start.3) | collective-permute-done | bytes 180256 | tf_op jit(solution)/shard_map/ppermute | solution.py:210
  14.4 5.3 %collective-permute-start.7 = (bf16[16,2816]{1,0:T(8,128)(2,1)S(1)}, bf16[16,2816]{1,0:T(8,128)(2,1)S(1)}, u32[]{:S(2)}, u32[]{:S(2)}) collective-permute-start(bf16[16,2816]{1,0:T(8,128)(2,1)S(1)} %slice.9), channel_id=1, source_target_pairs={{0,6},{1,7},{2,0},{3,1},{4,2},{5,3},{6,4},{7,5},{8,14},{9,15},{10,... | collective-permute-start | bytes 270344 | tf_op jit(solution)/shard_map/ppermute | solution.py:210
  19.7 0.1 collective-permute-start.6
  19.8 2.4 %collective-permute-start.5 = (bf16[32,2816]{1,0:T(8,128)(2,1)S(1)}, bf16[32,2816]{1,0:T(8,128)(2,1)S(1)}, u32[]{:S(2)}, u32[]{:S(2)}) collective-permute-start(bf16[32,2816]{1,0:T(8,128)(2,1)S(1)} %collective-permute-done.3.m2), channel_id=1, source_target_pairs={{0,7},{1,0},{2,1},{3,2},{4,3},{5,4},{6,5},{7,6},{8,15},{9,8},{10,9... | collective-permute-start | bytes 540680 | tf_op jit(solution)/shard_map/ppermute | solution.py:210
  22.3 1.1 %copy-done.1 = bf16[7,401,128]{2,1,0:T(8,128)(2,1)S(1)} copy-done((bf16[7,401,128]{2,1,0:T(8,128)(2,1)S(1)}, bf16[7,401,128]{2,1,0:T(8,128)(2,1)}, u32[]{:S(2)}) %copy-start.1) | copy-done | bytes 718616
  23.4 1.2 %mask.1.rhs = bf16[7,512,256]{2,1,0:T(8,128)(2,1)S(1)} custom-call(s32[7]{0:T(128)S(1)} %dynamic_slice.7.pairs, bf16[7,401,128]{2,1,0:T(8,128)(2,1)S(1)} %copy-done.1), custom_call_target="tpu_custom_call" | custom-call | flops 2000000000 | bytes 2500000 | tf_op jit(solution)/shard_map/mask/pallas_call | solution.py:248
  24.6 2.0 %collective-permute-done.6.p4 = bf16[16,2816]{1,0:T(8,128)(2,1)S(1)} collective-permute-done((bf16[16,2816]{1,0:T(8,128)(2,1)S(1)}, bf16[16,2816]{1,0:T(8,128)(2,1)S(1)}, u32[]{:S(2)}, u32[]{:S(2)}) %collective-permute-start.6) | collective-permute-done | bytes 90144 | tf_op jit(solution)/shard_map/ppermute | solution.py:210
  26.5 4.9 %collective-permute-done.4.p3 = bf16[32,2816]{1,0:T(8,128)(2,1)S(1)} collective-permute-done((bf16[32,2816]{1,0:T(8,128)(2,1)S(1)}, bf16[32,2816]{1,0:T(8,128)(2,1)S(1)}, u32[]{:S(2)}, u32[]{:S(2)}) %collective-permute-start.4) | collective-permute-done | bytes 180256 | tf_op jit(solution)/shard_map/ppermute | solution.py:210
  31.4 1.6 %legendre.1 = bf16[32,14,8,128]{3,2,1,0:T(8,128)(2,1)} custom-call(s32[1]{0:T(128)} %bitcast.place, bf16[7,512,256]{2,1,0:T(8,128)(2,1)S(1)} %mask.1.rhs, bf16[32,2816]{1,0:T(8,128)(2,1)S(1)} %pack.1.x0, bf16[32,2816]{1,0:T(8,128)(2,1)S(1)} %collective-permute-done.p1, bf16[32,2816]{1,0:T(8,128)(2,1)S(1)} %collective-permute-done.1.m1, ...), custom_call_target="tpu_custom_call" | custom-call | flops 469762048 | bytes 4000000 | tf_op jit(solution)/shard_map/legendre/pallas_call | solution.py:268
  33.0 8.6 %all-to-all-start = ((bf16[32,14,8,128]{3,2,1,0:T(8,128)(2,1)}), bf16[32,14,8,128]{3,2,1,0:T(8,128)(2,1)S(1)}, u32[]{:S(2)}, u32[]{:S(2)}) async-start(bf16[32,14,8,128]{3,2,1,0:T(8,128)(2,1)} %legendre.1), calls=%async_computation | async-start | bytes 1835008 | tf_op jit(solution)/shard_map/all_to_all | solution.py:277
  41.7 0.1 copy.5
  41.8 0.1 select_n.23
  42.0 0.1 dynamic_slice.6.lats
  42.1 4.9 %tables.1 = (bf16[8,256,1024]{2,1,0:T(8,128)(2,1)}, f32[8,8,1024]{2,1,0:T(8,128)S(1)}) custom-call(s32[8]{0:T(128)S(1)} %dynamic_slice.6.lats, f32[1,512]{1,0:T(1,128)S(1)} %pad_convert_fusion.waves), custom_call_target="tpu_custom_call" | custom-call | flops 4000000000 | bytes 4500000 | tf_op jit(solution)/shard_map/tables/pallas_call | solution.py:258
  47.0 10.3 %all-to-all-done = bf16[32,14,8,128]{3,2,1,0:T(8,128)(2,1)S(1)} async-done(((bf16[32,14,8,128]{3,2,1,0:T(8,128)(2,1)}), bf16[32,14,8,128]{3,2,1,0:T(8,128)(2,1)S(1)}, u32[]{:S(2)}, u32[]{:S(2)}) %all-to-all-start) | async-done | bytes 917536 | tf_op jit(solution)/shard_map/all_to_all | solution.py:277
  57.3 9.0 %synth.1 = bf16[8,64,1616]{2,1,0:T(8,128)(2,1)} custom-call(s32[8]{0:T(128)S(1)} %dynamic_slice.6.lats, bf16[448,8,128]{2,1,0:T(8,128)(2,1)S(1)} %bitcast.5, bf16[8,256,1024]{2,1,0:T(8,128)(2,1)} %get-tuple-element.7.tables, f32[8,8,1024]{2,1,0:T(8,128)S(1)} %get-tuple-element.8.coarse), custom_call_target="tpu_custom_call" | custom-call | flops 1879048192 | bytes 18000000 | tf_op jit(solution)/shard_map/synth/pallas_call | solution.py:279
  (17 shorter events, 0.1 us)
Async XLA Ops:
  0.0 0.9 %copy-start = (bf16[7,401,32]{1,2,0:T(8,128)(2,1)S(1)}, bf16[7,401,32]{1,2,0:T(8,128)(2,1)}, u32[]{:S(2)}) copy-start(bf16[7,401,32]{1,2,0:T(8,128)(2,1)} %param.5) | copy-start | bytes 538948
  1.1 13.4 %collective-permute-start.3 = (bf16[32,2816]{1,0:T(8,128)(2,1)S(1)}, bf16[32,2816]{1,0:T(8,128)(2,1)S(1)}, u32[]{:S(2)}, u32[]{:S(2)}) collective-permute-start(bf16[32,2816]{1,0:T(8,128)(2,1)S(1)} %pack.1.x0), channel_id=1, source_target_pairs={{0,6},{1,7},{2,0},{3,1},{4,2},{5,3},{6,4},{7,5},{8,14},{9,15},{10,... | collective-permute-start | bytes 540680 | tf_op jit(solution)/shard_map/ppermute | solution.py:210
  8.0 11.8 %collective-permute-start.2 = (bf16[32,2816]{1,0:T(8,128)(2,1)S(1)}, bf16[32,2816]{1,0:T(8,128)(2,1)S(1)}, u32[]{:S(2)}, u32[]{:S(2)}) collective-permute-start(bf16[32,2816]{1,0:T(8,128)(2,1)S(1)} %pack.1.x0), channel_id=1, source_target_pairs={{0,2},{1,3},{2,4},{3,5},{4,6},{5,7},{6,0},{7,1},{8,10},{9,11},{10,... | collective-permute-start | bytes 540680 | tf_op jit(solution)/shard_map/ppermute | solution.py:210
  8.0 14.3 %collective-permute-start.1 = (bf16[32,2816]{1,0:T(8,128)(2,1)S(1)}, bf16[32,2816]{1,0:T(8,128)(2,1)S(1)}, u32[]{:S(2)}, u32[]{:S(2)}) collective-permute-start(bf16[32,2816]{1,0:T(8,128)(2,1)S(1)} %pack.1.x0), channel_id=1, source_target_pairs={{0,7},{1,0},{2,1},{3,2},{4,3},{5,4},{6,5},{7,6},{8,15},{9,8},{10,9... | collective-permute-start | bytes 540680 | tf_op jit(solution)/shard_map/ppermute | solution.py:210
  11.1 13.5 %collective-permute-start = (bf16[32,2816]{1,0:T(8,128)(2,1)S(1)}, bf16[32,2816]{1,0:T(8,128)(2,1)S(1)}, u32[]{:S(2)}, u32[]{:S(2)}) collective-permute-start(bf16[32,2816]{1,0:T(8,128)(2,1)S(1)} %pack.1.x0), channel_id=1, source_target_pairs={{0,1},{1,2},{2,3},{3,4},{4,5},{5,6},{6,7},{7,0},{8,9},{9,10},{10,1... | collective-permute-start | bytes 540680 | tf_op jit(solution)/shard_map/ppermute | solution.py:210
  14.4 10.1 %collective-permute-start.7 = (bf16[16,2816]{1,0:T(8,128)(2,1)S(1)}, bf16[16,2816]{1,0:T(8,128)(2,1)S(1)}, u32[]{:S(2)}, u32[]{:S(2)}) collective-permute-start(bf16[16,2816]{1,0:T(8,128)(2,1)S(1)} %slice.9), channel_id=1, source_target_pairs={{0,6},{1,7},{2,0},{3,1},{4,2},{5,3},{6,4},{7,5},{8,14},{9,15},{10,... | collective-permute-start | bytes 270344 | tf_op jit(solution)/shard_map/ppermute | solution.py:210
  19.7 6.8 %collective-permute-start.6 = (bf16[16,2816]{1,0:T(8,128)(2,1)S(1)}, bf16[16,2816]{1,0:T(8,128)(2,1)S(1)}, u32[]{:S(2)}, u32[]{:S(2)}) collective-permute-start(bf16[16,2816]{1,0:T(8,128)(2,1)S(1)} %slice.8), channel_id=1, source_target_pairs={{0,2},{1,3},{2,4},{3,5},{4,6},{5,7},{6,0},{7,1},{8,10},{9,11},{10,... | collective-permute-start | bytes 270344 | tf_op jit(solution)/shard_map/ppermute | solution.py:210
  19.8 6.7 %collective-permute-start.5 = (bf16[32,2816]{1,0:T(8,128)(2,1)S(1)}, bf16[32,2816]{1,0:T(8,128)(2,1)S(1)}, u32[]{:S(2)}, u32[]{:S(2)}) collective-permute-start(bf16[32,2816]{1,0:T(8,128)(2,1)S(1)} %collective-permute-done.3.m2), channel_id=1, source_target_pairs={{0,7},{1,0},{2,1},{3,2},{4,3},{5,4},{6,5},{7,6},{8,15},{9,8},{10,9... | collective-permute-start | bytes 540680 | tf_op jit(solution)/shard_map/ppermute | solution.py:210
  22.3 9.2 %collective-permute-start.4 = (bf16[32,2816]{1,0:T(8,128)(2,1)S(1)}, bf16[32,2816]{1,0:T(8,128)(2,1)S(1)}, u32[]{:S(2)}, u32[]{:S(2)}) collective-permute-start(bf16[32,2816]{1,0:T(8,128)(2,1)S(1)} %collective-permute-done.2.p2), channel_id=1, source_target_pairs={{0,1},{1,2},{2,3},{3,4},{4,5},{5,6},{6,7},{7,0},{8,9},{9,10},{10,1... | collective-permute-start | bytes 540680 | tf_op jit(solution)/shard_map/ppermute | solution.py:210
  22.3 1.1 %copy-start.1 = (bf16[7,401,128]{2,1,0:T(8,128)(2,1)S(1)}, bf16[7,401,128]{2,1,0:T(8,128)(2,1)}, u32[]{:S(2)}) copy-start(bf16[7,401,128]{2,1,0:T(8,128)(2,1)} %spec.1) | copy-start | bytes 2155780
  33.0 8.6 %copy-start.2 = (s32[224]{0:T(256)S(1)}, s32[224]{0:T(256)}, u32[]{:S(2)}) copy-start(s32[224]{0:T(256)} %param.6) | copy-start | bytes 2692
  33.0 8.9 %copy-start.3 = (s32[256]{0:T(256)S(1)}, s32[256]{0:T(256)}, u32[]{:S(2)}) copy-start(s32[256]{0:T(256)} %param.7) | copy-start | bytes 3076
  33.0 24.3 %all-to-all-start = ((bf16[32,14,8,128]{3,2,1,0:T(8,128)(2,1)}), bf16[32,14,8,128]{3,2,1,0:T(8,128)(2,1)S(1)}, u32[]{:S(2)}, u32[]{:S(2)}) async-start(bf16[32,14,8,128]{3,2,1,0:T(8,128)(2,1)} %legendre.1), calls=%async_computation | async-start | bytes 1835008 | tf_op jit(solution)/shard_map/all_to_all | solution.py:277

commit v4 on v3

--- a/solution.py
+++ b/solution.py
@@ -168,7 +168,6 @@
         return pltpu.make_async_copy(rows.at[q], out.at[q], sems.at[q])
 
     def one_row(q, lhs, other, turn, spare):
-        fetch(q).wait()
         a = lats[q]
         lon = 20 + 4 * jnp.minimum(a, NLAT - 1 - a)
         result = lax.dot_general(lhs[...], fine[q], nt, preferred_element_type=jnp.float32)
@@ -189,6 +188,8 @@
         copy(q).start()
 
     def two_rows(i, carry):
+        fetch(2 * i).wait()
+        fetch(2 * i + 1).wait()
         one_row(2 * i, lhs_a, lhs_b, turn_b, turn_a)
         one_row(2 * i + 1, lhs_b, lhs_a, turn_a, turn_b)
         return carry

time: 66.6 us -> 63.5 us (0.953)
  Pallas kernels: 16.8 us -> 13.8 us
    pallas_call x1, Pallas kernels: 9.02 us -> 5.94 us  [on_device(): pl.pallas_call(synth_kernel, out_shape=jax.ShapeDtypeStruct((ROWS, 64, WI...]
  transfers between devices with their start and end apart: 9 -> 9, of which waited for: 4 -> 4; matrix products, arithmetic and copies ran while one was open for 3% -> 3% of each run, Pallas kernels for 9% -> 10%
where the time goes in v4:
time: 63.5 us; the launch traced here: 63.2 us
  starting transfers between devices  26.5 us (42%)
  waiting for transfers between devices  19 us (30%)
  Pallas kernels  13.8 us (22%)
  local copies, waits for them, and re-layouts  3.17 us (5%)
  other arithmetic  0.7 us (1%)
    ppermute x8, starting transfers between devices, shift(): return lax.ppermute(v, 'lev', [(i, (i + d) % 8) for i in range(8)])  17.9 us
    all_to_all x1, waiting for transfers between devices, on_device(): lax.all_to_all(fourier, 'wav', split_axis=0, concat_axis=0, tiled=True)  10.3 us
    ppermute x8, waiting for transfers between devices, shift(): return lax.ppermute(v, 'lev', [(i, (i + d) % 8) for i in range(8)])  8.75 us
    all_to_all x1, starting transfers between devices, on_device(): lax.all_to_all(fourier, 'wav', split_axis=0, concat_axis=0, tiled=True)  8.61 us
    pallas_call x1, Pallas kernels, on_device(): pl.pallas_call(synth_kernel, out_shape=jax.ShapeDtypeStruct((ROWS, 64, WI...  5.94 us
    pallas_call x1, Pallas kernels, on_device(): pl.pallas_call(table_kernel, out_shape=(pltpu.HBM((ROWS, FINE, 2 * KP), b...  4.95 us
    unnamed x8, local copies, waits for them, and re-layouts  2.06 us
    pallas_call x1, Pallas kernels, on_device(): pl.pallas_call(legendre_kernel, out_shape=pltpu.VMEM((32, 2 * SLOTS, ROWS...  1.6 us
  transfers between devices with their start and end apart: 9, of which 4 were waited for; matrix products, arithmetic and copies ran while one was open for 3% of the time, Pallas kernels for 10%

profile of v4, /device:TPU:1, one launch (start us, length us, event | category | flops | bytes accessed | tf_op | source)
XLA Modules:
  0.0 63.2 jit_solution(10462457937396142947)
XLA Ops:
  0.0 0.9 %copy-done = bf16[7,401,32]{1,2,0:T(8,128)(2,1)S(1)} copy-done((bf16[7,401,32]{1,2,0:T(8,128)(2,1)S(1)}, bf16[7,401,32]{1,2,0:T(8,128)(2,1)}, u32[]{:S(2)}) %copy-start) | copy-done | bytes 179672
  0.9 0.1 pack.1.x0
  1.1 6.9 %collective-permute-start.3 = (bf16[32,2816]{1,0:T(8,128)(2,1)S(1)}, bf16[32,2816]{1,0:T(8,128)(2,1)S(1)}, u32[]{:S(2)}, u32[]{:S(2)}) collective-permute-start(bf16[32,2816]{1,0:T(8,128)(2,1)S(1)} %pack.1.x0), channel_id=1, source_target_pairs={{0,6},{1,7},{2,0},{3,1},{4,2},{5,3},{6,4},{7,5},{8,14},{9,15},{10,... | collective-permute-start | bytes 540680 | tf_op jit(solution)/shard_map/ppermute | solution.py:211
  8.0 0.0 collective-permute-start.2
  8.0 3.1 %collective-permute-start.1 = (bf16[32,2816]{1,0:T(8,128)(2,1)S(1)}, bf16[32,2816]{1,0:T(8,128)(2,1)S(1)}, u32[]{:S(2)}, u32[]{:S(2)}) collective-permute-start(bf16[32,2816]{1,0:T(8,128)(2,1)S(1)} %pack.1.x0), channel_id=1, source_target_pairs={{0,7},{1,0},{2,1},{3,2},{4,3},{5,4},{6,5},{7,6},{8,15},{9,8},{10,9... | collective-permute-start | bytes 540680 | tf_op jit(solution)/shard_map/ppermute | solution.py:211
  11.1 0.0 collective-permute-start
  11.1 0.8 %dynamic_slice.7.pairs = s32[7]{0:T(128)S(1)} dynamic-slice(s32[224]{0:T(256)} %param.6, s32[]{:T(128)S(6)} %select_n.21), dynamic_slice_sizes={7} | dynamic-slice | bytes 60 | tf_op jit(solution)/shard_map/dynamic_slice | solution.py:227
  11.8 0.7 %broadcast_subtract_fusion = s32[224]{0:T(256)S(1)} fusion(s32[224]{0:T(256)} %param.6), kind=kLoop, calls=%fused_computation.2 | loop fusion | flops 224 | bytes 1792 | tf_op jit(solution)/shard_map/sub | solution.py:229
  12.5 1.9 %collective-permute-done.3.m2 = bf16[32,2816]{1,0:T(8,128)(2,1)S(1)} collective-permute-done((bf16[32,2816]{1,0:T(8,128)(2,1)S(1)}, bf16[32,2816]{1,0:T(8,128)(2,1)S(1)}, u32[]{:S(2)}, u32[]{:S(2)}) %collective-permute-start.3) | collective-permute-done | bytes 180256 | tf_op jit(solution)/shard_map/ppermute | solution.py:211
  14.4 5.3 %collective-permute-start.7 = (bf16[16,2816]{1,0:T(8,128)(2,1)S(1)}, bf16[16,2816]{1,0:T(8,128)(2,1)S(1)}, u32[]{:S(2)}, u32[]{:S(2)}) collective-permute-start(bf16[16,2816]{1,0:T(8,128)(2,1)S(1)} %slice.9), channel_id=1, source_target_pairs={{0,6},{1,7},{2,0},{3,1},{4,2},{5,3},{6,4},{7,5},{8,14},{9,15},{10,... | collective-permute-start | bytes 270344 | tf_op jit(solution)/shard_map/ppermute | solution.py:211
  19.7 0.1 collective-permute-start.6
  19.8 2.4 %collective-permute-start.5 = (bf16[32,2816]{1,0:T(8,128)(2,1)S(1)}, bf16[32,2816]{1,0:T(8,128)(2,1)S(1)}, u32[]{:S(2)}, u32[]{:S(2)}) collective-permute-start(bf16[32,2816]{1,0:T(8,128)(2,1)S(1)} %collective-permute-done.3.m2), channel_id=1, source_target_pairs={{0,7},{1,0},{2,1},{3,2},{4,3},{5,4},{6,5},{7,6},{8,15},{9,8},{10,9... | collective-permute-start | bytes 540680 | tf_op jit(solution)/shard_map/ppermute | solution.py:211
  22.3 1.1 %copy-done.1 = bf16[7,401,128]{2,1,0:T(8,128)(2,1)S(1)} copy-done((bf16[7,401,128]{2,1,0:T(8,128)(2,1)S(1)}, bf16[7,401,128]{2,1,0:T(8,128)(2,1)}, u32[]{:S(2)}) %copy-start.1) | copy-done | bytes 718616
  23.4 1.2 %mask.1.rhs = bf16[7,512,256]{2,1,0:T(8,128)(2,1)S(1)} custom-call(s32[7]{0:T(128)S(1)} %dynamic_slice.7.pairs, bf16[7,401,128]{2,1,0:T(8,128)(2,1)S(1)} %copy-done.1), custom_call_target="tpu_custom_call" | custom-call | flops 2000000000 | bytes 2500000 | tf_op jit(solution)/shard_map/mask/pallas_call | solution.py:249
  24.6 2.0 %collective-permute-done.6.p4 = bf16[16,2816]{1,0:T(8,128)(2,1)S(1)} collective-permute-done((bf16[16,2816]{1,0:T(8,128)(2,1)S(1)}, bf16[16,2816]{1,0:T(8,128)(2,1)S(1)}, u32[]{:S(2)}, u32[]{:S(2)}) %collective-permute-start.6) | collective-permute-done | bytes 90144 | tf_op jit(solution)/shard_map/ppermute | solution.py:211
  26.5 4.9 %collective-permute-done.4.p3 = bf16[32,2816]{1,0:T(8,128)(2,1)S(1)} collective-permute-done((bf16[32,2816]{1,0:T(8,128)(2,1)S(1)}, bf16[32,2816]{1,0:T(8,128)(2,1)S(1)}, u32[]{:S(2)}, u32[]{:S(2)}) %collective-permute-start.4) | collective-permute-done | bytes 180256 | tf_op jit(solution)/shard_map/ppermute | solution.py:211
  31.4 1.6 %legendre.1 = bf16[32,14,8,128]{3,2,1,0:T(8,128)(2,1)} custom-call(s32[1]{0:T(128)} %bitcast.place, bf16[7,512,256]{2,1,0:T(8,128)(2,1)S(1)} %mask.1.rhs, bf16[32,2816]{1,0:T(8,128)(2,1)S(1)} %pack.1.x0, bf16[32,2816]{1,0:T(8,128)(2,1)S(1)} %collective-permute-done.p1, bf16[32,2816]{1,0:T(8,128)(2,1)S(1)} %collective-permute-done.1.m1, ...), custom_call_target="tpu_custom_call" | custom-call | flops 469762048 | bytes 4000000 | tf_op jit(solution)/shard_map/legendre/pallas_call | solution.py:269
  33.0 8.6 %all-to-all-start = ((bf16[32,14,8,128]{3,2,1,0:T(8,128)(2,1)}), bf16[32,14,8,128]{3,2,1,0:T(8,128)(2,1)S(1)}, u32[]{:S(2)}, u32[]{:S(2)}) async-start(bf16[32,14,8,128]{3,2,1,0:T(8,128)(2,1)} %legendre.1), calls=%async_computation | async-start | bytes 1835008 | tf_op jit(solution)/shard_map/all_to_all | solution.py:278
  41.7 0.1 copy.5
  41.8 0.1 select_n.23
  42.0 0.1 dynamic_slice.6.lats
  42.1 4.9 %tables.1 = (bf16[8,256,1024]{2,1,0:T(8,128)(2,1)}, f32[8,8,1024]{2,1,0:T(8,128)S(1)}) custom-call(s32[8]{0:T(128)S(1)} %dynamic_slice.6.lats, f32[1,512]{1,0:T(1,128)S(1)} %pad_convert_fusion.waves), custom_call_target="tpu_custom_call" | custom-call | flops 4000000000 | bytes 4500000 | tf_op jit(solution)/shard_map/tables/pallas_call | solution.py:259
  47.0 10.3 %all-to-all-done = bf16[32,14,8,128]{3,2,1,0:T(8,128)(2,1)S(1)} async-done(((bf16[32,14,8,128]{3,2,1,0:T(8,128)(2,1)}), bf16[32,14,8,128]{3,2,1,0:T(8,128)(2,1)S(1)}, u32[]{:S(2)}, u32[]{:S(2)}) %all-to-all-start) | async-done | bytes 917536 | tf_op jit(solution)/shard_map/all_to_all | solution.py:278
  57.3 5.9 %synth.1 = bf16[8,64,1616]{2,1,0:T(8,128)(2,1)} custom-call(s32[8]{0:T(128)S(1)} %dynamic_slice.6.lats, bf16[448,8,128]{2,1,0:T(8,128)(2,1)S(1)} %bitcast.5, bf16[8,256,1024]{2,1,0:T(8,128)(2,1)} %get-tuple-element.7.tables, f32[8,8,1024]{2,1,0:T(8,128)S(1)} %get-tuple-element.8.coarse), custom_call_target="tpu_custom_call" | custom-call | flops 1879048192 | bytes 18000000 | tf_op jit(solution)/shard_map/synth/pallas_call | solution.py:280
  (17 shorter events, 0.1 us)
Async XLA Ops:
  0.0 0.9 %copy-start = (bf16[7,401,32]{1,2,0:T(8,128)(2,1)S(1)}, bf16[7,401,32]{1,2,0:T(8,128)(2,1)}, u32[]{:S(2)}) copy-start(bf16[7,401,32]{1,2,0:T(8,128)(2,1)} %param.5) | copy-start | bytes 538948
  1.1 13.4 %collective-permute-start.3 = (bf16[32,2816]{1,0:T(8,128)(2,1)S(1)}, bf16[32,2816]{1,0:T(8,128)(2,1)S(1)}, u32[]{:S(2)}, u32[]{:S(2)}) collective-permute-start(bf16[32,2816]{1,0:T(8,128)(2,1)S(1)} %pack.1.x0), channel_id=1, source_target_pairs={{0,6},{1,7},{2,0},{3,1},{4,2},{5,3},{6,4},{7,5},{8,14},{9,15},{10,... | collective-permute-start | bytes 540680 | tf_op jit(solution)/shard_map/ppermute | solution.py:211
  8.0 11.8 %collective-permute-start.2 = (bf16[32,2816]{1,0:T(8,128)(2,1)S(1)}, bf16[32,2816]{1,0:T(8,128)(2,1)S(1)}, u32[]{:S(2)}, u32[]{:S(2)}) collective-permute-start(bf16[32,2816]{1,0:T(8,128)(2,1)S(1)} %pack.1.x0), channel_id=1, source_target_pairs={{0,2},{1,3},{2,4},{3,5},{4,6},{5,7},{6,0},{7,1},{8,10},{9,11},{10,... | collective-permute-start | bytes 540680 | tf_op jit(solution)/shard_map/ppermute | solution.py:211
  8.0 14.3 %collective-permute-start.1 = (bf16[32,2816]{1,0:T(8,128)(2,1)S(1)}, bf16[32,2816]{1,0:T(8,128)(2,1)S(1)}, u32[]{:S(2)}, u32[]{:S(2)}) collective-permute-start(bf16[32,2816]{1,0:T(8,128)(2,1)S(1)} %pack.1.x0), channel_id=1, source_target_pairs={{0,7},{1,0},{2,1},{3,2},{4,3},{5,4},{6,5},{7,6},{8,15},{9,8},{10,9... | collective-permute-start | bytes 540680 | tf_op jit(solution)/shard_map/ppermute | solution.py:211
  11.1 13.5 %collective-permute-start = (bf16[32,2816]{1,0:T(8,128)(2,1)S(1)}, bf16[32,2816]{1,0:T(8,128)(2,1)S(1)}, u32[]{:S(2)}, u32[]{:S(2)}) collective-permute-start(bf16[32,2816]{1,0:T(8,128)(2,1)S(1)} %pack.1.x0), channel_id=1, source_target_pairs={{0,1},{1,2},{2,3},{3,4},{4,5},{5,6},{6,7},{7,0},{8,9},{9,10},{10,1... | collective-permute-start | bytes 540680 | tf_op jit(solution)/shard_map/ppermute | solution.py:211
  14.4 10.1 %collective-permute-start.7 = (bf16[16,2816]{1,0:T(8,128)(2,1)S(1)}, bf16[16,2816]{1,0:T(8,128)(2,1)S(1)}, u32[]{:S(2)}, u32[]{:S(2)}) collective-permute-start(bf16[16,2816]{1,0:T(8,128)(2,1)S(1)} %slice.9), channel_id=1, source_target_pairs={{0,6},{1,7},{2,0},{3,1},{4,2},{5,3},{6,4},{7,5},{8,14},{9,15},{10,... | collective-permute-start | bytes 270344 | tf_op jit(solution)/shard_map/ppermute | solution.py:211
  19.7 6.8 %collective-permute-start.6 = (bf16[16,2816]{1,0:T(8,128)(2,1)S(1)}, bf16[16,2816]{1,0:T(8,128)(2,1)S(1)}, u32[]{:S(2)}, u32[]{:S(2)}) collective-permute-start(bf16[16,2816]{1,0:T(8,128)(2,1)S(1)} %slice.8), channel_id=1, source_target_pairs={{0,2},{1,3},{2,4},{3,5},{4,6},{5,7},{6,0},{7,1},{8,10},{9,11},{10,... | collective-permute-start | bytes 270344 | tf_op jit(solution)/shard_map/ppermute | solution.py:211
  19.8 6.7 %collective-permute-start.5 = (bf16[32,2816]{1,0:T(8,128)(2,1)S(1)}, bf16[32,2816]{1,0:T(8,128)(2,1)S(1)}, u32[]{:S(2)}, u32[]{:S(2)}) collective-permute-start(bf16[32,2816]{1,0:T(8,128)(2,1)S(1)} %collective-permute-done.3.m2), channel_id=1, source_target_pairs={{0,7},{1,0},{2,1},{3,2},{4,3},{5,4},{6,5},{7,6},{8,15},{9,8},{10,9... | collective-permute-start | bytes 540680 | tf_op jit(solution)/shard_map/ppermute | solution.py:211
  22.3 9.2 %collective-permute-start.4 = (bf16[32,2816]{1,0:T(8,128)(2,1)S(1)}, bf16[32,2816]{1,0:T(8,128)(2,1)S(1)}, u32[]{:S(2)}, u32[]{:S(2)}) collective-permute-start(bf16[32,2816]{1,0:T(8,128)(2,1)S(1)} %collective-permute-done.2.p2), channel_id=1, source_target_pairs={{0,1},{1,2},{2,3},{3,4},{4,5},{5,6},{6,7},{7,0},{8,9},{9,10},{10,1... | collective-permute-start | bytes 540680 | tf_op jit(solution)/shard_map/ppermute | solution.py:211
  22.3 1.1 %copy-start.1 = (bf16[7,401,128]{2,1,0:T(8,128)(2,1)S(1)}, bf16[7,401,128]{2,1,0:T(8,128)(2,1)}, u32[]{:S(2)}) copy-start(bf16[7,401,128]{2,1,0:T(8,128)(2,1)} %spec.1) | copy-start | bytes 2155780
  33.0 8.6 %copy-start.2 = (s32[224]{0:T(256)S(1)}, s32[224]{0:T(256)}, u32[]{:S(2)}) copy-start(s32[224]{0:T(256)} %param.6) | copy-start | bytes 2692
  33.0 8.9 %copy-start.3 = (s32[256]{0:T(256)S(1)}, s32[256]{0:T(256)}, u32[]{:S(2)}) copy-start(s32[256]{0:T(256)} %param.7) | copy-start | bytes 3076
  33.0 24.3 %all-to-all-start = ((bf16[32,14,8,128]{3,2,1,0:T(8,128)(2,1)}), bf16[32,14,8,128]{3,2,1,0:T(8,128)(2,1)S(1)}, u32[]{:S(2)}, u32[]{:S(2)}) async-start(bf16[32,14,8,128]{3,2,1,0:T(8,128)(2,1)} %legendre.1), calls=%async_computation | async-start | bytes 1835008 | tf_op jit(solution)/shard_map/all_to_all | solution.py:278

commit v5 on v3

--- a/solution.py
+++ b/solution.py
@@ -51,12 +51,12 @@
     out[:, SLOTS * MAIN : PACKED] = total.astype(jnp.bfloat16)
 
 
-def mask_kernel(pairs, spec, out, scr):
+def mask_kernel(device, wave_pair, spec, out, scr):
     t_main = lax.broadcasted_iota(jnp.int32, (MAIN, 128), 0)
     t_rest = lax.broadcasted_iota(jnp.int32, (128, 128), 0) + MAIN
     for s in range(SLOTS):
-        border = WAVES - pairs[s]
-        border = jnp.where(pairs[s] >= 0, border, FOLD)
+        pair = wave_pair[device[0] * SLOTS + s]
+        border = jnp.where(pair >= 0, WAVES - pair, FOLD)
         main = spec[s, 0:MAIN, :].astype(jnp.float32)
         low = jnp.where(t_main < border, main, 0.0)
         out[s, 0:MAIN, 0:128] = low.astype(jnp.bfloat16)
@@ -69,7 +69,7 @@
         out[s, MAIN:KP, 128:256] = (rest - low).astype(jnp.bfloat16)
 
 
-def legendre_kernel(place, rhs, x0, p1, m1, p2, m2, p3, m3, p4, m4, out):
+def legendre_kernel(place, _tables, rhs, x0, p1, m1, p2, m2, p3, m3, p4, m4, out):
     z = place[0]
     for s in range(SLOTS):
         def lhs(ref):
@@ -84,11 +84,19 @@
                 out[pl.ds(4 * block, 4), 2 * s + h] = part.reshape(4, ROWS, 128).astype(jnp.bfloat16)
 
 
-def table_kernel(lats, waves, fine, coarse):
-    m = waves[...]
+def table_kernel(device, lat_slot, pairs, fine_out, coarse_out, scr, fine, coarse, sems):
+    def copies(q):
+        return (pltpu.make_async_copy(fine.at[q], fine_out.at[q], sems.at[0, q]),
+                pltpu.make_async_copy(coarse.at[q], coarse_out.at[q], sems.at[1, q]))
+
+    scr[...] = jnp.full((1, KP), -1, jnp.int32)
+    scr[:, 0:KEEP] = pairs[...]
+    pair = scr[...]
+    half = lax.broadcasted_iota(jnp.int32, (1, KP), 1) % 2
+    m = jnp.where(pair < 0, -1, jnp.where(half == 0, pair, WAVES - 1 - pair)).astype(jnp.float32)
 
     def one_row(q, carry):
-        a = lats[q]
+        a = lat_slot[device[0] * ROWS + q]
         lon = 20 + 4 * jnp.minimum(a, NLAT - 1 - a)
         highest = jnp.minimum(WAVES - 1, (lon - 1) // 2).astype(jnp.float32)
         n = jnp.full((1, KP), lon, jnp.int32).astype(jnp.float32)
@@ -114,18 +122,17 @@
         cos_c, sin_c = cos_sin(step.astype(jnp.float32) * m, n, inv)
         coarse[q, :, 0:KP] = cos_c
         coarse[q, :, KP : 2 * KP] = sin_c
+        for copy in copies(q):
+            copy.start()
         return carry
 
     lax.fori_loop(0, ROWS, one_row, 0)
-
-
-def synth_kernel(lats, recv, tables, coarse, out, scr, turn_a, turn_b, lhs_a, lhs_b, rows,
-                 fine, sems, in_sems):
-    def fetch(q):
-        return pltpu.make_async_copy(tables.at[q], fine.at[q], in_sems.at[q])
-
     for q in range(ROWS):
-        fetch(q).start()
+        for copy in copies(q):
+            copy.wait()
+
+
+def synth_kernel(device, lat_slot, recv, fine, coarse, out, scr, turn_a, turn_b, lhs_a, lhs_b, rows, sems):
     for i in range(7):
         scr[512 * i : 512 * (i + 1), :] = (
             recv[64 * i : 64 * (i + 1)].astype(jnp.float32).reshape(512, 128))
@@ -168,8 +175,7 @@
         return pltpu.make_async_copy(rows.at[q], out.at[q], sems.at[q])
 
     def one_row(q, lhs, other, turn, spare):
-        fetch(q).wait()
-        a = lats[q]
+        a = lat_slot[device[0] * ROWS + q]
         lon = 20 + 4 * jnp.minimum(a, NLAT - 1 - a)
         result = lax.dot_general(lhs[...], fine[q], nt, preferred_element_type=jnp.float32)
         rotate(jnp.minimum(q + 1, ROWS - 1), turn, other)
@@ -205,6 +211,20 @@
     return pl.CostEstimate(flops=flops, transcendentals=0, bytes_accessed=moved)
 
 
+def half_of(x, first):
+    def kernel(ref, out):
+        out[...] = ref[first : first + QBLK // 2, :]
+
+    return pl.pallas_call(
+        kernel,
+        out_shape=pltpu.VMEM((QBLK // 2, PACKED), jnp.bfloat16),
+        in_specs=[pl.BlockSpec(memory_space=pltpu.VMEM)],
+        out_specs=pl.BlockSpec(memory_space=pltpu.VMEM),
+        compiler_params=pltpu.CompilerParams(vmem_limit_bytes=2**21),
+        name="half",
+    )(pltpu.with_memory_space_constraint(x, pltpu.VMEM))
+
+
 def gather_pieces(x):
     def shift(v, d):
         return lax.ppermute(v, "lev", [(i, (i + d) % 8) for i in range(8)])
@@ -212,8 +232,7 @@
     p1, m1 = shift(x, 1), shift(x, -1)
     p2, m2 = shift(x, 2), shift(x, -2)
     p3, m3 = shift(p2, 1), shift(m2, -1)
-    half = QBLK // 2
-    p4, m4 = shift(p2[:half], 2), shift(m2[half:], -2)
+    p4, m4 = shift(half_of(p2, 0), 2), shift(half_of(m2, QBLK // 2), -2)
     return x, p1, m1, p2, m2, p3, m3, p4, m4
 
 
@@ -221,13 +240,11 @@
     bf16, f32 = jnp.bfloat16, jnp.float32
     smem = pl.BlockSpec(memory_space=pltpu.SMEM)
     vmem = pl.BlockSpec(memory_space=pltpu.VMEM)
+    hbm = pl.BlockSpec(memory_space=pltpu.HBM)
     z = lax.axis_index("lev").astype(jnp.int32)
     w = lax.axis_index("wav").astype(jnp.int32)
-    own_pairs = lax.dynamic_slice_in_dim(wave_pair, w * SLOTS, SLOTS)
-    own_lats = lax.dynamic_slice_in_dim(lat_slot, w * ROWS, ROWS)
-    waves = jnp.stack([wave_pair, WAVES - 1 - wave_pair], axis=1)
-    waves = jnp.where(wave_pair[:, None] >= 0, waves, -1).reshape(1, KEEP)
-    waves = jnp.pad(waves, ((0, 0), (0, KP - KEEP)), constant_values=-1).astype(f32)
+    device = w.reshape(1)
+    pairs = jnp.broadcast_to(wave_pair[:, None], (KEEP // 2, 2)).reshape(1, KEEP)
 
     def here(v):
         return pltpu.with_memory_space_constraint(v, pltpu.VMEM)
@@ -248,38 +265,42 @@
     rhs = pl.pallas_call(
         mask_kernel,
         out_shape=pltpu.VMEM((SLOTS, KP, 256), bf16),
-        in_specs=[smem, vmem], out_specs=vmem,
+        in_specs=[smem, smem, vmem], out_specs=vmem,
         scratch_shapes=[pltpu.VMEM((128, 128), f32)],
         cost_estimate=cost(2_000_000_000, 2_500_000),
         compiler_params=params(6),
         name="mask",
-    )(own_pairs, spectral)
+    )(device, wave_pair, spectral)
 
     fine, coarse = pl.pallas_call(
         table_kernel,
         out_shape=(pltpu.HBM((ROWS, FINE, 2 * KP), bf16),
-                   pltpu.VMEM((ROWS, 8, 2 * KP), f32)),
-        in_specs=[smem, vmem], out_specs=(vmem, vmem),
+                   pltpu.HBM((ROWS, 8, 2 * KP), f32)),
+        in_specs=[smem, smem, vmem], out_specs=(hbm, hbm),
+        scratch_shapes=[pltpu.VMEM((1, KP), jnp.int32),
+                        pltpu.VMEM((ROWS, FINE, 2 * KP), bf16),
+                        pltpu.VMEM((ROWS, 8, 2 * KP), f32),
+                        pltpu.SemaphoreType.DMA((2, ROWS))],
         cost_estimate=cost(4_000_000_000, 4_500_000),
         compiler_params=params(8),
         name="tables",
-    )(own_lats, waves)
+    )(device, lat_slot, pairs)
 
     fourier = pl.pallas_call(
         legendre_kernel,
         out_shape=pltpu.VMEM((32, 2 * SLOTS, ROWS, 128), bf16),
-        in_specs=[smem] + [vmem] * 10, out_specs=vmem,
+        in_specs=[smem, hbm] + [vmem] * 10, out_specs=vmem,
         cost_estimate=cost(2 * 256 * 512 * 256 * SLOTS, 4_000_000),
         compiler_params=params(12),
         name="legendre",
-    )(z.reshape(1), here(rhs), *[here(p) for p in pieces])
+    )(z.reshape(1), pltpu.with_memory_space_constraint(coarse, pltpu.HBM), here(rhs), *[here(p) for p in pieces])
 
     received = lax.all_to_all(fourier, "wav", split_axis=0, concat_axis=0, tiled=True)
 
     return pl.pallas_call(
         synth_kernel,
         out_shape=jax.ShapeDtypeStruct((ROWS, 64, WIDTH), bf16),
-        in_specs=[smem, vmem, pl.BlockSpec(memory_space=pltpu.HBM), vmem],
+        in_specs=[smem, smem, vmem, vmem, vmem],
         out_specs=pl.BlockSpec(memory_space=pltpu.HBM),
         scratch_shapes=[pltpu.VMEM((KP * ROWS, 128), f32),
                         pltpu.VMEM((128, KP), f32),
@@ -287,14 +308,12 @@
                         pltpu.VMEM((64 * COARSE, 2 * KP), bf16),
                         pltpu.VMEM((64 * COARSE, 2 * KP), bf16),
                         pltpu.VMEM((ROWS, 64, WIDTH), bf16),
-                        pltpu.VMEM((ROWS, FINE, 2 * KP), bf16),
-                        pltpu.SemaphoreType.DMA((ROWS,)),
                         pltpu.SemaphoreType.DMA((ROWS,))],
         cost_estimate=cost(2 * 448 * 1024 * 256 * ROWS, 18_000_000),
         compiler_params=params(16),
         name="synth",
-    )(own_lats, here(received.reshape(KEEP, ROWS, 128)),
-      pltpu.with_memory_space_constraint(fine, pltpu.HBM), here(coarse))
+    )(device, lat_slot, here(received.reshape(KEEP, ROWS, 128)),
+      here(fine), here(coarse))
 
 
 def solution(mesh):

time: 66.6 us -> 61.9 us (0.929)
  blocking collectives: 0 us -> 24.4 us
  waiting for transfers between devices: 19 us -> 7.05 us
  starting transfers between devices: 26.5 us -> 16.4 us
  Pallas kernels: 16.8 us -> 11.2 us
  other arithmetic: 0.7 us -> 0 us
    all_to_all x0 -> x1, blocking collectives: none -> 24.4 us  [on_device(): lax.all_to_all(fourier, 'wav', split_axis=0, concat_axis=0, tiled=True)]
    all_to_all x1 -> x0, waiting for transfers between devices: 10.3 us -> none  [on_device(): lax.all_to_all(fourier, 'wav', split_axis=0, concat_axis=0, tiled=True)]
    all_to_all x1 -> x0, starting transfers between devices: 8.61 us -> none  [on_device(): lax.all_to_all(fourier, 'wav', split_axis=0, concat_axis=0, tiled=True)]
    pallas_call x1, Pallas kernels: 9.02 us -> 5.28 us  [on_device(): pl.pallas_call(synth_kernel, out_shape=jax.ShapeDtypeStruct((ROWS, 64, WI...]
    ppermute x8, waiting for transfers between devices: 8.75 us -> 7.05 us  [shift(): return lax.ppermute(v, 'lev', [(i, (i + d) % 8) for i in range(8)])]
    ppermute x8, starting transfers between devices: 17.9 us -> 16.4 us  [shift(): return lax.ppermute(v, 'lev', [(i, (i + d) % 8) for i in range(8)])]
    pallas_call x1, Pallas kernels: 4.95 us -> 3.99 us  [on_device(): pl.pallas_call(table_kernel, out_shape=(pltpu.HBM((ROWS, FINE, 2 * KP), b...]
    pallas_call x1, Pallas kernels: 1.6 us -> 0.67 us  [on_device(): pl.pallas_call(legendre_kernel, out_shape=pltpu.VMEM((32, 2 * SLOTS, ROWS...]
  transfers between devices with their start and end apart: 9 -> 8, of which waited for: 4 -> 3; matrix products, arithmetic and copies ran while one was open for 3% -> 1% of each run, Pallas kernels for 9% -> 8%
where the time goes in v5:
time: 61.9 us; the launch traced here: 61.8 us
  blocking collectives  24.4 us (39%)
  starting transfers between devices  16.4 us (26%)
  Pallas kernels  11.2 us (18%)
  waiting for transfers between devices  7.05 us (11%)
  local copies, waits for them, and re-layouts  2.54 us (4%)
    all_to_all x1, blocking collectives, on_device(): lax.all_to_all(fourier, 'wav', split_axis=0, concat_axis=0, tiled=True)  24.4 us
    ppermute x8, starting transfers between devices, shift(): return lax.ppermute(v, 'lev', [(i, (i + d) % 8) for i in range(8)])  16.4 us
    ppermute x8, waiting for transfers between devices, shift(): return lax.ppermute(v, 'lev', [(i, (i + d) % 8) for i in range(8)])  7.05 us
    pallas_call x1, Pallas kernels, on_device(): pl.pallas_call(synth_kernel, out_shape=jax.ShapeDtypeStruct((ROWS, 64, WI...  5.28 us
    pallas_call x1, Pallas kernels, on_device(): pl.pallas_call(table_kernel, out_shape=(pltpu.HBM((ROWS, FINE, 2 * KP), b...  3.99 us
    unnamed x14, local copies, waits for them, and re-layouts  1.64 us
  transfers between devices with their start and end apart: 8, of which 3 were waited for; matrix products, arithmetic and copies ran while one was open for 1% of the time, Pallas kernels for 8%

profile of v5, /device:TPU:1, one launch (start us, length us, event | category | flops | bytes accessed | tf_op | source)
XLA Modules:
  0.0 61.8 jit_solution(1832248321552034890)
XLA Ops:
  0.0 0.9 %copy-done.2 = bf16[7,401,32]{1,2,0:T(8,128)(2,1)S(1)} copy-done((bf16[7,401,32]{1,2,0:T(8,128)(2,1)S(1)}, bf16[7,401,32]{1,2,0:T(8,128)(2,1)}, u32[]{:S(2)}) %copy-start.2) | copy-done | bytes 179672
  0.9 0.1 pack.1.x0
  1.1 6.9 %collective-permute-start.3 = (bf16[32,2816]{1,0:T(8,128)(2,1)S(1)}, bf16[32,2816]{1,0:T(8,128)(2,1)S(1)}, u32[]{:S(2)}, u32[]{:S(2)}) collective-permute-start(bf16[32,2816]{1,0:T(8,128)(2,1)S(1)} %pack.1.x0), channel_id=1, source_target_pairs={{0,6},{1,7},{2,0},{3,1},{4,2},{5,3},{6,4},{7,5},{8,14},{9,15},{10,... | collective-permute-start | bytes 540680 | tf_op jit(solution)/shard_map/ppermute | solution.py:230
  8.0 0.0 collective-permute-start.2
  8.0 3.1 %collective-permute-start.1 = (bf16[32,2816]{1,0:T(8,128)(2,1)S(1)}, bf16[32,2816]{1,0:T(8,128)(2,1)S(1)}, u32[]{:S(2)}, u32[]{:S(2)}) collective-permute-start(bf16[32,2816]{1,0:T(8,128)(2,1)S(1)} %pack.1.x0), channel_id=1, source_target_pairs={{0,7},{1,0},{2,1},{3,2},{4,3},{5,4},{6,5},{7,6},{8,15},{9,8},{10,9... | collective-permute-start | bytes 540680 | tf_op jit(solution)/shard_map/ppermute | solution.py:230
  11.1 0.0 collective-permute-start
  11.1 0.8 %broadcast_in_dim.2 = s32[224,2]{1,0:T(8,128)S(1)} broadcast(s32[224]{0:T(256)} %wave_pair.1), dimensions={0} | broadcast | bytes 2688 | tf_op jit(solution)/shard_map/broadcast_in_dim | solution.py:247
  11.9 0.1 reshape.15.pairs
  12.0 0.0 copy-start.4
  12.0 0.7 %copy-done.4 = s32[256]{0:T(256)S(1)} copy-done((s32[256]{0:T(256)S(1)}, s32[256]{0:T(256)}, u32[]{:S(2)}) %copy-start.4) | copy-done | bytes 1048
  12.7 4.0 %tables.1 = (bf16[8,256,1024]{2,1,0:T(8,128)(2,1)}, f32[8,8,1024]{2,1,0:T(8,128)}) custom-call(s32[1]{0:T(128)} %bitcast.device, s32[256]{0:T(256)S(1)} %copy-done.4, s32[1,448]{1,0:T(1,128)S(1)} %reshape.15.pairs), custom_call_target="tpu_custom_call" | custom-call | flops 4000000000 | bytes 4500000 | tf_op jit(solution)/shard_map/tables/pallas_call | solution.py:275
  16.7 0.0 collective-permute-done.3.ref.m2
  16.7 3.0 %collective-permute-start.7 = (bf16[16,2816]{1,0:T(8,128)(2,1)S(1)}, bf16[16,2816]{1,0:T(8,128)(2,1)S(1)}, u32[]{:S(2)}, u32[]{:S(2)}) collective-permute-start(bf16[16,2816]{1,0:T(8,128)(2,1)S(1)} %half.3), channel_id=1, source_target_pairs={{0,6},{1,7},{2,0},{3,1},{4,2},{5,3},{6,4},{7,5},{8,14},{9,15},{10,... | collective-permute-start | bytes 270344 | tf_op jit(solution)/shard_map/ppermute | solution.py:230
  19.7 0.1 collective-permute-start.6
  19.8 3.3 %collective-permute-start.5 = (bf16[32,2816]{1,0:T(8,128)(2,1)S(1)}, bf16[32,2816]{1,0:T(8,128)(2,1)S(1)}, u32[]{:S(2)}, u32[]{:S(2)}) collective-permute-start(bf16[32,2816]{1,0:T(8,128)(2,1)S(1)} %collective-permute-done.3.ref.m2), channel_id=1, source_target_pairs={{0,7},{1,0},{2,1},{3,2},{4,3},{5,4},{6,5},{7,6},{8,15},{9,8},{10,9... | collective-permute-start | bytes 540680 | tf_op jit(solution)/shard_map/ppermute | solution.py:230
  23.2 1.2 %mask.1.rhs = bf16[7,512,256]{2,1,0:T(8,128)(2,1)S(1)} custom-call(s32[1]{0:T(128)} %bitcast.device, s32[224]{0:T(256)S(1)} %copy-done.3, bf16[7,401,128]{2,1,0:T(8,128)(2,1)S(1)} %copy-done.6), custom_call_target="tpu_custom_call" | custom-call | flops 2000000000 | bytes 2500000 | tf_op jit(solution)/shard_map/mask/pallas_call | solution.py:265
  24.4 2.2 %collective-permute-done.6.p4 = bf16[16,2816]{1,0:T(8,128)(2,1)S(1)} collective-permute-done((bf16[16,2816]{1,0:T(8,128)(2,1)S(1)}, bf16[16,2816]{1,0:T(8,128)(2,1)S(1)}, u32[]{:S(2)}, u32[]{:S(2)}) %collective-permute-start.6) | collective-permute-done | bytes 90144 | tf_op jit(solution)/shard_map/ppermute | solution.py:230
  26.6 0.7 %collective-permute-done.5.m3 = bf16[32,2816]{1,0:T(8,128)(2,1)S(1)} collective-permute-done((bf16[32,2816]{1,0:T(8,128)(2,1)S(1)}, bf16[32,2816]{1,0:T(8,128)(2,1)S(1)}, u32[]{:S(2)}, u32[]{:S(2)}) %collective-permute-start.5) | collective-permute-done | bytes 180256 | tf_op jit(solution)/shard_map/ppermute | solution.py:230
  27.3 4.1 %collective-permute-done.4.p3 = bf16[32,2816]{1,0:T(8,128)(2,1)S(1)} collective-permute-done((bf16[32,2816]{1,0:T(8,128)(2,1)S(1)}, bf16[32,2816]{1,0:T(8,128)(2,1)S(1)}, u32[]{:S(2)}, u32[]{:S(2)}) %collective-permute-start.4) | collective-permute-done | bytes 180256 | tf_op jit(solution)/shard_map/ppermute | solution.py:230
  31.4 0.7 %legendre.1 = bf16[32,14,8,128]{3,2,1,0:T(8,128)(2,1)S(1)} custom-call(s32[1]{0:T(128)} %bitcast.1.place, f32[8,8,1024]{2,1,0:T(8,128)} %get-tuple-element.7._tables.coarse, bf16[7,512,256]{2,1,0:T(8,128)(2,1)S(1)} %mask.1.rhs, bf16[32,2816]{1,0:T(8,128)(2,1)S(1)} %pack.1.x0, bf16[32,2816]{1,0:T(8,128)(2,1)S(1)} %collective-permute-done.p1, ...), custom_call_target="tpu_custom_call" | custom-call | flops 469762048 | bytes 4000000 | tf_op jit(solution)/shard_map/legendre/pallas_call | solution.py:289
  32.1 0.0 copy-start.1
  32.1 0.0 copy-start.5
  32.1 24.4 %all_to_all.5 = bf16[32,14,8,128]{3,2,1,0:T(8,128)(2,1)S(1)} all-to-all(bf16[32,14,8,128]{3,2,1,0:T(8,128)(2,1)S(1)} %legendre.1), channel_id=1, replica_groups=mesh['wav'=32,'lev'=8] {'wav'}, dimensions={0} | all-to-all | bytes 1835008 | tf_op jit(solution)/shard_map/all_to_all | solution.py:298
  56.5 5.3 %synth.1 = bf16[8,64,1616]{2,1,0:T(8,128)(2,1)} custom-call(s32[1]{0:T(128)} %bitcast.device, s32[256]{0:T(256)S(1)} %copy-done.5, bf16[448,8,128]{2,1,0:T(8,128)(2,1)S(1)} %bitcast.4, bf16[8,256,1024]{2,1,0:T(8,128)(2,1)S(1)} %copy-done, f32[8,8,1024]{2,1,0:T(8,128)S(1)} %copy-done.1), custom_call_target="tpu_custom_call" | custom-call | flops 1879048192 | bytes 18000000 | tf_op jit(solution)/shard_map/synth/pallas_call | solution.py:300
  (16 shorter events, 0.0 us)
Async XLA Ops:
  0.0 0.9 %copy-start.2 = (bf16[7,401,32]{1,2,0:T(8,128)(2,1)S(1)}, bf16[7,401,32]{1,2,0:T(8,128)(2,1)}, u32[]{:S(2)}) copy-start(bf16[7,401,32]{1,2,0:T(8,128)(2,1)} %param.5) | copy-start | bytes 538948
  1.1 15.6 %collective-permute-start.3 = (bf16[32,2816]{1,0:T(8,128)(2,1)S(1)}, bf16[32,2816]{1,0:T(8,128)(2,1)S(1)}, u32[]{:S(2)}, u32[]{:S(2)}) collective-permute-start(bf16[32,2816]{1,0:T(8,128)(2,1)S(1)} %pack.1.x0), channel_id=1, source_target_pairs={{0,6},{1,7},{2,0},{3,1},{4,2},{5,3},{6,4},{7,5},{8,14},{9,15},{10,... | collective-permute-start | bytes 540680 | tf_op jit(solution)/shard_map/ppermute | solution.py:230
  8.0 11.8 %collective-permute-start.2 = (bf16[32,2816]{1,0:T(8,128)(2,1)S(1)}, bf16[32,2816]{1,0:T(8,128)(2,1)S(1)}, u32[]{:S(2)}, u32[]{:S(2)}) collective-permute-start(bf16[32,2816]{1,0:T(8,128)(2,1)S(1)} %pack.1.x0), channel_id=1, source_target_pairs={{0,2},{1,3},{2,4},{3,5},{4,6},{5,7},{6,0},{7,1},{8,10},{9,11},{10,... | collective-permute-start | bytes 540680 | tf_op jit(solution)/shard_map/ppermute | solution.py:230
  8.0 15.2 %collective-permute-start.1 = (bf16[32,2816]{1,0:T(8,128)(2,1)S(1)}, bf16[32,2816]{1,0:T(8,128)(2,1)S(1)}, u32[]{:S(2)}, u32[]{:S(2)}) collective-permute-start(bf16[32,2816]{1,0:T(8,128)(2,1)S(1)} %pack.1.x0), channel_id=1, source_target_pairs={{0,7},{1,0},{2,1},{3,2},{4,3},{5,4},{6,5},{7,6},{8,15},{9,8},{10,9... | collective-permute-start | bytes 540680 | tf_op jit(solution)/shard_map/ppermute | solution.py:230
  11.1 13.2 %collective-permute-start = (bf16[32,2816]{1,0:T(8,128)(2,1)S(1)}, bf16[32,2816]{1,0:T(8,128)(2,1)S(1)}, u32[]{:S(2)}, u32[]{:S(2)}) collective-permute-start(bf16[32,2816]{1,0:T(8,128)(2,1)S(1)} %pack.1.x0), channel_id=1, source_target_pairs={{0,1},{1,2},{2,3},{3,4},{4,5},{5,6},{6,7},{7,0},{8,9},{9,10},{10,1... | collective-permute-start | bytes 540680 | tf_op jit(solution)/shard_map/ppermute | solution.py:230
  12.0 0.7 %copy-start.4 = (s32[256]{0:T(256)S(1)}, s32[256]{0:T(256)}, u32[]{:S(2)}) copy-start(s32[256]{0:T(256)} %lat_slot.3) | copy-start | bytes 3076
  12.7 10.5 %copy-start.3 = (s32[224]{0:T(256)S(1)}, s32[224]{0:T(256)}, u32[]{:S(2)}) copy-start(s32[224]{0:T(256)} %wave_pair.1) | copy-start | bytes 2692
  12.7 10.5 %copy-start.6 = (bf16[7,401,128]{2,1,0:T(8,128)(2,1)S(1)}, bf16[7,401,128]{2,1,0:T(8,128)(2,1)}, u32[]{:S(2)}) copy-start(bf16[7,401,128]{2,1,0:T(8,128)(2,1)} %spec.1) | copy-start | bytes 2155780
  16.7 7.6 %collective-permute-start.7 = (bf16[16,2816]{1,0:T(8,128)(2,1)S(1)}, bf16[16,2816]{1,0:T(8,128)(2,1)S(1)}, u32[]{:S(2)}, u32[]{:S(2)}) collective-permute-start(bf16[16,2816]{1,0:T(8,128)(2,1)S(1)} %half.3), channel_id=1, source_target_pairs={{0,6},{1,7},{2,0},{3,1},{4,2},{5,3},{6,4},{7,5},{8,14},{9,15},{10,... | collective-permute-start | bytes 270344 | tf_op jit(solution)/shard_map/ppermute | solution.py:230
  19.7 6.8 %collective-permute-start.6 = (bf16[16,2816]{1,0:T(8,128)(2,1)S(1)}, bf16[16,2816]{1,0:T(8,128)(2,1)S(1)}, u32[]{:S(2)}, u32[]{:S(2)}) collective-permute-start(bf16[16,2816]{1,0:T(8,128)(2,1)S(1)} %half.2), channel_id=1, source_target_pairs={{0,2},{1,3},{2,4},{3,5},{4,6},{5,7},{6,0},{7,1},{8,10},{9,11},{10,... | collective-permute-start | bytes 270344 | tf_op jit(solution)/shard_map/ppermute | solution.py:230
  19.8 7.4 %collective-permute-start.5 = (bf16[32,2816]{1,0:T(8,128)(2,1)S(1)}, bf16[32,2816]{1,0:T(8,128)(2,1)S(1)}, u32[]{:S(2)}, u32[]{:S(2)}) collective-permute-start(bf16[32,2816]{1,0:T(8,128)(2,1)S(1)} %collective-permute-done.3.ref.m2), channel_id=1, source_target_pairs={{0,7},{1,0},{2,1},{3,2},{4,3},{5,4},{6,5},{7,6},{8,15},{9,8},{10,9... | collective-permute-start | bytes 540680 | tf_op jit(solution)/shard_map/ppermute | solution.py:230
  23.1 8.3 %collective-permute-start.4 = (bf16[32,2816]{1,0:T(8,128)(2,1)S(1)}, bf16[32,2816]{1,0:T(8,128)(2,1)S(1)}, u32[]{:S(2)}, u32[]{:S(2)}) collective-permute-start(bf16[32,2816]{1,0:T(8,128)(2,1)S(1)} %collective-permute-done.2.ref.p2), channel_id=1, source_target_pairs={{0,1},{1,2},{2,3},{3,4},{4,5},{5,6},{6,7},{7,0},{8,9},{9,10},{10,1... | collective-permute-start | bytes 540680 | tf_op jit(solution)/shard_map/ppermute | solution.py:230
  31.4 25.1 %copy-start = (bf16[8,256,1024]{2,1,0:T(8,128)(2,1)S(1)}, bf16[8,256,1024]{2,1,0:T(8,128)(2,1)}, u32[]{:S(2)}) copy-start(bf16[8,256,1024]{2,1,0:T(8,128)(2,1)} %get-tuple-element.8.fine) | copy-start | bytes 12582916
  32.1 24.4 %copy-start.1 = (f32[8,8,1024]{2,1,0:T(8,128)S(1)}, f32[8,8,1024]{2,1,0:T(8,128)}, u32[]{:S(2)}) copy-start(f32[8,8,1024]{2,1,0:T(8,128)} %get-tuple-element.7._tables.coarse) | copy-start | bytes 786436
  32.1 24.4 %copy-start.5 = (s32[256]{0:T(256)S(1)}, s32[256]{0:T(256)}, u32[]{:S(2)}) copy-start(s32[256]{0:T(256)} %lat_slot.3) | copy-start | bytes 3076

commit v6 on v5

--- a/solution.py
+++ b/solution.py
@@ -4,6 +4,7 @@
 from jax.experimental import pallas as pl
 from jax.experimental.pallas import tpu as pltpu
 from jax.sharding import PartitionSpec as P
+
 
 NLAT = 800
 WAVES = 400
@@ -69,19 +70,28 @@
         out[s, MAIN:KP, 128:256] = (rest - low).astype(jnp.bfloat16)
 
 
-def legendre_kernel(place, _tables, rhs, x0, p1, m1, p2, m2, p3, m3, p4, m4, out):
+def legendre_blocks(place, rhs, refs, offsets, out):
     z = place[0]
     for s in range(SLOTS):
         def lhs(ref):
             return jnp.concatenate(
                 [ref[:, MAIN * s : MAIN * (s + 1)], ref[:, SLOTS * MAIN : PACKED]], axis=1)
-        left = jnp.concatenate([lhs(r) for r in (x0, p1, m1, p2, m2, p3, m3, p4, m4)], axis=0)
+
+        left = jnp.concatenate([lhs(r) for r in refs], axis=0)
         got = jnp.dot(left, rhs[s], preferred_element_type=jnp.float32)
-        for i, d in enumerate((0, 1, -1, 2, -2, 3, -3, 4)):
+        for i, d in enumerate(offsets):
             block = lax.rem(z - d + 8, 8)
             for h in range(2):
                 part = got[QBLK * i : QBLK * (i + 1), 128 * h : 128 * (h + 1)]
                 out[pl.ds(4 * block, 4), 2 * s + h] = part.reshape(4, ROWS, 128).astype(jnp.bfloat16)
+
+
+def near_kernel(place, rhs, x0, p1, m1, p2, m2, out):
+    legendre_blocks(place, rhs, (x0, p1, m1, p2, m2), (0, 1, -1, 2, -2), out)
+
+
+def far_kernel(place, _tables, _near, rhs, p3, m3, p4, m4, out):
+    legendre_blocks(place, rhs, (p3, m3, p4, m4), (3, -3, 4), out)
 
 
 def table_kernel(device, lat_slot, pairs, fine_out, coarse_out, scr, fine, coarse, sems):
@@ -178,8 +188,10 @@
         a = lat_slot[device[0] * ROWS + q]
         lon = 20 + 4 * jnp.minimum(a, NLAT - 1 - a)
         result = lax.dot_general(lhs[...], fine[q], nt, preferred_element_type=jnp.float32)
-        rotate(jnp.minimum(q + 1, ROWS - 1), turn, other)
-        turn_row(jnp.minimum(q + 2, ROWS - 1), spare)
+        if other is not None:
+            rotate(q + 1, turn, other)
+        if spare is not None:
+            turn_row(q + 2, spare)
 
         def put(jc, block):
             width = min(FINE, WIDTH - FINE * jc)
@@ -202,7 +214,9 @@
     turn_row(0, turn_a)
     turn_row(1, turn_b)
     rotate(0, turn_a, lhs_a)
-    lax.fori_loop(0, ROWS // 2, two_rows, 0)
+    lax.fori_loop(0, ROWS // 2 - 1, two_rows, 0)
+    one_row(ROWS - 2, lhs_a, lhs_b, turn_b, None)
+    one_row(ROWS - 1, lhs_b, None, None, None)
     for q in range(ROWS):
         copy(q).wait()
 
@@ -236,7 +250,7 @@
     return x, p1, m1, p2, m2, p3, m3, p4, m4
 
 
-def on_device(spectral, legendre, wave_pair, lat_slot):
+def program(spectral, legendre, wave_pair, lat_slot):
     bf16, f32 = jnp.bfloat16, jnp.float32
     smem = pl.BlockSpec(memory_space=pltpu.SMEM)
     vmem = pl.BlockSpec(memory_space=pltpu.VMEM)
@@ -286,14 +300,25 @@
         name="tables",
     )(device, lat_slot, pairs)
 
+    near = pl.pallas_call(
+        near_kernel,
+        out_shape=pltpu.VMEM((32, 2 * SLOTS, ROWS, 128), bf16),
+        in_specs=[smem] + [vmem] * 6, out_specs=vmem,
+        cost_estimate=cost(1_000_000_000, 3_000_000),
+        compiler_params=params(8),
+        name="near",
+    )(z.reshape(1), here(rhs), *[here(p) for p in pieces[:5]])
+
     fourier = pl.pallas_call(
-        legendre_kernel,
+        far_kernel,
         out_shape=pltpu.VMEM((32, 2 * SLOTS, ROWS, 128), bf16),
-        in_specs=[smem, hbm] + [vmem] * 10, out_specs=vmem,
-        cost_estimate=cost(2 * 256 * 512 * 256 * SLOTS, 4_000_000),
-        compiler_params=params(12),
-        name="legendre",
-    )(z.reshape(1), pltpu.with_memory_space_constraint(coarse, pltpu.HBM), here(rhs), *[here(p) for p in pieces])
+        in_specs=[smem, hbm] + [vmem] * 6, out_specs=vmem,
+        input_output_aliases={2: 0},
+        cost_estimate=cost(2 * 96 * 512 * 256 * SLOTS, 2_000_000),
+        compiler_params=params(8),
+        name="far",
+    )(z.reshape(1), pltpu.with_memory_space_constraint(coarse, pltpu.HBM), here(near), here(rhs),
+      *[here(p) for p in pieces[5:]])
 
     received = lax.all_to_all(fourier, "wav", split_axis=0, concat_axis=0, tiled=True)
 
@@ -318,7 +343,7 @@
 
 def solution(mesh):
     return jax.shard_map(
-        on_device,
+        program,
         mesh=mesh,
         in_specs=(P("wav", None, "lev"), P("wav", None, "lev"), P(), P()),
         out_specs=P("wav", "lev", None),

time: 61.9 us -> 61 us (0.985)
  waiting for transfers between devices: 7.05 us -> 5.34 us
  blocking collectives: 24.4 us -> 25.9 us
  starting transfers between devices: 16.4 us -> 15.6 us
    ppermute x8, waiting for transfers between devices: 7.05 us -> 5.34 us  [shift(): return lax.ppermute(v, 'lev', [(i, (i + d) % 8) for i in range(8)])]
    all_to_all x1, blocking collectives: 24.4 us -> 25.9 us  [program(): lax.all_to_all(fourier, 'wav', split_axis=0, concat_axis=0, tiled=True)]
    ppermute x8, starting transfers between devices: 16.4 us -> 15.6 us  [shift(): return lax.ppermute(v, 'lev', [(i, (i + d) % 8) for i in range(8)])]
    pallas_call x5 -> x6, Pallas kernels: 11.2 us -> 11.4 us  [the longest x1 5.18 us: program(): pl.pallas_call(synth_kernel, out_shape=jax.ShapeDtypeStruct((ROWS, 64, WI...]
  transfers between devices with their start and end apart: 8 -> 8, of which waited for: 3 -> 2; matrix products, arithmetic and copies ran while one was open for 1% -> 1% of each run, Pallas kernels for 8% -> 9%
where the time goes in v6:
time: 61 us; the launch traced here: 60.9 us
  blocking collectives  25.9 us (42%)
  starting transfers between devices  15.6 us (26%)
  Pallas kernels  11.4 us (19%)
  waiting for transfers between devices  5.34 us (9%)
  local copies, waits for them, and re-layouts  2.54 us (4%)
    all_to_all x1, blocking collectives, program(): lax.all_to_all(fourier, 'wav', split_axis=0, concat_axis=0, tiled=True)  25.9 us
    ppermute x8, starting transfers between devices, shift(): return lax.ppermute(v, 'lev', [(i, (i + d) % 8) for i in range(8)])  15.6 us
    ppermute x8, waiting for transfers between devices, shift(): return lax.ppermute(v, 'lev', [(i, (i + d) % 8) for i in range(8)])  5.34 us
    pallas_call x1, Pallas kernels, program(): pl.pallas_call(synth_kernel, out_shape=jax.ShapeDtypeStruct((ROWS, 64, WI...  5.18 us
    pallas_call x1, Pallas kernels, program(): pl.pallas_call(table_kernel, out_shape=(pltpu.HBM((ROWS, FINE, 2 * KP), b...  3.99 us
    unnamed x14, local copies, waits for them, and re-layouts  1.64 us
  transfers between devices with their start and end apart: 8, of which 2 were waited for; matrix products, arithmetic and copies ran while one was open for 1% of the time, Pallas kernels for 9%

profile of v6, /device:TPU:1, one launch (start us, length us, event | category | flops | bytes accessed | tf_op | source)
XLA Modules:
  0.0 60.9 jit_solution(8531364494803654553)
XLA Ops:
  0.0 0.9 %copy-done.2 = bf16[7,401,32]{1,2,0:T(8,128)(2,1)S(1)} copy-done((bf16[7,401,32]{1,2,0:T(8,128)(2,1)S(1)}, bf16[7,401,32]{1,2,0:T(8,128)(2,1)}, u32[]{:S(2)}) %copy-start.2) | copy-done | bytes 179672
  0.9 0.1 pack.1.x0
  1.1 6.9 %collective-permute-start.3 = (bf16[32,2816]{1,0:T(8,128)(2,1)S(1)}, bf16[32,2816]{1,0:T(8,128)(2,1)S(1)}, u32[]{:S(2)}, u32[]{:S(2)}) collective-permute-start(bf16[32,2816]{1,0:T(8,128)(2,1)S(1)} %pack.1.x0), channel_id=1, source_target_pairs={{0,6},{1,7},{2,0},{3,1},{4,2},{5,3},{6,4},{7,5},{8,14},{9,15},{10,... | collective-permute-start | bytes 540680 | tf_op jit(solution)/shard_map/ppermute | solution.py:244
  8.0 0.0 collective-permute-start.2
  8.0 3.1 %collective-permute-start.1 = (bf16[32,2816]{1,0:T(8,128)(2,1)S(1)}, bf16[32,2816]{1,0:T(8,128)(2,1)S(1)}, u32[]{:S(2)}, u32[]{:S(2)}) collective-permute-start(bf16[32,2816]{1,0:T(8,128)(2,1)S(1)} %pack.1.x0), channel_id=1, source_target_pairs={{0,7},{1,0},{2,1},{3,2},{4,3},{5,4},{6,5},{7,6},{8,15},{9,8},{10,9... | collective-permute-start | bytes 540680 | tf_op jit(solution)/shard_map/ppermute | solution.py:244
  11.1 0.8 %broadcast_in_dim.2 = s32[224,2]{1,0:T(8,128)S(1)} broadcast(s32[224]{0:T(256)} %wave_pair.1), dimensions={0} | broadcast | bytes 2688 | tf_op jit(solution)/shard_map/broadcast_in_dim | solution.py:261
  11.9 0.1 reshape.16.pairs
  12.0 0.0 copy-start.4
  12.0 0.7 %copy-done.4 = s32[256]{0:T(256)S(1)} copy-done((s32[256]{0:T(256)S(1)}, s32[256]{0:T(256)}, u32[]{:S(2)}) %copy-start.4) | copy-done | bytes 1048
  12.7 4.0 %tables.1 = (bf16[8,256,1024]{2,1,0:T(8,128)(2,1)}, f32[8,8,1024]{2,1,0:T(8,128)}) custom-call(s32[1]{0:T(128)} %bitcast.device, s32[256]{0:T(256)S(1)} %copy-done.4, s32[1,448]{1,0:T(1,128)S(1)} %reshape.16.pairs), custom_call_target="tpu_custom_call" | custom-call | flops 4000000000 | bytes 4500000 | tf_op jit(solution)/shard_map/tables/pallas_call | solution.py:289
  16.7 0.0 collective-permute-done.3.m2.ref
  16.7 2.7 %collective-permute-start.5 = (bf16[32,2816]{1,0:T(8,128)(2,1)S(1)}, bf16[32,2816]{1,0:T(8,128)(2,1)S(1)}, u32[]{:S(2)}, u32[]{:S(2)}) collective-permute-start(bf16[32,2816]{1,0:T(8,128)(2,1)S(1)} %collective-permute-done.3.m2.ref), channel_id=1, source_target_pairs={{0,7},{1,0},{2,1},{3,2},{4,3},{5,4},{6,5},{7,6},{8,15},{9,8},{10,9... | collective-permute-start | bytes 540680 | tf_op jit(solution)/shard_map/ppermute | solution.py:244
  19.5 0.3 collective-permute-start.4
  19.8 1.2 %mask.1.rhs = bf16[7,512,256]{2,1,0:T(8,128)(2,1)S(1)} custom-call(s32[1]{0:T(128)} %bitcast.device, s32[224]{0:T(256)S(1)} %copy-done.3, bf16[7,401,128]{2,1,0:T(8,128)(2,1)S(1)} %copy-done.6), custom_call_target="tpu_custom_call" | custom-call | flops 2000000000 | bytes 2500000 | tf_op jit(solution)/shard_map/mask/pallas_call | solution.py:279
  21.0 1.4 %collective-permute-start.7 = (bf16[16,2816]{1,0:T(8,128)(2,1)S(1)}, bf16[16,2816]{1,0:T(8,128)(2,1)S(1)}, u32[]{:S(2)}, u32[]{:S(2)}) collective-permute-start(bf16[16,2816]{1,0:T(8,128)(2,1)S(1)} %half.3), channel_id=1, source_target_pairs={{0,6},{1,7},{2,0},{3,1},{4,2},{5,3},{6,4},{7,5},{8,14},{9,15},{10,... | collective-permute-start | bytes 270344 | tf_op jit(solution)/shard_map/ppermute | solution.py:244
  22.4 1.1 %collective-permute-start.6 = (bf16[16,2816]{1,0:T(8,128)(2,1)S(1)}, bf16[16,2816]{1,0:T(8,128)(2,1)S(1)}, u32[]{:S(2)}, u32[]{:S(2)}) collective-permute-start(bf16[16,2816]{1,0:T(8,128)(2,1)S(1)} %half.2), channel_id=1, source_target_pairs={{0,2},{1,3},{2,4},{3,5},{4,6},{5,7},{6,0},{7,1},{8,10},{9,11},{10,... | collective-permute-start | bytes 270344 | tf_op jit(solution)/shard_map/ppermute | solution.py:244
  23.5 0.5 near.1._near
  24.0 2.3 %collective-permute-done.7.m4 = bf16[16,2816]{1,0:T(8,128)(2,1)S(1)} collective-permute-done((bf16[16,2816]{1,0:T(8,128)(2,1)S(1)}, bf16[16,2816]{1,0:T(8,128)(2,1)S(1)}, u32[]{:S(2)}, u32[]{:S(2)}) %collective-permute-start.7) | collective-permute-done | bytes 90144 | tf_op jit(solution)/shard_map/ppermute | solution.py:244
  26.3 3.0 %collective-permute-done.6.p4 = bf16[16,2816]{1,0:T(8,128)(2,1)S(1)} collective-permute-done((bf16[16,2816]{1,0:T(8,128)(2,1)S(1)}, bf16[16,2816]{1,0:T(8,128)(2,1)S(1)}, u32[]{:S(2)}, u32[]{:S(2)}) %collective-permute-start.6) | collective-permute-done | bytes 90144 | tf_op jit(solution)/shard_map/ppermute | solution.py:244
  29.3 0.4 far.1
  29.8 0.0 copy-start.1
  29.8 0.0 copy-start.5
  29.8 25.9 %all_to_all.5 = bf16[32,14,8,128]{3,2,1,0:T(8,128)(2,1)S(1)} all-to-all(bf16[32,14,8,128]{3,2,1,0:T(8,128)(2,1)S(1)} %far.1), channel_id=1, replica_groups=mesh['wav'=32,'lev'=8] {'wav'}, dimensions={0} | all-to-all | bytes 1835008 | tf_op jit(solution)/shard_map/all_to_all | solution.py:323
  55.7 5.2 %synth.1 = bf16[8,64,1616]{2,1,0:T(8,128)(2,1)} custom-call(s32[1]{0:T(128)} %bitcast.device, s32[256]{0:T(256)S(1)} %copy-done.5, bf16[448,8,128]{2,1,0:T(8,128)(2,1)S(1)} %bitcast.4, bf16[8,256,1024]{2,1,0:T(8,128)(2,1)S(1)} %copy-done, f32[8,8,1024]{2,1,0:T(8,128)S(1)} %copy-done.1), custom_call_target="tpu_custom_call" | custom-call | flops 1879048192 | bytes 18000000 | tf_op jit(solution)/shard_map/synth/pallas_call | solution.py:325
  (17 shorter events, 0.0 us)
Async XLA Ops:
  0.0 0.9 %copy-start.2 = (bf16[7,401,32]{1,2,0:T(8,128)(2,1)S(1)}, bf16[7,401,32]{1,2,0:T(8,128)(2,1)}, u32[]{:S(2)}) copy-start(bf16[7,401,32]{1,2,0:T(8,128)(2,1)} %param.5) | copy-start | bytes 538948
  1.1 15.6 %collective-permute-start.3 = (bf16[32,2816]{1,0:T(8,128)(2,1)S(1)}, bf16[32,2816]{1,0:T(8,128)(2,1)S(1)}, u32[]{:S(2)}, u32[]{:S(2)}) collective-permute-start(bf16[32,2816]{1,0:T(8,128)(2,1)S(1)} %pack.1.x0), channel_id=1, source_target_pairs={{0,6},{1,7},{2,0},{3,1},{4,2},{5,3},{6,4},{7,5},{8,14},{9,15},{10,... | collective-permute-start | bytes 540680 | tf_op jit(solution)/shard_map/ppermute | solution.py:244
  8.0 11.5 %collective-permute-start.2 = (bf16[32,2816]{1,0:T(8,128)(2,1)S(1)}, bf16[32,2816]{1,0:T(8,128)(2,1)S(1)}, u32[]{:S(2)}, u32[]{:S(2)}) collective-permute-start(bf16[32,2816]{1,0:T(8,128)(2,1)S(1)} %pack.1.x0), channel_id=1, source_target_pairs={{0,2},{1,3},{2,4},{3,5},{4,6},{5,7},{6,0},{7,1},{8,10},{9,11},{10,... | collective-permute-start | bytes 540680 | tf_op jit(solution)/shard_map/ppermute | solution.py:244
  8.0 14.4 %collective-permute-start.1 = (bf16[32,2816]{1,0:T(8,128)(2,1)S(1)}, bf16[32,2816]{1,0:T(8,128)(2,1)S(1)}, u32[]{:S(2)}, u32[]{:S(2)}) collective-permute-start(bf16[32,2816]{1,0:T(8,128)(2,1)S(1)} %pack.1.x0), channel_id=1, source_target_pairs={{0,7},{1,0},{2,1},{3,2},{4,3},{5,4},{6,5},{7,6},{8,15},{9,8},{10,9... | collective-permute-start | bytes 540680 | tf_op jit(solution)/shard_map/ppermute | solution.py:244
  11.1 12.4 %collective-permute-start = (bf16[32,2816]{1,0:T(8,128)(2,1)S(1)}, bf16[32,2816]{1,0:T(8,128)(2,1)S(1)}, u32[]{:S(2)}, u32[]{:S(2)}) collective-permute-start(bf16[32,2816]{1,0:T(8,128)(2,1)S(1)} %pack.1.x0), channel_id=1, source_target_pairs={{0,1},{1,2},{2,3},{3,4},{4,5},{5,6},{6,7},{7,0},{8,9},{9,10},{10,1... | collective-permute-start | bytes 540680 | tf_op jit(solution)/shard_map/ppermute | solution.py:244
  12.0 0.7 %copy-start.4 = (s32[256]{0:T(256)S(1)}, s32[256]{0:T(256)}, u32[]{:S(2)}) copy-start(s32[256]{0:T(256)} %lat_slot.3) | copy-start | bytes 3076
  12.7 7.1 %copy-start.3 = (s32[224]{0:T(256)S(1)}, s32[224]{0:T(256)}, u32[]{:S(2)}) copy-start(s32[224]{0:T(256)} %wave_pair.1) | copy-start | bytes 2692
  12.7 7.1 %copy-start.6 = (bf16[7,401,128]{2,1,0:T(8,128)(2,1)S(1)}, bf16[7,401,128]{2,1,0:T(8,128)(2,1)}, u32[]{:S(2)}) copy-start(bf16[7,401,128]{2,1,0:T(8,128)(2,1)} %spec.1) | copy-start | bytes 2155780
  16.7 12.6 %collective-permute-start.5 = (bf16[32,2816]{1,0:T(8,128)(2,1)S(1)}, bf16[32,2816]{1,0:T(8,128)(2,1)S(1)}, u32[]{:S(2)}, u32[]{:S(2)}) collective-permute-start(bf16[32,2816]{1,0:T(8,128)(2,1)S(1)} %collective-permute-done.3.m2.ref), channel_id=1, source_target_pairs={{0,7},{1,0},{2,1},{3,2},{4,3},{5,4},{6,5},{7,6},{8,15},{9,8},{10,9... | collective-permute-start | bytes 540680 | tf_op jit(solution)/shard_map/ppermute | solution.py:244
  19.5 9.9 %collective-permute-start.4 = (bf16[32,2816]{1,0:T(8,128)(2,1)S(1)}, bf16[32,2816]{1,0:T(8,128)(2,1)S(1)}, u32[]{:S(2)}, u32[]{:S(2)}) collective-permute-start(bf16[32,2816]{1,0:T(8,128)(2,1)S(1)} %collective-permute-done.2.p2.ref), channel_id=1, source_target_pairs={{0,1},{1,2},{2,3},{3,4},{4,5},{5,6},{6,7},{7,0},{8,9},{9,10},{10,1... | collective-permute-start | bytes 540680 | tf_op jit(solution)/shard_map/ppermute | solution.py:244
  21.0 5.3 %collective-permute-start.7 = (bf16[16,2816]{1,0:T(8,128)(2,1)S(1)}, bf16[16,2816]{1,0:T(8,128)(2,1)S(1)}, u32[]{:S(2)}, u32[]{:S(2)}) collective-permute-start(bf16[16,2816]{1,0:T(8,128)(2,1)S(1)} %half.3), channel_id=1, source_target_pairs={{0,6},{1,7},{2,0},{3,1},{4,2},{5,3},{6,4},{7,5},{8,14},{9,15},{10,... | collective-permute-start | bytes 270344 | tf_op jit(solution)/shard_map/ppermute | solution.py:244
  22.4 6.9 %collective-permute-start.6 = (bf16[16,2816]{1,0:T(8,128)(2,1)S(1)}, bf16[16,2816]{1,0:T(8,128)(2,1)S(1)}, u32[]{:S(2)}, u32[]{:S(2)}) collective-permute-start(bf16[16,2816]{1,0:T(8,128)(2,1)S(1)} %half.2), channel_id=1, source_target_pairs={{0,2},{1,3},{2,4},{3,5},{4,6},{5,7},{6,0},{7,1},{8,10},{9,11},{10,... | collective-permute-start | bytes 270344 | tf_op jit(solution)/shard_map/ppermute | solution.py:244
  29.3 26.4 %copy-start = (bf16[8,256,1024]{2,1,0:T(8,128)(2,1)S(1)}, bf16[8,256,1024]{2,1,0:T(8,128)(2,1)}, u32[]{:S(2)}) copy-start(bf16[8,256,1024]{2,1,0:T(8,128)(2,1)} %get-tuple-element.8.fine) | copy-start | bytes 12582916
  29.8 25.9 %copy-start.1 = (f32[8,8,1024]{2,1,0:T(8,128)S(1)}, f32[8,8,1024]{2,1,0:T(8,128)}, u32[]{:S(2)}) copy-start(f32[8,8,1024]{2,1,0:T(8,128)} %get-tuple-element.7._tables.coarse) | copy-start | bytes 786436
  29.8 25.9 %copy-start.5 = (s32[256]{0:T(256)S(1)}, s32[256]{0:T(256)}, u32[]{:S(2)}) copy-start(s32[256]{0:T(256)} %lat_slot.3) | copy-start | bytes 3076

commit v7 on v6

--- a/solution.py
+++ b/solution.py
@@ -41,10 +41,16 @@
     return horner(COS, v), u * horner(SIN, v)
 
 
-def pack_kernel(leg, out, scr):
+def pack_kernel(source, out, scr, leg, sems):
+    def fetch(s):
+        return pltpu.make_async_copy(source.at[s], leg.at[s], sems.at[s])
+
+    for s in range(SLOTS):
+        fetch(s).start()
     total = jnp.zeros((QBLK, 128), jnp.float32)
     scr[...] = total
     for s in range(SLOTS):
+        fetch(s).wait()
         out[:, MAIN * s : MAIN * (s + 1)] = leg[s, :, 0:MAIN]
         scr[:, 0:REST] = leg[s, :, MAIN:FOLD].astype(jnp.float32)
         tail = scr[...]
@@ -269,11 +275,13 @@
     packed = pl.pallas_call(
         pack_kernel,
         out_shape=pltpu.VMEM((QBLK, PACKED), bf16),
-        in_specs=[vmem], out_specs=vmem,
-        scratch_shapes=[pltpu.VMEM((QBLK, 128), f32)],
+        in_specs=[hbm], out_specs=vmem,
+        scratch_shapes=[pltpu.VMEM((QBLK, 128), f32),
+                        pltpu.VMEM((SLOTS, QBLK, FOLD), bf16),
+                        pltpu.SemaphoreType.DMA((SLOTS,))],
         compiler_params=params(4),
         name="pack",
-    )(jnp.transpose(legendre, (0, 2, 1)))
+    )(pltpu.with_memory_space_constraint(jnp.transpose(legendre, (0, 2, 1)), pltpu.HBM))
     pieces = gather_pieces(packed)
 
     rhs = pl.pallas_call(

time: 61 us -> 61.4 us (level)
  Pallas kernels: 11.4 us -> 12.6 us
  local copies, waits for them, and re-layouts: 2.54 us -> 1.6 us
    pallas_call x1, Pallas kernels: 0.11 us -> 1.32 us  [program(): pl.pallas_call(pack_kernel, out_shape=pltpu.VMEM((QBLK, PACKED), bf16), i...]
    unnamed x14 -> x12, local copies, waits for them, and re-layouts: 1.64 us -> 0.7 us
where the time goes in v7:
time: 61.4 us; the launch traced here: 61.2 us
  blocking collectives  25.9 us (42%)
  starting transfers between devices  15.6 us (25%)
  Pallas kernels  12.6 us (21%)
  waiting for transfers between devices  5.34 us (9%)
  local copies, waits for them, and re-layouts  1.6 us (3%)
    all_to_all x1, blocking collectives, program(): lax.all_to_all(fourier, 'wav', split_axis=0, concat_axis=0, tiled=True)  25.9 us
    ppermute x8, starting transfers between devices, shift(): return lax.ppermute(v, 'lev', [(i, (i + d) % 8) for i in range(8)])  15.6 us
    ppermute x8, waiting for transfers between devices, shift(): return lax.ppermute(v, 'lev', [(i, (i + d) % 8) for i in range(8)])  5.34 us
    pallas_call x1, Pallas kernels, program(): pl.pallas_call(synth_kernel, out_shape=jax.ShapeDtypeStruct((ROWS, 64, WI...  5.18 us
    pallas_call x1, Pallas kernels, program(): pl.pallas_call(table_kernel, out_shape=(pltpu.HBM((ROWS, FINE, 2 * KP), b...  3.98 us
    pallas_call x1, Pallas kernels, program(): pl.pallas_call(pack_kernel, out_shape=pltpu.VMEM((QBLK, PACKED), bf16), i...  1.32 us
  transfers between devices with their start and end apart: 8, of which 2 were waited for; matrix products, arithmetic and copies ran while one was open for 1% of the time, Pallas kernels for 9%

profile of v7, /device:TPU:1, one launch (start us, length us, event | category | flops | bytes accessed | tf_op | source)
XLA Modules:
  0.0 61.2 jit_solution(13348137943742805791)
XLA Ops:
  0.0 1.3 %pack.1.x0 = bf16[32,2816]{1,0:T(8,128)(2,1)S(1)} custom-call(bf16[7,32,401]{2,1,0:T(8,128)(2,1)} %bitcast.5), custom_call_target="tpu_custom_call" | custom-call | tf_op jit(solution)/shard_map/pack/pallas_call | solution.py:275
  1.3 6.9 %collective-permute-start.3 = (bf16[32,2816]{1,0:T(8,128)(2,1)S(1)}, bf16[32,2816]{1,0:T(8,128)(2,1)S(1)}, u32[]{:S(2)}, u32[]{:S(2)}) collective-permute-start(bf16[32,2816]{1,0:T(8,128)(2,1)S(1)} %pack.1.x0), channel_id=1, source_target_pairs={{0,6},{1,7},{2,0},{3,1},{4,2},{5,3},{6,4},{7,5},{8,14},{9,15},{10,... | collective-permute-start | bytes 540680 | tf_op jit(solution)/shard_map/ppermute | solution.py:250
  8.3 3.1 %collective-permute-start.1 = (bf16[32,2816]{1,0:T(8,128)(2,1)S(1)}, bf16[32,2816]{1,0:T(8,128)(2,1)S(1)}, u32[]{:S(2)}, u32[]{:S(2)}) collective-permute-start(bf16[32,2816]{1,0:T(8,128)(2,1)S(1)} %pack.1.x0), channel_id=1, source_target_pairs={{0,7},{1,0},{2,1},{3,2},{4,3},{5,4},{6,5},{7,6},{8,15},{9,8},{10,9... | collective-permute-start | bytes 540680 | tf_op jit(solution)/shard_map/ppermute | solution.py:250
  11.4 0.0 collective-permute-start
  11.4 0.8 %broadcast_in_dim.2 = s32[224,2]{1,0:T(8,128)S(1)} broadcast(s32[224]{0:T(256)} %wave_pair.1), dimensions={0} | broadcast | bytes 2688 | tf_op jit(solution)/shard_map/broadcast_in_dim | solution.py:267
  12.2 0.1 reshape.16.pairs
  12.3 0.0 copy-start.3
  12.3 0.7 %copy-done.3 = s32[256]{0:T(256)S(1)} copy-done((s32[256]{0:T(256)S(1)}, s32[256]{0:T(256)}, u32[]{:S(2)}) %copy-start.3) | copy-done | bytes 1048
  13.0 4.0 %tables.1 = (bf16[8,256,1024]{2,1,0:T(8,128)(2,1)}, f32[8,8,1024]{2,1,0:T(8,128)}) custom-call(s32[1]{0:T(128)} %bitcast.device, s32[256]{0:T(256)S(1)} %copy-done.3, s32[1,448]{1,0:T(1,128)S(1)} %reshape.16.pairs), custom_call_target="tpu_custom_call" | custom-call | flops 4000000000 | bytes 4500000 | tf_op jit(solution)/shard_map/tables/pallas_call | solution.py:297
  17.0 2.7 %collective-permute-start.5 = (bf16[32,2816]{1,0:T(8,128)(2,1)S(1)}, bf16[32,2816]{1,0:T(8,128)(2,1)S(1)}, u32[]{:S(2)}, u32[]{:S(2)}) collective-permute-start(bf16[32,2816]{1,0:T(8,128)(2,1)S(1)} %collective-permute-done.3.m2.ref), channel_id=1, source_target_pairs={{0,7},{1,0},{2,1},{3,2},{4,3},{5,4},{6,5},{7,6},{8,15},{9,8},{10,9... | collective-permute-start | bytes 540680 | tf_op jit(solution)/shard_map/ppermute | solution.py:250
  19.7 0.3 collective-permute-start.4
  20.1 1.2 %mask.1.rhs = bf16[7,512,256]{2,1,0:T(8,128)(2,1)S(1)} custom-call(s32[1]{0:T(128)} %bitcast.device, s32[224]{0:T(256)S(1)} %copy-done.2, bf16[7,401,128]{2,1,0:T(8,128)(2,1)S(1)} %copy-done.5), custom_call_target="tpu_custom_call" | custom-call | flops 2000000000 | bytes 2500000 | tf_op jit(solution)/shard_map/mask/pallas_call | solution.py:287
  21.3 1.4 %collective-permute-start.7 = (bf16[16,2816]{1,0:T(8,128)(2,1)S(1)}, bf16[16,2816]{1,0:T(8,128)(2,1)S(1)}, u32[]{:S(2)}, u32[]{:S(2)}) collective-permute-start(bf16[16,2816]{1,0:T(8,128)(2,1)S(1)} %half.3), channel_id=1, source_target_pairs={{0,6},{1,7},{2,0},{3,1},{4,2},{5,3},{6,4},{7,5},{8,14},{9,15},{10,... | collective-permute-start | bytes 270344 | tf_op jit(solution)/shard_map/ppermute | solution.py:250
  22.7 1.1 %collective-permute-start.6 = (bf16[16,2816]{1,0:T(8,128)(2,1)S(1)}, bf16[16,2816]{1,0:T(8,128)(2,1)S(1)}, u32[]{:S(2)}, u32[]{:S(2)}) collective-permute-start(bf16[16,2816]{1,0:T(8,128)(2,1)S(1)} %half.2), channel_id=1, source_target_pairs={{0,2},{1,3},{2,4},{3,5},{4,6},{5,7},{6,0},{7,1},{8,10},{9,11},{10,... | collective-permute-start | bytes 270344 | tf_op jit(solution)/shard_map/ppermute | solution.py:250
  23.8 0.0 collective-permute-done.p1
  23.8 0.5 near.1._near
  24.3 2.3 %collective-permute-done.7.m4 = bf16[16,2816]{1,0:T(8,128)(2,1)S(1)} collective-permute-done((bf16[16,2816]{1,0:T(8,128)(2,1)S(1)}, bf16[16,2816]{1,0:T(8,128)(2,1)S(1)}, u32[]{:S(2)}, u32[]{:S(2)}) %collective-permute-start.7) | collective-permute-done | bytes 90144 | tf_op jit(solution)/shard_map/ppermute | solution.py:250
  26.6 3.0 %collective-permute-done.6.p4 = bf16[16,2816]{1,0:T(8,128)(2,1)S(1)} collective-permute-done((bf16[16,2816]{1,0:T(8,128)(2,1)S(1)}, bf16[16,2816]{1,0:T(8,128)(2,1)S(1)}, u32[]{:S(2)}, u32[]{:S(2)}) %collective-permute-start.6) | collective-permute-done | bytes 90144 | tf_op jit(solution)/shard_map/ppermute | solution.py:250
  29.6 0.0 collective-permute-done.5.m3
  29.6 0.4 far.1
  30.1 0.0 copy-start.1
  30.1 0.0 copy-start.4
  30.1 25.9 %all_to_all.5 = bf16[32,14,8,128]{3,2,1,0:T(8,128)(2,1)S(1)} all-to-all(bf16[32,14,8,128]{3,2,1,0:T(8,128)(2,1)S(1)} %far.1), channel_id=1, replica_groups=mesh['wav'=32,'lev'=8] {'wav'}, dimensions={0} | all-to-all | bytes 1835008 | tf_op jit(solution)/shard_map/all_to_all | solution.py:331
  56.0 5.2 %synth.1 = bf16[8,64,1616]{2,1,0:T(8,128)(2,1)} custom-call(s32[1]{0:T(128)} %bitcast.device, s32[256]{0:T(256)S(1)} %copy-done.4, bf16[448,8,128]{2,1,0:T(8,128)(2,1)S(1)} %bitcast.4, bf16[8,256,1024]{2,1,0:T(8,128)(2,1)S(1)} %copy-done, f32[8,8,1024]{2,1,0:T(8,128)S(1)} %copy-done.1), custom_call_target="tpu_custom_call" | custom-call | flops 1879048192 | bytes 18000000 | tf_op jit(solution)/shard_map/synth/pallas_call | solution.py:333
  (15 shorter events, 0.0 us)
Async XLA Ops:
  1.3 15.6 %collective-permute-start.3 = (bf16[32,2816]{1,0:T(8,128)(2,1)S(1)}, bf16[32,2816]{1,0:T(8,128)(2,1)S(1)}, u32[]{:S(2)}, u32[]{:S(2)}) collective-permute-start(bf16[32,2816]{1,0:T(8,128)(2,1)S(1)} %pack.1.x0), channel_id=1, source_target_pairs={{0,6},{1,7},{2,0},{3,1},{4,2},{5,3},{6,4},{7,5},{8,14},{9,15},{10,... | collective-permute-start | bytes 540680 | tf_op jit(solution)/shard_map/ppermute | solution.py:250
  8.2 11.5 %collective-permute-start.2 = (bf16[32,2816]{1,0:T(8,128)(2,1)S(1)}, bf16[32,2816]{1,0:T(8,128)(2,1)S(1)}, u32[]{:S(2)}, u32[]{:S(2)}) collective-permute-start(bf16[32,2816]{1,0:T(8,128)(2,1)S(1)} %pack.1.x0), channel_id=1, source_target_pairs={{0,2},{1,3},{2,4},{3,5},{4,6},{5,7},{6,0},{7,1},{8,10},{9,11},{10,... | collective-permute-start | bytes 540680 | tf_op jit(solution)/shard_map/ppermute | solution.py:250
  8.3 14.4 %collective-permute-start.1 = (bf16[32,2816]{1,0:T(8,128)(2,1)S(1)}, bf16[32,2816]{1,0:T(8,128)(2,1)S(1)}, u32[]{:S(2)}, u32[]{:S(2)}) collective-permute-start(bf16[32,2816]{1,0:T(8,128)(2,1)S(1)} %pack.1.x0), channel_id=1, source_target_pairs={{0,7},{1,0},{2,1},{3,2},{4,3},{5,4},{6,5},{7,6},{8,15},{9,8},{10,9... | collective-permute-start | bytes 540680 | tf_op jit(solution)/shard_map/ppermute | solution.py:250
  11.4 12.4 %collective-permute-start = (bf16[32,2816]{1,0:T(8,128)(2,1)S(1)}, bf16[32,2816]{1,0:T(8,128)(2,1)S(1)}, u32[]{:S(2)}, u32[]{:S(2)}) collective-permute-start(bf16[32,2816]{1,0:T(8,128)(2,1)S(1)} %pack.1.x0), channel_id=1, source_target_pairs={{0,1},{1,2},{2,3},{3,4},{4,5},{5,6},{6,7},{7,0},{8,9},{9,10},{10,1... | collective-permute-start | bytes 540680 | tf_op jit(solution)/shard_map/ppermute | solution.py:250
  12.3 0.7 %copy-start.3 = (s32[256]{0:T(256)S(1)}, s32[256]{0:T(256)}, u32[]{:S(2)}) copy-start(s32[256]{0:T(256)} %lat_slot.3) | copy-start | bytes 3076
  13.0 7.1 %copy-start.2 = (s32[224]{0:T(256)S(1)}, s32[224]{0:T(256)}, u32[]{:S(2)}) copy-start(s32[224]{0:T(256)} %wave_pair.1) | copy-start | bytes 2692
  13.0 7.1 %copy-start.5 = (bf16[7,401,128]{2,1,0:T(8,128)(2,1)S(1)}, bf16[7,401,128]{2,1,0:T(8,128)(2,1)}, u32[]{:S(2)}) copy-start(bf16[7,401,128]{2,1,0:T(8,128)(2,1)} %spec.1) | copy-start | bytes 2155780
  17.0 12.6 %collective-permute-start.5 = (bf16[32,2816]{1,0:T(8,128)(2,1)S(1)}, bf16[32,2816]{1,0:T(8,128)(2,1)S(1)}, u32[]{:S(2)}, u32[]{:S(2)}) collective-permute-start(bf16[32,2816]{1,0:T(8,128)(2,1)S(1)} %collective-permute-done.3.m2.ref), channel_id=1, source_target_pairs={{0,7},{1,0},{2,1},{3,2},{4,3},{5,4},{6,5},{7,6},{8,15},{9,8},{10,9... | collective-permute-start | bytes 540680 | tf_op jit(solution)/shard_map/ppermute | solution.py:250
  19.7 9.9 %collective-permute-start.4 = (bf16[32,2816]{1,0:T(8,128)(2,1)S(1)}, bf16[32,2816]{1,0:T(8,128)(2,1)S(1)}, u32[]{:S(2)}, u32[]{:S(2)}) collective-permute-start(bf16[32,2816]{1,0:T(8,128)(2,1)S(1)} %collective-permute-done.2.p2.ref), channel_id=1, source_target_pairs={{0,1},{1,2},{2,3},{3,4},{4,5},{5,6},{6,7},{7,0},{8,9},{9,10},{10,1... | collective-permute-start | bytes 540680 | tf_op jit(solution)/shard_map/ppermute | solution.py:250
  21.3 5.3 %collective-permute-start.7 = (bf16[16,2816]{1,0:T(8,128)(2,1)S(1)}, bf16[16,2816]{1,0:T(8,128)(2,1)S(1)}, u32[]{:S(2)}, u32[]{:S(2)}) collective-permute-start(bf16[16,2816]{1,0:T(8,128)(2,1)S(1)} %half.3), channel_id=1, source_target_pairs={{0,6},{1,7},{2,0},{3,1},{4,2},{5,3},{6,4},{7,5},{8,14},{9,15},{10,... | collective-permute-start | bytes 270344 | tf_op jit(solution)/shard_map/ppermute | solution.py:250
  22.7 6.9 %collective-permute-start.6 = (bf16[16,2816]{1,0:T(8,128)(2,1)S(1)}, bf16[16,2816]{1,0:T(8,128)(2,1)S(1)}, u32[]{:S(2)}, u32[]{:S(2)}) collective-permute-start(bf16[16,2816]{1,0:T(8,128)(2,1)S(1)} %half.2), channel_id=1, source_target_pairs={{0,2},{1,3},{2,4},{3,5},{4,6},{5,7},{6,0},{7,1},{8,10},{9,11},{10,... | collective-permute-start | bytes 270344 | tf_op jit(solution)/shard_map/ppermute | solution.py:250
  29.6 26.4 %copy-start = (bf16[8,256,1024]{2,1,0:T(8,128)(2,1)S(1)}, bf16[8,256,1024]{2,1,0:T(8,128)(2,1)}, u32[]{:S(2)}) copy-start(bf16[8,256,1024]{2,1,0:T(8,128)(2,1)} %get-tuple-element.8.fine) | copy-start | bytes 12582916
  30.1 25.9 %copy-start.1 = (f32[8,8,1024]{2,1,0:T(8,128)S(1)}, f32[8,8,1024]{2,1,0:T(8,128)}, u32[]{:S(2)}) copy-start(f32[8,8,1024]{2,1,0:T(8,128)} %get-tuple-element.7._tables.coarse) | copy-start | bytes 786436
  30.1 25.9 %copy-start.4 = (s32[256]{0:T(256)S(1)}, s32[256]{0:T(256)}, u32[]{:S(2)}) copy-start(s32[256]{0:T(256)} %lat_slot.3) | copy-start | bytes 3076
